TPU v7x, 32 devices: a whole 2x2x4 slice. The times are simulated.
32 devices in a mesh: wide: 16 (over z, y, core), narrow: 2 (over x).
Axes of the slice: x: 2, y: 2, z: 4, core: 2. Of those that a mesh axis runs over, the one named last changes fastest.
Arguments:
- hidden_in: bfloat16 [16384, 1024], P(('wide', 'narrow')), may hold values from -6 to 6
- segment_ids: int32 [32, 512], P(('wide', 'narrow')), may hold values from 0 to 7, never falling along the last dimension, each value on 1 to 256 neighbouring positions
- expert_ids: int32 [16384, 8], P(('wide', 'narrow')), may hold values from 0 to 15, all different within a row; in each aligned block of 512 rows (0 to 511, 512 to 1023, ...) at most 512 rows name the same one
- attn_gain: float32 [1024], replicated, may hold values from 0.5 to 1.5
- w_query: bfloat16 [1024, 1024], replicated, may hold values from -0.1875 to 0.1875
- w_key: bfloat16 [1024, 512], replicated, may hold values from -0.1875 to 0.1875
- w_value: bfloat16 [1024, 512], replicated, may hold values from -0.1875 to 0.1875
- w_out: bfloat16 [1024, 1024], replicated, may hold values from -0.75 to 0.75
- ffn_gain: float32 [1024], replicated, may hold values from 0.5 to 1.5
- router: bfloat16 [1024, 16], replicated, may hold values from -0.1875 to 0.1875
- w_gate: bfloat16 [16, 1024, 512], P('wide', None, 'narrow'), may hold values from -0.1875 to 0.1875
- w_up: bfloat16 [16, 1024, 512], P('wide', None, 'narrow'), may hold values from -0.1875 to 0.1875
- w_down: bfloat16 [16, 512, 1024], P('wide', 'narrow'), may hold values from -0.75 to 0.75
- grad_out: bfloat16 [16384, 1024], P(('wide', 'narrow')), may hold values from -6 to 6
Outputs:
- hidden_out: bfloat16 [16384, 1024], P(('wide', 'narrow'))
- grad_in: bfloat16 [16384, 1024], P(('wide', 'narrow'))
- grad_attn_gain: float32 [1024], replicated
- grad_query: float32 [1024, 1024], replicated
- grad_key: float32 [1024, 512], replicated
- grad_value: float32 [1024, 512], replicated
- grad_out_proj: float32 [1024, 1024], replicated
- grad_ffn_gain: float32 [1024], replicated
- grad_router: float32 [1024, 16], replicated
- grad_gate: float32 [16, 1024, 512], P('wide', None, 'narrow')
- grad_up: float32 [16, 1024, 512], P('wide', None, 'narrow')
- grad_down: float32 [16, 512, 1024], P('wide', 'narrow')
Inputs may be any that keep to these rules, and one draw needn't show every extreme that they name: `segment_ids`: each packed row has 8 documents numbered in order from 0, each of 1 to half of 512 tokens, one of exactly half of 512. `expert_ids`: each token names 8 different experts. Among the 512 tokens of one packed row no expert is named more than 512 times, and in every draw some row names some expert exactly 512 times.
All inputs are finite; a program needn't handle non-finite values.
Results may differ from a plain program's by a relative error of at most 0.015.
Values may be sent and summed in bfloat16 or wider, within the bound.
A program may use at most 320 MiB of HBM per device.

v0:
```python
import jax
import jax.numpy as jnp
from jax import lax
from jax.sharding import PartitionSpec as P

HD = 64


EPSILON = 1e-05


def norm_scale(values):
    return lax.rsqrt(jnp.mean(values * values, axis=-1, keepdims=True) + EPSILON)


def norm_back(values, inv_rms, gain_vector, grad_rows):
    weighted = grad_rows * gain_vector
    inner = jnp.mean(weighted * values, axis=-1, keepdims=True)
    value_grad = inv_rms * weighted - values * (inv_rms * inv_rms * inv_rms) * inner
    return (value_grad, jnp.sum(grad_rows * values * inv_rms, axis=0))


def rope_tables(length, head_dim):
    half_size = head_dim // 2
    freqs = 10000.0 ** (-(jnp.arange(half_size, dtype=jnp.float32) * 2.0) / head_dim)
    angles = jnp.arange(length, dtype=jnp.float32)[:, None] * freqs[None, :]
    return (jnp.cos(angles), jnp.sin(angles))


def rotate(values, cosine_table, sine_table, direction):
    half_size = values.shape[-1] // 2
    first_half = values[..., :half_size]
    second_half = values[..., half_size:]
    cosine_part = cosine_table[:, None, :]
    sine_part = sine_table[:, None, :] * direction
    return jnp.concatenate(
        [
            first_half * cosine_part - second_half * sine_part,
            second_half * cosine_part + first_half * sine_part,
        ],
        axis=-1,
    )


def attention_probs(grouped, key_rows, allowed, head_dim):
    scores = jnp.einsum(
        "qngd,knd->ngqk", grouped, key_rows, preferred_element_type=jnp.float32
    ) * head_dim ** (-0.5)
    return jnp.where(allowed, scores, -1e30)


def on_device(
    hidden_in,
    segment_ids,
    expert_ids,
    attn_gain,
    w_query,
    w_key,
    w_value,
    w_out,
    ffn_gain,
    router,
    w_gate,
    w_up,
    w_down,
    grad_out,
):
    f32 = jnp.float32
    bf16 = jnp.bfloat16
    length, model_width = hidden_in.shape
    head_dim = HD
    head_count = w_query.shape[1] // head_dim
    kv_count = w_key.shape[1] // head_dim
    group_size = head_count // kv_count
    experts = router.shape[1]
    top_count = expert_ids.shape[1]
    slot_count = min(length, 2 * length * top_count // experts)
    inputs = hidden_in.astype(f32)
    scale_one = norm_scale(inputs)
    normed = (inputs * scale_one * attn_gain).astype(bf16)
    query_pre = jnp.dot(normed, w_query, preferred_element_type=f32)
    key_pre = jnp.dot(normed, w_key, preferred_element_type=f32)
    value_pre = jnp.dot(normed, w_value, preferred_element_type=f32)
    cosine_table, sine_table = rope_tables(length, head_dim)
    query_rows = rotate(
        query_pre.reshape(length, head_count, head_dim), cosine_table, sine_table, 1.0
    ).astype(bf16)
    key_rows = rotate(
        key_pre.reshape(length, kv_count, head_dim), cosine_table, sine_table, 1.0
    ).astype(bf16)
    value_rows = value_pre.astype(bf16).reshape(length, kv_count, head_dim)
    grouped = query_rows.reshape(length, kv_count, group_size, head_dim)
    segments = segment_ids[0]
    places = jnp.arange(length, dtype=jnp.int32)
    allowed = (segments[:, None] == segments[None, :]) & (places[:, None] >= places[None, :])
    scores = attention_probs(grouped, key_rows, allowed, head_dim)
    row_max = jnp.max(scores, axis=-1, keepdims=True)
    log_total = row_max + jnp.log(jnp.sum(jnp.exp(scores - row_max), axis=-1, keepdims=True))
    weights_prob = jnp.exp(scores - log_total)
    attended = jnp.einsum(
        "ngqk,knd->qngd", weights_prob.astype(bf16), value_rows, preferred_element_type=f32
    )
    attended = attended.reshape(length, head_count * head_dim).astype(bf16)
    mixed_rows = inputs + jnp.dot(attended, w_out, preferred_element_type=f32)
    scale_two = norm_scale(mixed_rows)
    ffn_normed = (mixed_rows * scale_two * ffn_gain).astype(bf16)
    logits = jnp.dot(ffn_normed, router, preferred_element_type=f32)
    chosen = jnp.take_along_axis(logits, expert_ids, axis=1)
    gate_probs = jax.nn.softmax(chosen, axis=-1)
    picked = expert_ids[:, :, None] == jnp.arange(experts, dtype=jnp.int32)[None, None, :]
    member = jnp.any(picked, axis=1)
    ranks = jnp.cumsum(member.astype(jnp.int32), axis=0) - 1
    slot_of = jnp.sum(jnp.where(picked, ranks[:, None, :], 0), axis=2)
    flat_slot = (expert_ids * slot_count + slot_of).reshape(-1)
    token_of_copy = jnp.repeat(jnp.arange(length, dtype=jnp.int32), top_count)
    send_index = (
        jnp.full((experts * slot_count,), length, jnp.int32).at[flat_slot].set(token_of_copy)
    )
    padded = jnp.concatenate([ffn_normed, jnp.zeros((1, model_width), bf16)], axis=0)
    outgoing = padded[send_index].reshape(experts, slot_count, model_width)
    incoming = lax.all_to_all(outgoing, "wide", split_axis=0, concat_axis=0, tiled=True)
    rows_in = incoming.reshape(-1, model_width)
    full_gate, full_up, full_down = (
        lax.all_gather(w_gate, "narrow", axis=2, tiled=True),
        lax.all_gather(w_up, "narrow", axis=2, tiled=True),
        lax.all_gather(w_down, "narrow", axis=1, tiled=True),
    )
    gate_act = jnp.dot(rows_in, full_gate[0], preferred_element_type=f32)
    up_act = jnp.dot(rows_in, full_up[0], preferred_element_type=f32)
    hidden_act = (jax.nn.silu(gate_act) * up_act).astype(bf16)
    outputs = jnp.dot(hidden_act, full_down[0], preferred_element_type=f32).astype(bf16)
    returned = lax.all_to_all(
        outputs.reshape(experts, slot_count, model_width),
        "wide",
        split_axis=0,
        concat_axis=0,
        tiled=True,
    )
    gathered = returned.reshape(-1, model_width)[flat_slot].reshape(length, top_count, model_width)
    moe_rows = jnp.sum(gate_probs[:, :, None] * gathered.astype(f32), axis=1)
    hidden_out = (mixed_rows + moe_rows).astype(bf16)
    cotangent = grad_out.astype(f32)
    gate_grads = jnp.einsum("sd,skd->sk", grad_out, gathered, preferred_element_type=f32)
    chosen_grads = gate_probs * (
        gate_grads - jnp.sum(gate_probs * gate_grads, axis=-1, keepdims=True)
    )
    logit_grads = jnp.sum(jnp.where(picked, chosen_grads[:, :, None], 0.0), axis=1).astype(bf16)
    router_grad = jnp.einsum("sd,se->de", ffn_normed, logit_grads, preferred_element_type=f32)
    normed_two_grad = jnp.einsum("se,de->sd", logit_grads, router, preferred_element_type=f32)
    slot_gates = jnp.zeros((experts * slot_count,), f32).at[flat_slot].set(gate_probs.reshape(-1))
    padded_grad = jnp.concatenate([grad_out, jnp.zeros((1, model_width), bf16)], axis=0)
    out_grads = (slot_gates[:, None] * padded_grad[send_index].astype(f32)).astype(bf16)
    grads_in = lax.all_to_all(
        out_grads.reshape(experts, slot_count, model_width),
        "wide",
        split_axis=0,
        concat_axis=0,
        tiled=True,
    )
    grads_in = grads_in.reshape(-1, model_width)
    hidden_grad = jnp.einsum("rd,fd->rf", grads_in, full_down[0], preferred_element_type=f32)
    down_w_grad = jnp.einsum("rf,rd->fd", hidden_act, grads_in, preferred_element_type=f32)
    sigmoid_gate = jax.nn.sigmoid(gate_act)
    gate_grad = (
        hidden_grad * up_act * sigmoid_gate * (1.0 + gate_act * (1.0 - sigmoid_gate))
    ).astype(bf16)
    up_grad = (hidden_grad * gate_act * sigmoid_gate).astype(bf16)
    gate_w_grad = jnp.einsum("rd,rf->df", rows_in, gate_grad, preferred_element_type=f32)
    up_w_grad = jnp.einsum("rd,rf->df", rows_in, up_grad, preferred_element_type=f32)
    copy_grads = (
        jnp.einsum("rf,df->rd", gate_grad, full_gate[0], preferred_element_type=f32)
        + jnp.einsum("rf,df->rd", up_grad, full_up[0], preferred_element_type=f32)
    ).astype(bf16)
    gate_w_grad, up_w_grad, down_w_grad = (
        lax.psum_scatter(
            gate_w_grad[None].astype(jnp.bfloat16), "narrow", scatter_dimension=2, tiled=True
        ).astype(jnp.float32),
        lax.psum_scatter(
            up_w_grad[None].astype(jnp.bfloat16), "narrow", scatter_dimension=2, tiled=True
        ).astype(jnp.float32),
        lax.psum_scatter(
            down_w_grad[None].astype(jnp.bfloat16), "narrow", scatter_dimension=1, tiled=True
        ).astype(jnp.float32),
    )
    copy_back = lax.all_to_all(
        copy_grads.reshape(experts, slot_count, model_width),
        "wide",
        split_axis=0,
        concat_axis=0,
        tiled=True,
    )
    copy_rows_back = copy_back.reshape(-1, model_width)[flat_slot].reshape(
        length, top_count, model_width
    )
    normed_two_grad = normed_two_grad + jnp.sum(copy_rows_back.astype(f32), axis=1)
    mixed_part, ffn_gain_grad = norm_back(mixed_rows, scale_two, ffn_gain, normed_two_grad)
    mixed_grad = cotangent + mixed_part
    branch_grad = mixed_grad.astype(bf16)
    out_w_grad = jnp.einsum("sh,sd->hd", attended, branch_grad, preferred_element_type=f32)
    attended_grad = jnp.einsum("sd,hd->sh", branch_grad, w_out, preferred_element_type=f32).astype(
        bf16
    )
    attended_grad = attended_grad.reshape(length, kv_count, group_size, head_dim)
    scores = attention_probs(grouped, key_rows, allowed, head_dim)
    weights_prob = jnp.exp(scores - log_total)
    value_grad = jnp.einsum(
        "ngqk,qngd->knd", weights_prob.astype(bf16), attended_grad, preferred_element_type=f32
    )
    prob_grad = jnp.einsum("qngd,knd->ngqk", attended_grad, value_rows, preferred_element_type=f32)
    score_grad = (
        weights_prob * (prob_grad - jnp.sum(weights_prob * prob_grad, axis=-1, keepdims=True))
    ).astype(bf16)
    query_grad = jnp.einsum(
        "ngqk,knd->qngd", score_grad, key_rows, preferred_element_type=f32
    ) * head_dim ** (-0.5)
    key_grad = jnp.einsum(
        "ngqk,qngd->knd", score_grad, grouped, preferred_element_type=f32
    ) * head_dim ** (-0.5)
    query_grad = rotate(
        query_grad.reshape(length, head_count, head_dim), cosine_table, sine_table, -1.0
    )
    query_grad = query_grad.reshape(length, -1).astype(bf16)
    key_grad = rotate(key_grad, cosine_table, sine_table, -1.0).reshape(length, -1).astype(bf16)
    value_grad = value_grad.reshape(length, -1).astype(bf16)
    query_w_grad = jnp.einsum("sd,sh->dh", normed, query_grad, preferred_element_type=f32)
    key_w_grad = jnp.einsum("sd,sh->dh", normed, key_grad, preferred_element_type=f32)
    value_w_grad = jnp.einsum("sd,sh->dh", normed, value_grad, preferred_element_type=f32)
    normed_one_grad = (
        jnp.einsum("sh,dh->sd", query_grad, w_query, preferred_element_type=f32)
        + jnp.einsum("sh,dh->sd", key_grad, w_key, preferred_element_type=f32)
        + jnp.einsum("sh,dh->sd", value_grad, w_value, preferred_element_type=f32)
    )
    input_part, attn_gain_grad = norm_back(inputs, scale_one, attn_gain, normed_one_grad)
    grad_in = (mixed_grad + input_part).astype(bf16)
    summed = lax.psum(
        (
            attn_gain_grad,
            query_w_grad,
            key_w_grad,
            value_w_grad,
            out_w_grad,
            ffn_gain_grad,
            router_grad,
        ),
        ("wide", "narrow"),
    )
    return (
        hidden_out,
        grad_in,
        summed[0],
        summed[1],
        summed[2],
        summed[3],
        summed[4],
        summed[5],
        summed[6],
        gate_w_grad,
        up_w_grad,
        down_w_grad,
    )


def solution(mesh):
    return jax.shard_map(
        on_device,
        mesh=mesh,
        in_specs=(
            P(("wide", "narrow"), None),
            P(("wide", "narrow"), None),
            P(("wide", "narrow"), None),
            P(),
            P(),
            P(),
            P(),
            P(),
            P(),
            P(),
            P("wide", None, "narrow"),
            P("wide", None, "narrow"),
            P("wide", "narrow", None),
            P(("wide", "narrow"), None),
        ),
        out_specs=(
            P(("wide", "narrow"), None),
            P(("wide", "narrow"), None),
            P(),
            P(),
            P(),
            P(),
            P(),
            P(),
            P(),
            P("wide", None, "narrow"),
            P("wide", None, "narrow"),
            P("wide", "narrow", None),
        ),
        check_vma=False,
    )
```

profile of v0, /device:TPU:0, one launch (start us, length us, event | category | flops | bytes accessed | tf_op | source)
XLA Modules:
  0.0 2124.6 jit_solution(18212974689426877776)
XLA Ops:
  24.0 8.3 exponential_reduce_fusion
  32.3 8.5 fusion.22
  46.2 15.5 scatter_custom_fusion
  64.7 35.5 %gather_fusion = bf16[8192,1024]{1,0:T(8,128)(2,1)} fusion(bf16[513,1024]{1,0:T(8,128)(2,1)S(1)} %concatenate.31, s32[8192]{0:T(1024)S(1)} %fusion.53), kind=kCustom, calls=%fused_computation | custom fusion | bytes 33587200 | tf_op jit(solution)/shard_map/gather | solution.py:120
  109.9 22.7 %all-gather.4.cloned.1.call-done = bf16[1,1024,512]{2,1,0:T(8,128)(2,1)} async-done(((bf16[1,1024,256]{2,1,0:T(8,128)(2,1)}), bf16[1,1024,512]{2,1,0:T(8,128)(2,1)}) %all-gather.4.cloned.1.call-update) | async-done | bytes 1048592 | tf_op jit(solution)/shard_map/all_gather | solution.py:124
  132.6 271.7 %all-to-all-done = bf16[16,512,1024]{2,1,0:T(8,128)(2,1)} async-done(((bf16[16,512,1024]{2,1,0:T(8,128)(2,1)}), bf16[16,512,1024]{2,1,0:T(8,128)(2,1)}, u32[]{:S(2)}, u32[]{:S(2)}) %all-to-all-start) | async-done | bytes 16777248 | tf_op jit(solution)/shard_map/all_to_all | solution.py:121
  404.3 16.4 fusion.44
  420.8 21.8 %multiply_convert_fusion.2 = (bf16[8192,512]{1,0:T(8,128)(2,1)}, f32[8192,512]{1,0:T(8,128)}) fusion(f32[8192,512]{1,0:T(8,128)} %fusion.44, bf16[8192,1024]{1,0:T(8,128)(2,1)} %bitcast.18, bf16[1,1024,512]{2,1,0:T(8,128)(2,1)} %all-gather.6.cloned.1.call-done), kind=kOutput, calls=%fused_computation.20 | convolution fusion | flops 8615100416 | bytes 59768832 | tf_op jit(solution)/shard_map/dot_general | solution.py:129
  442.6 14.8 convolution_convert_fusion
  457.4 70.6 %all-to-all-start.1 = ((bf16[16,512,1024]{2,1,0:T(8,128)(2,1)}), bf16[16,512,1024]{2,1,0:T(8,128)(2,1)}, u32[]{:S(2)}, u32[]{:S(2)}) async-start(bf16[16,512,1024]{2,1,0:T(8,128)(2,1)} %bitcast.172), calls=%async_computation.1 | async-start | bytes 33554432 | tf_op jit(solution)/shard_map/all_to_all | solution.py:132
  528.7 33.0 %gather_fusion.4 = f32[4096]{0:T(1024)S(1)} fusion(f32[512,16]{0,1:T(8,128)S(1)} %fusion.82, s32[4096]{0:T(1024)S(1)} %reshape.343), kind=kCustom, calls=%fused_computation.4 | custom fusion | bytes 65536 | tf_op jit(solution)/shard_map/jit(take_along_axis)/gather | solution.py:108
  563.3 35.5 %gather_fusion.2 = bf16[8192,1024]{1,0:T(8,128)(2,1)} fusion(bf16[513,1024]{1,0:T(8,128)(2,1)S(1)} %concatenate.32, s32[8192]{0:T(1024)S(1)} %copy-done.42), kind=kCustom, calls=%fused_computation.2 | custom fusion | bytes 33587200 | tf_op jit(solution)/shard_map/gather | solution.py:152
  598.9 225.7 %all-to-all-done.1 = bf16[16,512,1024]{2,1,0:T(8,128)(2,1)} async-done(((bf16[16,512,1024]{2,1,0:T(8,128)(2,1)}), bf16[16,512,1024]{2,1,0:T(8,128)(2,1)}, u32[]{:S(2)}, u32[]{:S(2)}) %all-to-all-start.1) | async-done | bytes 16777248 | tf_op jit(solution)/shard_map/all_to_all | solution.py:132
  824.6 28.9 %gather_fusion.1 = bf16[4096,1024]{1,0:T(8,128)(2,1)} fusion(bf16[8192,1024]{1,0:T(8,128)(2,1)} %bitcast.23, s32[4096]{0:T(1024)S(1)} %broadcast_clamp_fusion), kind=kCustom, calls=%fused_computation.1 | custom fusion | bytes 16793600 | tf_op jit(solution)/shard_map/gather | solution.py:139
  853.5 7.9 fusion.5
  861.9 15.5 scatter_custom_fusion.1
  877.5 9.2 fusion
  886.7 432.1 %all_to_all.20 = bf16[16,512,1024]{2,1,0:T(8,128)(2,1)} all-to-all(bf16[16,512,1024]{2,1,0:T(8,128)(2,1)S(1)} %fusion), channel_id=1, replica_groups=mesh['wide'=16,'narrow'=2] {'wide'}, dimensions={0} | all-to-all | bytes 33554432 | tf_op jit(solution)/shard_map/all_to_all | solution.py:153
  1318.7 28.7 %multiply_convert_fusion = (bf16[8192,512]{1,0:T(8,128)(2,1)}, bf16[8192,512]{1,0:T(8,128)(2,1)}) fusion(f32[8192,512]{1,0:T(8,128)} %fusion.44, f32[8192,512]{1,0:T(8,128)} %get-tuple-element.49, bf16[8192,1024]{1,0:T(8,128)(2,1)} %bitcast.170, bf16[1,512,1024]{2,1,0:T(8,128)(2,1)} %all-gather.8.cloned.1.call-done), kind=kOutput, calls=%fused_computation.17 | convolution fusion | flops 8644460544 | bytes 68157440 | tf_op jit(solution)/shard_map/rd,fd->rf/dot_general | solution.py:161
  1347.4 18.8 fusion.42
  1366.2 23.6 %add_convert_fusion = bf16[8192,1024]{1,0:T(8,128)(2,1)} fusion(f32[8192,1024]{1,0:T(8,128)} %fusion.42, bf16[8192,512]{1,0:T(8,128)(2,1)} %get-tuple-element.25, bf16[1,1024,512]{2,1,0:T(8,128)(2,1)} %all-gather.6.cloned.1.call-done), kind=kOutput, calls=%fused_computation.9 | convolution fusion | flops 8606711808 | bytes 59768832 | tf_op jit(solution)/shard_map/rf,df->rd/dot_general | solution.py:172
  1397.5 9.8 multiply_reduce_fusion
  1407.4 15.6 fusion.27
  1423.1 15.9 fusion.25
  1439.0 15.6 fusion.26
  1454.7 238.4 %all-to-all-done.3 = bf16[16,512,1024]{2,1,0:T(8,128)(2,1)} async-done(((bf16[16,512,1024]{2,1,0:T(8,128)(2,1)}), bf16[16,512,1024]{2,1,0:T(8,128)(2,1)}, u32[]{:S(2)}, u32[]{:S(2)}) %all-to-all-start.3) | async-done | bytes 16777248 | tf_op jit(solution)/shard_map/all_to_all | solution.py:185
  1693.2 29.0 %gather_fusion.3 = bf16[4096,1024]{1,0:T(8,128)(2,1)} fusion(bf16[8192,1024]{1,0:T(8,128)(2,1)} %bitcast.30, s32[4096]{0:T(1024)S(1)} %copy-done.44), kind=kCustom, calls=%fused_computation.3 | custom fusion | bytes 16793600 | tf_op jit(solution)/shard_map/gather | solution.py:192
  1722.2 11.9 convert_reduce_fusion
  1745.3 14.7 fusion.1
  1762.1 11.0 fusion.3
  1817.6 107.0 %all-reduce.2 = (f32[1024]{0:T(1024)}, f32[1024]{0:T(1024)}) all-reduce(f32[1024]{0:T(1024)S(1)} %get-tuple-element.14, f32[1024]{0:T(1024)S(1)} %get-tuple-element.12), channel_id=1, replica_groups=mesh['wide'=16,'narrow'=2] {'wide','narrow'}, use_global_device_ids=true, to_apply=%region_20.21 | all-reduce | flops 2048 | bytes 16384 | tf_op jit(solution)/shard_map/psum | solution.py:235
  1928.4 177.5 %all-reduce.6.cloned.1.call-done = (f32[1024,1024]{1,0:T(8,128)}, f32[1024,512]{1,0:T(8,128)}, f32[1024,512]{1,0:T(8,128)}, f32[1024,1024]{1,0:T(8,128)}, f32[1024,16]{0,1:T(8,128)}) async-done(((f32[1024,1024]{1,0:T(8,128)}, f32[1024,512]{1,0:T(8,128)}, f32[1024,512]{1,0:T(8,128)}, f32[1024,1024]{1,0:T(8,128)}, f32[1024,16]{0,1:T(8,128)}), (f32[1024,1024]{1,0:T(8,128)}, f32[1024,512]{1,0:T(8,128)}, ...) | async-done | bytes 12648464 | tf_op jit(solution)/shard_map/psum | solution.py:235
  (234 shorter events, 117.8 us)
Async XLA Ops:
  7.2 33.7 %copy-start = (bf16[1024,1024]{1,0:T(8,128)(2,1)S(1)}, bf16[1024,1024]{1,0:T(8,128)(2,1)}, u32[]{:S(2)}) copy-start(bf16[1024,1024]{1,0:T(8,128)(2,1)} %param.21) | copy-start | bytes 6291460
  16.5 15.8 copy-start.20
  40.9 21.0 copy-start.54
  44.1 56.1 %copy-start.56 = (f32[512]{0:T(512)}, f32[512]{0:T(512)S(1)}, u32[]{:S(2)}) copy-start(f32[512]{0:T(512)S(1)} %get-tuple-element.40) | copy-start | bytes 6148
  46.0 54.2 %copy-start.48 = (s32[4096,1]{0,1:T(1,128)}, s32[4096,1]{0,1:T(1,128)S(1)}, u32[]{:S(2)}) copy-start(s32[4096,1]{0,1:T(1,128)S(1)} %compare_select_fusion) | copy-start | bytes 49156
  61.8 38.4 %copy-start.41 = (s32[8192]{0:T(1024)}, s32[8192]{0:T(1024)S(1)}, u32[]{:S(2)}) copy-start(s32[8192]{0:T(1024)S(1)} %fusion.53) | copy-start | bytes 98308
  100.2 304.1 %all-to-all-start = ((bf16[16,512,1024]{2,1,0:T(8,128)(2,1)}), bf16[16,512,1024]{2,1,0:T(8,128)(2,1)}, u32[]{:S(2)}, u32[]{:S(2)}) async-start(bf16[16,512,1024]{2,1,0:T(8,128)(2,1)} %bitcast.168), calls=%async_computation | async-start | bytes 33554432 | tf_op jit(solution)/shard_map/all_to_all | solution.py:121
  107.7 24.9 %all-gather.4.cloned.1.call-start = ((), (), s32[]{:S(2)}) async-start(), calls=%async_computation.7 | async-start | bytes 1572864 | tf_op jit(solution)/shard_map/all_gather | solution.py:124
  108.4 312.3 %all-gather.6.cloned.1.call-start = ((), (), s32[]{:S(2)}) async-start(), calls=%async_computation.8 | async-start | bytes 1572864 | tf_op jit(solution)/shard_map/all_gather | solution.py:125
  109.2 333.4 %all-gather.8.cloned.1.call-start = ((), (), s32[]{:S(2)}) async-start(), calls=%async_computation.9 | async-start | bytes 1572864 | tf_op jit(solution)/shard_map/all_gather | solution.py:126
  457.4 70.9 %copy-start.8 = (bf16[512,1024]{1,0:T(8,128)(2,1)S(1)}, bf16[512,1024]{1,0:T(8,128)(2,1)}, u32[]{:S(2)}) copy-start(bf16[512,1024]{1,0:T(8,128)(2,1)} %copy-done.7) | copy-start | bytes 3145732
  457.4 70.9 %copy-start.45 = (bf16[1024,16]{0,1:T(8,128)(2,1)S(1)}, bf16[1024,16]{0,1:T(8,128)(2,1)}, u32[]{:S(2)}) copy-start(bf16[1024,16]{0,1:T(8,128)(2,1)} %param.23) | copy-start | bytes 98308
  457.4 367.2 %all-to-all-start.1 = ((bf16[16,512,1024]{2,1,0:T(8,128)(2,1)}), bf16[16,512,1024]{2,1,0:T(8,128)(2,1)}, u32[]{:S(2)}, u32[]{:S(2)}) async-start(bf16[16,512,1024]{2,1,0:T(8,128)(2,1)} %bitcast.172), calls=%async_computation.1 | async-start | bytes 33554432 | tf_op jit(solution)/shard_map/all_to_all | solution.py:132
  528.7 34.6 %copy-start.42 = (s32[8192]{0:T(1024)S(1)}, s32[8192]{0:T(1024)}, u32[]{:S(2)}) copy-start(s32[8192]{0:T(1024)} %copy-done.41) | copy-start | bytes 98308
  563.3 35.5 %copy-start.49 = (s32[4096,1]{0,1:T(1,128)S(1)}, s32[4096,1]{0,1:T(1,128)}, u32[]{:S(2)}) copy-start(s32[4096,1]{0,1:T(1,128)} %copy-done.48) | copy-start | bytes 49156
  598.9 254.7 %copy-start.43 = (s32[4096]{0:T(1024)}, s32[4096]{0:T(1024)S(1)}, u32[]{:S(2)}) copy-start(s32[4096]{0:T(1024)S(1)} %broadcast_clamp_fusion) | copy-start | bytes 49156
  824.6 28.9 %copy-start.17 = (bf16[512,1024]{1,0:T(8,128)(2,1)S(1)}, bf16[512,1024]{1,0:T(8,128)(2,1)}, u32[]{:S(2)}) copy-start(bf16[512,1024]{1,0:T(8,128)(2,1)} %param.27) | copy-start | bytes 3145732
  1318.7 28.7 %copy-start.62 = (bf16[1,1024,512]{2,1,0:T(8,128)(2,1)S(1)}, bf16[1,1024,512]{2,1,0:T(8,128)(2,1)}, u32[]{:S(2)}) copy-start(bf16[1,1024,512]{2,1,0:T(8,128)(2,1)} %all-gather.4.cloned.1.call-done) | copy-start | bytes 3145732
  1389.8 303.3 %all-to-all-start.3 = ((bf16[16,512,1024]{2,1,0:T(8,128)(2,1)}), bf16[16,512,1024]{2,1,0:T(8,128)(2,1)}, u32[]{:S(2)}, u32[]{:S(2)}) async-start(bf16[16,512,1024]{2,1,0:T(8,128)(2,1)} %bitcast.169), calls=%async_computation.3 | async-start | bytes 33554432 | tf_op jit(solution)/shard_map/all_to_all | solution.py:185
  1396.5 408.3 %reduce-scatter.8.cloned.1.call-start = ((), (), s32[]{:S(2)}) async-start(), calls=%async_computation.12 | async-start | bytes 1572864 | tf_op jit(solution)/shard_map/reduce_scatter | solution.py:181
  1423.0 384.0 %reduce-scatter.4.cloned.1.call-start = ((), (), s32[]{:S(2)}) async-start(), calls=%async_computation.10 | async-start | bytes 1572864 | tf_op jit(solution)/shard_map/reduce_scatter | solution.py:175
  1438.9 254.2 %copy-start.44 = (s32[4096]{0:T(1024)S(1)}, s32[4096]{0:T(1024)}, u32[]{:S(2)}) copy-start(s32[4096]{0:T(1024)} %copy-done.43) | copy-start | bytes 49156
  1439.0 370.1 %reduce-scatter.6.cloned.1.call-start = ((), (), s32[]{:S(2)}) async-start(), calls=%async_computation.11 | async-start | bytes 1572864 | tf_op jit(solution)/shard_map/reduce_scatter | solution.py:178
  1454.7 651.3 %all-reduce.6.cloned.1.call-start = ((), (), s32[]{:S(2)}) async-start(), calls=%async_computation.13 | async-start | bytes 25296896 | tf_op jit(solution)/shard_map/psum | solution.py:235
  1722.2 11.9 copy-start.46
  1722.2 11.9 copy-start.55
  1722.2 11.9 copy-start.57
  1745.3 14.7 slice-start
  1745.3 14.7 slice-start.1
  1745.3 15.6 slice-start.2
  1745.3 16.8 slice-start.3
  1815.0 109.5 %copy-start.59 = (f32[512]{0:T(512)S(1)}, f32[512]{0:T(512)}, u32[]{:S(2)}) copy-start(f32[512]{0:T(512)} %get-tuple-element.37) | copy-start | bytes 6148
  (45 other events, 219.7 us)
Sparse Core Ops, SparseCore 0:
  110.1 22.4 all-gather.3
  134.1 21.2 all-gather.5
  157.0 21.2 all-gather.7
  1423.1 21.6 reduce-scatter.7
  1446.9 20.3 reduce-scatter.3
  1469.4 20.3 reduce-scatter.5
  1804.9 301.0 all-reduce.5
where the time goes:
time: 2130 us; the launch traced here: 2120 us
  waiting for transfers between devices  938 us (44%)
  blocking collectives  539 us (25%)
  matrix products  260 us (12%)
  local copies, waits for them, and re-layouts  215 us (10%)
  starting transfers between devices  85 us (4%)
  other arithmetic  71.7 us (3%)
    all_to_all x1, blocking collectives, on_device(): lax.all_to_all(out_grads.reshape(experts, slot_count, model_width), 'wide...  432 us
    all_to_all x1, waiting for transfers between devices, on_device(): lax.all_to_all(outgoing, 'wide', split_axis=0, concat_axis=0, tiled=True)  272 us
    all_to_all x1, waiting for transfers between devices, on_device(): lax.all_to_all(copy_grads.reshape(experts, slot_count, model_width), 'wid...  238 us
    all_to_all x1, waiting for transfers between devices, on_device(): lax.all_to_all(outputs.reshape(experts, slot_count, model_width), 'wide',...  226 us
    psum x1, waiting for transfers between devices, on_device(): lax.psum((attn_gain_grad, query_w_grad, key_w_grad, value_w_grad, out_w_g...  178 us
    psum x1, blocking collectives, on_device(): lax.psum((attn_gain_grad, query_w_grad, key_w_grad, value_w_grad, out_w_g...  107 us
    all_to_all x1, starting transfers between devices, on_device(): lax.all_to_all(outputs.reshape(experts, slot_count, model_width), 'wide',...  70.6 us
  transfers between devices with their start and end apart: 10, of which 5 were waited for; matrix products, arithmetic and copies ran while one was open for 14% of the time, Pallas kernels for 0%

commit v1 on v0

--- a/solution.py
+++ b/solution.py
@@ -73,8 +73,12 @@
     kv_count = w_key.shape[1] // head_dim
     group_size = head_count // kv_count
     experts = router.shape[1]
-    top_count = expert_ids.shape[1]
-    slot_count = min(length, 2 * length * top_count // experts)
+    rows_grad = lax.all_gather(grad_out, "wide", axis=0, tiled=True)
+    full_gate, full_up, full_down = (
+        lax.all_gather(w_gate, "narrow", axis=2, tiled=True),
+        lax.all_gather(w_up, "narrow", axis=2, tiled=True),
+        lax.all_gather(w_down, "narrow", axis=1, tiled=True),
+    )
     inputs = hidden_in.astype(f32)
     scale_one = norm_scale(inputs)
     normed = (inputs * scale_one * attn_gain).astype(bf16)
@@ -105,59 +109,33 @@
     scale_two = norm_scale(mixed_rows)
     ffn_normed = (mixed_rows * scale_two * ffn_gain).astype(bf16)
     logits = jnp.dot(ffn_normed, router, preferred_element_type=f32)
-    chosen = jnp.take_along_axis(logits, expert_ids, axis=1)
-    gate_probs = jax.nn.softmax(chosen, axis=-1)
     picked = expert_ids[:, :, None] == jnp.arange(experts, dtype=jnp.int32)[None, None, :]
     member = jnp.any(picked, axis=1)
-    ranks = jnp.cumsum(member.astype(jnp.int32), axis=0) - 1
-    slot_of = jnp.sum(jnp.where(picked, ranks[:, None, :], 0), axis=2)
-    flat_slot = (expert_ids * slot_count + slot_of).reshape(-1)
-    token_of_copy = jnp.repeat(jnp.arange(length, dtype=jnp.int32), top_count)
-    send_index = (
-        jnp.full((experts * slot_count,), length, jnp.int32).at[flat_slot].set(token_of_copy)
-    )
-    padded = jnp.concatenate([ffn_normed, jnp.zeros((1, model_width), bf16)], axis=0)
-    outgoing = padded[send_index].reshape(experts, slot_count, model_width)
-    incoming = lax.all_to_all(outgoing, "wide", split_axis=0, concat_axis=0, tiled=True)
-    rows_in = incoming.reshape(-1, model_width)
-    full_gate, full_up, full_down = (
-        lax.all_gather(w_gate, "narrow", axis=2, tiled=True),
-        lax.all_gather(w_up, "narrow", axis=2, tiled=True),
-        lax.all_gather(w_down, "narrow", axis=1, tiled=True),
-    )
+    masked = jnp.where(member, logits, -jnp.inf)
+    powers = jnp.where(member, jnp.exp(masked - jnp.max(masked, axis=-1, keepdims=True)), 0.0)
+    gate_probs = powers / jnp.sum(powers, axis=-1, keepdims=True)
+    row_gates = lax.all_to_all(gate_probs.T, "wide", split_axis=0, concat_axis=0, tiled=True)
+    row_gates = row_gates.reshape(-1, 1)
+    rows_in = lax.all_gather(ffn_normed, "wide", axis=0, tiled=True)
     gate_act = jnp.dot(rows_in, full_gate[0], preferred_element_type=f32)
     up_act = jnp.dot(rows_in, full_up[0], preferred_element_type=f32)
     hidden_act = (jax.nn.silu(gate_act) * up_act).astype(bf16)
     outputs = jnp.dot(hidden_act, full_down[0], preferred_element_type=f32).astype(bf16)
-    returned = lax.all_to_all(
-        outputs.reshape(experts, slot_count, model_width),
-        "wide",
-        split_axis=0,
-        concat_axis=0,
-        tiled=True,
-    )
-    gathered = returned.reshape(-1, model_width)[flat_slot].reshape(length, top_count, model_width)
-    moe_rows = jnp.sum(gate_probs[:, :, None] * gathered.astype(f32), axis=1)
-    hidden_out = (mixed_rows + moe_rows).astype(bf16)
+    moe_rows = lax.psum_scatter(
+        (row_gates * outputs.astype(f32)).astype(bf16), "wide", scatter_dimension=0, tiled=True
+    )
+    hidden_out = (mixed_rows + moe_rows.astype(f32)).astype(bf16)
     cotangent = grad_out.astype(f32)
-    gate_grads = jnp.einsum("sd,skd->sk", grad_out, gathered, preferred_element_type=f32)
-    chosen_grads = gate_probs * (
-        gate_grads - jnp.sum(gate_probs * gate_grads, axis=-1, keepdims=True)
-    )
-    logit_grads = jnp.sum(jnp.where(picked, chosen_grads[:, :, None], 0.0), axis=1).astype(bf16)
+    gate_dots = jnp.sum(outputs.astype(f32) * rows_grad.astype(f32), axis=-1)
+    gate_grads = lax.all_to_all(
+        gate_dots.reshape(experts, length), "wide", split_axis=0, concat_axis=0, tiled=True
+    ).T
+    logit_grads = (
+        gate_probs * (gate_grads - jnp.sum(gate_probs * gate_grads, axis=-1, keepdims=True))
+    ).astype(bf16)
     router_grad = jnp.einsum("sd,se->de", ffn_normed, logit_grads, preferred_element_type=f32)
     normed_two_grad = jnp.einsum("se,de->sd", logit_grads, router, preferred_element_type=f32)
-    slot_gates = jnp.zeros((experts * slot_count,), f32).at[flat_slot].set(gate_probs.reshape(-1))
-    padded_grad = jnp.concatenate([grad_out, jnp.zeros((1, model_width), bf16)], axis=0)
-    out_grads = (slot_gates[:, None] * padded_grad[send_index].astype(f32)).astype(bf16)
-    grads_in = lax.all_to_all(
-        out_grads.reshape(experts, slot_count, model_width),
-        "wide",
-        split_axis=0,
-        concat_axis=0,
-        tiled=True,
-    )
-    grads_in = grads_in.reshape(-1, model_width)
+    grads_in = (row_gates * rows_grad.astype(f32)).astype(bf16)
     hidden_grad = jnp.einsum("rd,fd->rf", grads_in, full_down[0], preferred_element_type=f32)
     down_w_grad = jnp.einsum("rf,rd->fd", hidden_act, grads_in, preferred_element_type=f32)
     sigmoid_gate = jax.nn.sigmoid(gate_act)
@@ -171,6 +149,7 @@
         jnp.einsum("rf,df->rd", gate_grad, full_gate[0], preferred_element_type=f32)
         + jnp.einsum("rf,df->rd", up_grad, full_up[0], preferred_element_type=f32)
     ).astype(bf16)
+    rows_back = lax.psum_scatter(copy_grads, "wide", scatter_dimension=0, tiled=True)
     gate_w_grad, up_w_grad, down_w_grad = (
         lax.psum_scatter(
             gate_w_grad[None].astype(jnp.bfloat16), "narrow", scatter_dimension=2, tiled=True
@@ -182,17 +161,7 @@
             down_w_grad[None].astype(jnp.bfloat16), "narrow", scatter_dimension=1, tiled=True
         ).astype(jnp.float32),
     )
-    copy_back = lax.all_to_all(
-        copy_grads.reshape(experts, slot_count, model_width),
-        "wide",
-        split_axis=0,
-        concat_axis=0,
-        tiled=True,
-    )
-    copy_rows_back = copy_back.reshape(-1, model_width)[flat_slot].reshape(
-        length, top_count, model_width
-    )
-    normed_two_grad = normed_two_grad + jnp.sum(copy_rows_back.astype(f32), axis=1)
+    normed_two_grad = normed_two_grad + rows_back.astype(f32)
     mixed_part, ffn_gain_grad = norm_back(mixed_rows, scale_two, ffn_gain, normed_two_grad)
     mixed_grad = cotangent + mixed_part
     branch_grad = mixed_grad.astype(bf16)
@@ -232,17 +201,29 @@
     )
     input_part, attn_gain_grad = norm_back(inputs, scale_one, attn_gain, normed_one_grad)
     grad_in = (mixed_grad + input_part).astype(bf16)
-    summed = lax.psum(
-        (
-            attn_gain_grad,
-            query_w_grad,
-            key_w_grad,
-            value_w_grad,
-            out_w_grad,
-            ffn_gain_grad,
-            router_grad,
-        ),
-        ("wide", "narrow"),
+    small = jnp.concatenate(
+        [
+            attn_gain_grad.reshape(-1, 128),
+            ffn_gain_grad.reshape(-1, 128),
+            router_grad.reshape(-1, 128),
+        ],
+        axis=0,
+    )
+    everywhere = ("wide", "narrow")
+    columns = jnp.concatenate([query_w_grad, key_w_grad, value_w_grad, out_w_grad], axis=1)
+    shares = lax.psum_scatter(columns.astype(bf16), everywhere, scatter_dimension=0, tiled=True)
+    columns = lax.all_gather(shares, everywhere, axis=0, tiled=True).astype(f32)
+    small = lax.psum(small, everywhere)
+    gain_rows = model_width // 128
+    query_width, key_width = w_query.shape[1], w_key.shape[1]
+    summed = (
+        small[:gain_rows].reshape(-1),
+        columns[:, :query_width],
+        columns[:, query_width : query_width + key_width],
+        columns[:, query_width + key_width : query_width + 2 * key_width],
+        columns[:, query_width + 2 * key_width :],
+        small[gain_rows : 2 * gain_rows].reshape(-1),
+        small[2 * gain_rows :].reshape(router.shape),
     )
     return (
         hidden_out,

time: 2130 us -> 1270 us (0.60)
  blocking collectives: 539 us -> 9.34 us
  local copies, waits for them, and re-layouts: 215 us -> 30 us
  starting transfers between devices: 85 us -> 8.24 us
  waiting for transfers between devices: 938 us -> 885 us
    all_to_all x3 -> x1, waiting for transfers between devices: 736 us -> 0.01 us  [on_device(): lax.all_to_all(gate_probs.T, 'wide', split_axis=0, concat_axis=0, tiled=T...]
    all_to_all x1, blocking collectives: 432 us -> 9.34 us  [on_device(): lax.all_to_all(gate_dots.reshape(experts, length), 'wide', split_axis=0,...]
    reduce_scatter x0 -> x3, waiting for transfers between devices: none -> 369 us  [the longest x1 177 us: on_device(): lax.psum_scatter((row_gates * outputs.astype(f32)).astype(bf16), 'wide',...]
    all_gather x0 -> x3, waiting for transfers between devices: none -> 317 us  [the longest x1 128 us: on_device(): rows_grad = lax.all_gather(grad_out, 'wide', axis=0, tiled=True)]
    gather x9 -> x0, local copies, waits for them, and re-layouts: 162 us -> none  [the longest x1 35.5 us: on_device(): outgoing = padded[send_index].reshape(experts, slot_count, model_width)]
    psum x1 -> x0, blocking collectives: 107 us -> none  [on_device(): lax.psum((attn_gain_grad, query_w_grad, key_w_grad, value_w_grad, out_w_g...]
    all_to_all x3 -> x1, starting transfers between devices: 84.7 us -> 7.32 us  [on_device(): lax.all_to_all(gate_probs.T, 'wide', split_axis=0, concat_axis=0, tiled=T...]
    psum x1, waiting for transfers between devices: 178 us -> 120 us  [on_device(): small = lax.psum(small, everywhere)]
  transfers between devices with their start and end apart: 10 -> 14, of which waited for: 5 -> 12; matrix products, arithmetic and copies ran while one was open for 14% -> 14% of each run, Pallas kernels for 0% -> 0%
where the time goes in v1:
time: 1270 us; the launch traced here: 1260 us
  waiting for transfers between devices  885 us (70%)
  matrix products  257 us (20%)
  other arithmetic  56.9 us (4%)
  local copies, waits for them, and re-layouts  30 us (2%)
  between operations  15 us (1%)
    reduce_scatter x1, waiting for transfers between devices, on_device(): lax.psum_scatter((row_gates * outputs.astype(f32)).astype(bf16), 'wide',...  177 us
    reduce_scatter x1, waiting for transfers between devices, on_device(): lax.psum_scatter(copy_grads, 'wide', scatter_dimension=0, tiled=True)  141 us
    all_gather x1, waiting for transfers between devices, on_device(): rows_grad = lax.all_gather(grad_out, 'wide', axis=0, tiled=True)  128 us
    psum x1, waiting for transfers between devices, on_device(): small = lax.psum(small, everywhere)  120 us
    all_gather x1, waiting for transfers between devices, on_device(): rows_in = lax.all_gather(ffn_normed, 'wide', axis=0, tiled=True)  117 us
    all_gather x1, waiting for transfers between devices, on_device(): columns = lax.all_gather(shares, everywhere, axis=0, tiled=True).astype(f32)  71.2 us
    reduce_scatter x1, waiting for transfers between devices, on_device(): lax.psum_scatter(columns.astype(bf16), everywhere, scatter_dimension=0, t...  51.4 us
    dot_general x1, matrix products, on_device(): jnp.einsum('rd,fd->rf', grads_in, full_down[0], preferred_element_type=f32)  32.4 us
  transfers between devices with their start and end apart: 14, of which 12 were waited for; matrix products, arithmetic and copies ran while one was open for 14% of the time, Pallas kernels for 0%

profile of v1, /device:TPU:0, one launch (start us, length us, event | category | flops | bytes accessed | tf_op | source)
XLA Modules:
  0.0 1261.9 jit_solution(9160530426510023094)
XLA Ops:
  17.5 7.6 fusion.83
  25.2 8.2 exponential_reduce_fusion
  33.4 8.5 fusion.25
  51.4 7.3 all-to-all-start
  58.8 116.9 %all-gather.7.cloned.1.call-done = bf16[8192,1024]{1,0:T(8,128)(2,1)} async-done(((bf16[512,1024]{1,0:T(8,128)(2,1)}), bf16[8192,1024]{1,0:T(8,128)(2,1)}) %all-gather.7.cloned.1.call-update) | async-done | bytes 16777232 | tf_op jit(solution)/shard_map/all_gather | solution.py:119
  175.7 16.1 %fusion.47 = f32[8192,512]{1,0:T(8,128)} fusion(bf16[8192,1024]{1,0:T(8,128)(2,1)} %all-gather.7.cloned.1.call-done, bf16[1,1024,512]{2,1,0:T(8,128)(2,1)} %all-gather.11.cloned.1.call-done), kind=kOutput, calls=%fused_computation.74 | convolution fusion | flops 8589934592 | bytes 34603008 | tf_op jit(solution)/shard_map/dot_general | solution.py:121
  191.9 4.8 all-gather.9.cloned.1.call-done
  196.7 16.0 %fusion.51 = f32[8192,512]{1,0:T(8,128)} fusion(bf16[8192,1024]{1,0:T(8,128)(2,1)} %all-gather.7.cloned.1.call-done, bf16[1,1024,512]{2,1,0:T(8,128)(2,1)} %all-gather.9.cloned.1.call-done), kind=kOutput, calls=%fused_computation.78 | convolution fusion | flops 8589934592 | bytes 34603008 | tf_op jit(solution)/shard_map/dot_general | solution.py:120
  212.7 6.7 all-gather.13.cloned.1.call-done
  219.4 128.5 %all-gather.15.cloned.1.call-done = bf16[8192,1024]{1,0:T(8,128)(2,1)} async-done(((bf16[512,1024]{1,0:T(8,128)(2,1)}), bf16[8192,1024]{1,0:T(8,128)(2,1)}) %all-gather.15.cloned.1.call-update) | async-done | bytes 16777232 | tf_op jit(solution)/shard_map/all_gather | solution.py:76
  347.9 32.4 %multiply_convert_fusion = (bf16[8192,512]{1,0:T(8,128)(2,1)}, bf16[8192,512]{1,0:T(8,128)(2,1)}, bf16[8192,512]{1,0:T(8,128)(2,1)}) fusion(f32[8192,512]{1,0:T(8,128)} %fusion.51, f32[8192,512]{1,0:T(8,128)} %fusion.47, bf16[1,512,1024]{2,1,0:T(8,128)(2,1)} %all-gather.13.cloned.1.call-done, bf16[8192,1024]{1,0:T(8,128)(2,1)} %all-gather.15.cloned.1.call-done, ...), kind=kOutput, calls=%fused_computation.13 | convolution fusion | flops 8682209280 | bytes 76578816 | tf_op jit(solution)/shard_map/rd,fd->rf/dot_general | solution.py:139
  380.3 18.8 %fusion.49 = f32[8192,1024]{1,0:T(8,128)} fusion(bf16[8192,512]{1,0:T(8,128)(2,1)} %get-tuple-element.65, bf16[1,1024,512]{2,1,0:T(8,128)(2,1)S(1)} %copy-done.62), kind=kOutput, calls=%fused_computation.76 | convolution fusion | flops 8589934592 | bytes 42991616 | tf_op jit(solution)/shard_map/rf,df->rd/dot_general | solution.py:149
  399.2 21.5 %add_convert_fusion = bf16[8192,1024]{1,0:T(8,128)(2,1)} fusion(f32[8192,1024]{1,0:T(8,128)} %fusion.49, bf16[8192,512]{1,0:T(8,128)(2,1)} %get-tuple-element.64, bf16[1,1024,512]{2,1,0:T(8,128)(2,1)S(1)} %copy-done.60), kind=kOutput, calls=%fused_computation.6 | convolution fusion | flops 8606711808 | bytes 59768832 | tf_op jit(solution)/shard_map/rf,df->rd/dot_general | solution.py:150
  421.9 23.6 %fusion.1 = (f32[8192]{0:T(1024)S(1)}, bf16[8192,1024]{1,0:T(8,128)(2,1)}) fusion(bf16[8192,1024]{1,0:T(8,128)(2,1)} %all-gather.15.cloned.1.call-done, f32[8192]{0:T(1024)S(1)} %bitcast.185, bf16[8192,512]{1,0:T(8,128)(2,1)} %get-tuple-element.66, bf16[1,512,1024]{2,1,0:T(8,128)(2,1)S(1)} %copy-done.61), kind=kOutput, calls=%fused_computation.4 | convolution fusion | flops 8648646656 | bytes 43057152 | tf_op jit(solution)/shard_map/dot_general | solution.py:123
  445.7 9.3 all_to_all.21
  455.1 141.3 %reduce-scatter.11.cloned.1.call-done = bf16[512,1024]{1,0:T(8,128)(2,1)} async-done(((bf16[8192,1024]{1,0:T(8,128)(2,1)}), bf16[512,1024]{1,0:T(8,128)(2,1)}) %reduce-scatter.11.cloned.1.call-update) | async-done | bytes 1048592 | tf_op jit(solution)/shard_map/reduce_scatter | solution.py:152
  600.4 176.6 %reduce-scatter.9.cloned.1.call-done = bf16[512,1024]{1,0:T(8,128)(2,1)} async-done(((bf16[8192,1024]{1,0:T(8,128)(2,1)}), bf16[512,1024]{1,0:T(8,128)(2,1)}) %reduce-scatter.9.cloned.1.call-update) | async-done | bytes 1048592 | tf_op jit(solution)/shard_map/reduce_scatter | solution.py:124
  788.6 9.4 fusion.41
  798.0 16.0 %fusion.3 = (f32[8,2,512]{2,1,0:T(2,128)}, f32[8,512,512,2]{2,1,3,0:T(8,128)}) fusion(f32[8,2,512,512]{2,3,1,0:T(8,128)} %get-tuple-element.93, f32[8,2,512]{2,1,0:T(2,128)S(1)} %bitcast.181, bf16[512,8,64,1]{0,2,3,1:T(8,128)(2,1)} %bitcast.165, bf16[512,8,2,64]{0,3,2,1:T(8,128)(2,1)} %bitcast.160), kind=kOutput, calls=%fused_computation.9 | convolution fusion | flops 549445632 | bytes 35192832 | tf_op jit(solution)/shard_map/qngd,knd->ngqk/dot_general | solution.py:178
  814.1 11.3 fusion.5
  825.4 6.3 fusion.37
  839.1 15.2 %pad_maximum_fusion = bf16[1024,3072]{0,1:T(8,128)(2,1)} fusion(bf16[1024,1024]{0,1:T(8,128)(2,1)S(1)} %copy-done.20, bf16[1024,512]{0,1:T(8,128)(2,1)S(1)} %convolution_convert_fusion.6, bf16[1024,512]{0,1:T(8,128)(2,1)S(1)} %convolution_convert_fusion.7, bf16[1024,1024]{0,1:T(8,128)(2,1)S(1)} %convolution_convert_fusion.1), kind=kLoop, calls=%fused_computation.23 | loop fusion | flops 25165824 | bytes 12582912 | tf_op jit(solution)/shard_map/concatenate | solution.py:213
  854.3 8.7 copy.93
  863.1 15.7 %fusion.32 = bf16[1,1024,512]{2,1,0:T(8,128)(2,1)} fusion(bf16[8192,1024]{1,0:T(8,128)(2,1)} %all-gather.7.cloned.1.call-done, bf16[8192,512]{1,0:T(8,128)(2,1)} %get-tuple-element.64), kind=kOutput, calls=%fused_computation.61 | convolution fusion | flops 8590458880 | bytes 26214400 | tf_op jit(solution)/shard_map/rd,rf->df/dot_general | solution.py:147
  878.9 16.1 %fusion.31 = bf16[1,1024,512]{2,1,0:T(8,128)(2,1)} fusion(bf16[8192,1024]{1,0:T(8,128)(2,1)} %all-gather.7.cloned.1.call-done, bf16[8192,512]{1,0:T(8,128)(2,1)} %get-tuple-element.65), kind=kOutput, calls=%fused_computation.60 | convolution fusion | flops 8590458880 | bytes 26214400 | tf_op jit(solution)/shard_map/rd,rf->df/dot_general | solution.py:146
  895.3 18.9 %fusion.38 = bf16[1,512,1024]{2,1,0:T(8,128)(2,1)} fusion(bf16[8192,512]{1,0:T(8,128)(2,1)} %get-tuple-element.66, bf16[8192,1024]{1,0:T(8,128)(2,1)} %all-gather.15.cloned.1.call-done, f32[8192]{0:T(1024)S(1)} %bitcast.186), kind=kOutput, calls=%fused_computation.66 | convolution fusion | flops 8615624704 | bytes 26247168 | tf_op jit(solution)/shard_map/rf,rd->fd/dot_general | solution.py:140
  925.9 51.4 %reduce-scatter.19.cloned.1.call-done = bf16[32,3072]{1,0:T(8,128)(2,1)} async-done(((bf16[1024,3072]{1,0:T(8,128)(2,1)}), bf16[32,3072]{1,0:T(8,128)(2,1)}) %reduce-scatter.19.cloned.1.call-update) | async-done | bytes 196624 | tf_op jit(solution)/shard_map/reduce_scatter | solution.py:214
  977.3 22.2 %reduce-scatter.15.cloned.1.call-done = bf16[1,1024,256]{2,1,0:T(8,128)(2,1)} async-done(((bf16[1,1024,512]{2,1,0:T(8,128)(2,1)}), bf16[1,1024,256]{2,1,0:T(8,128)(2,1)}) %reduce-scatter.15.cloned.1.call-update) | async-done | bytes 524304 | tf_op jit(solution)/shard_map/reduce_scatter | solution.py:157
  1001.6 21.0 %reduce-scatter.13.cloned.1.call-done = bf16[1,1024,256]{2,1,0:T(8,128)(2,1)} async-done(((bf16[1,1024,512]{2,1,0:T(8,128)(2,1)}), bf16[1,1024,256]{2,1,0:T(8,128)(2,1)}) %reduce-scatter.13.cloned.1.call-update) | async-done | bytes 524304 | tf_op jit(solution)/shard_map/reduce_scatter | solution.py:154
  1024.7 21.1 %reduce-scatter.17.cloned.1.call-done = bf16[1,256,1024]{2,1,0:T(8,128)(2,1)} async-done(((bf16[1,512,1024]{2,1,0:T(8,128)(2,1)}), bf16[1,256,1024]{2,1,0:T(8,128)(2,1)}) %reduce-scatter.17.cloned.1.call-update) | async-done | bytes 524304 | tf_op jit(solution)/shard_map/reduce_scatter | solution.py:160
  1051.7 120.4 %all-reduce.2.cloned.1.call-done = f32[144,128]{1,0:T(8,128)} async-done(((f32[144,128]{1,0:T(8,128)}), f32[144,128]{1,0:T(8,128)}) %all-reduce.2.cloned.1.call-update) | async-done | bytes 73744 | tf_op jit(solution)/shard_map/psum | solution.py:216
  1175.3 71.2 %all-gather.17.cloned.1.call-done = bf16[1024,3072]{1,0:T(8,128)(2,1)} async-done(((bf16[32,3072]{1,0:T(8,128)(2,1)}), bf16[1024,3072]{1,0:T(8,128)(2,1)}) %all-gather.17.cloned.1.call-update) | async-done | bytes 6291472 | tf_op jit(solution)/shard_map/all_gather | solution.py:215
  (214 shorter events, 77.4 us)
Async XLA Ops:
  7.2 34.8 %copy-start = (bf16[1024,1024]{1,0:T(8,128)(2,1)S(1)}, bf16[1024,1024]{1,0:T(8,128)(2,1)}, u32[]{:S(2)}) copy-start(bf16[1024,1024]{1,0:T(8,128)(2,1)} %param.21) | copy-start | bytes 6291460
  7.2 51.6 %all-gather.11.cloned.1.call-start = ((), (), s32[]{:S(2)}) async-start(), calls=%async_computation.10 | async-start | bytes 1572864 | tf_op jit(solution)/shard_map/all_gather | solution.py:79
  8.0 167.8 %all-gather.7.cloned.1.call-start = ((), (), s32[]{:S(2)}) async-start(), calls=%async_computation.8 | async-start | bytes 17825792 | tf_op jit(solution)/shard_map/all_gather | solution.py:119
  14.6 18.8 %copy-start.13 = (bf16[512,512]{0,1:T(8,128)(2,1)}, bf16[512,512]{0,1:T(8,128)(2,1)S(1)}, u32[]{:S(2)}) copy-start(bf16[512,512]{0,1:T(8,128)(2,1)S(1)} %convolution_convert_fusion.8) | copy-start | bytes 1572868
  45.9 150.8 %all-gather.9.cloned.1.call-start = ((), (), s32[]{:S(2)}) async-start(), calls=%async_computation.9 | async-start | bytes 1572864 | tf_op jit(solution)/shard_map/all_gather | solution.py:78
  46.7 172.8 %all-gather.13.cloned.1.call-start = ((), (), s32[]{:S(2)}) async-start(), calls=%async_computation.11 | async-start | bytes 1572864 | tf_op jit(solution)/shard_map/all_gather | solution.py:80
  47.2 300.7 %all-gather.15.cloned.1.call-start = ((), (), s32[]{:S(2)}) async-start(), calls=%async_computation.13 | async-start | bytes 17825792 | tf_op jit(solution)/shard_map/all_gather | solution.py:76
  51.4 161.3 %all-to-all-start = ((f32[16,1,512]{2,1,0:T(1,128)}), f32[16,1,512]{2,1,0:T(1,128)S(1)}, u32[]{:S(2)}, u32[]{:S(2)}) async-start(f32[16,1,512]{2,1,0:T(1,128)} %copy.73), calls=%async_computation | async-start | bytes 65536 | tf_op jit(solution)/shard_map/all_to_all | solution.py:117
  58.7 537.7 %reduce-scatter.11.cloned.1.call-start = ((), (), s32[]{:S(2)}) async-start(), calls=%async_computation.14 | async-start | bytes 17825792 | tf_op jit(solution)/shard_map/reduce_scatter | solution.py:152
  212.7 208.1 %copy-start.50 = (f32[16,1,512]{2,1,0:T(1,128)}, f32[16,1,512]{2,1,0:T(1,128)S(1)}, u32[]{:S(2)}) copy-start(f32[16,1,512]{2,1,0:T(1,128)S(1)} %all-to-all-done) | copy-start | bytes 98308
  347.9 32.4 %copy-start.62 = (bf16[1,1024,512]{2,1,0:T(8,128)(2,1)S(1)}, bf16[1,1024,512]{2,1,0:T(8,128)(2,1)}, u32[]{:S(2)}) copy-start(bf16[1,1024,512]{2,1,0:T(8,128)(2,1)} %all-gather.9.cloned.1.call-done) | copy-start | bytes 3145732
  380.3 18.8 %copy-start.60 = (bf16[1,1024,512]{2,1,0:T(8,128)(2,1)S(1)}, bf16[1,1024,512]{2,1,0:T(8,128)(2,1)}, u32[]{:S(2)}) copy-start(bf16[1,1024,512]{2,1,0:T(8,128)(2,1)} %all-gather.11.cloned.1.call-done) | copy-start | bytes 3145732
  420.7 356.3 %reduce-scatter.9.cloned.1.call-start = ((), (), s32[]{:S(2)}) async-start(), calls=%async_computation.12 | async-start | bytes 17825792 | tf_op jit(solution)/shard_map/reduce_scatter | solution.py:124
  445.5 150.9 %copy-start.41 = (bf16[1024,16]{0,1:T(8,128)(2,1)S(1)}, bf16[1024,16]{0,1:T(8,128)(2,1)}, u32[]{:S(2)}) copy-start(bf16[1024,16]{0,1:T(8,128)(2,1)} %param.23) | copy-start | bytes 98308
  445.5 150.8 %copy-start.47 = (f32[1024]{0:T(1024)S(1)}, f32[1024]{0:T(1024)}, u32[]{:S(2)}) copy-start(f32[1024]{0:T(1024)} %param.22) | copy-start | bytes 12292
  445.6 150.8 %copy-start.49 = (f32[512]{0:T(512)S(1)}, f32[512]{0:T(512)}, u32[]{:S(2)}) copy-start(f32[512]{0:T(512)} %copy-done.48) | copy-start | bytes 6148
  445.6 331.4 %copy-start.10 = (bf16[512,1024]{1,0:T(8,128)(2,1)S(1)}, bf16[512,1024]{1,0:T(8,128)(2,1)}, u32[]{:S(2)}) copy-start(bf16[512,1024]{1,0:T(8,128)(2,1)} %param.27) | copy-start | bytes 3145732
  445.6 331.4 %copy-start.58 = (f32[512]{0:T(512)S(1)}, f32[512]{0:T(512)}, u32[]{:S(2)}) copy-start(f32[512]{0:T(512)} %get-tuple-element.87) | copy-start | bytes 6148
  445.6 531.7 %reduce-scatter.19.cloned.1.call-start = ((), (), s32[]{:S(2)}) async-start(), calls=%async_computation.20 | async-start | bytes 6488064 | tf_op jit(solution)/shard_map/reduce_scatter | solution.py:214
  455.0 326.2 %copy-start.36 = (f32[16,1,512]{2,1,0:T(1,128)}, f32[16,1,512]{2,1,0:T(1,128)S(1)}, u32[]{:S(2)}) copy-start(f32[16,1,512]{2,1,0:T(1,128)S(1)} %all_to_all.21) | copy-start | bytes 98308
  788.6 25.4 %slice-start = ((s8[16777216]{0:T(1024)(128)(4,1)}), s8[4194304]{0:T(1024)(128)(4,1)S(1)}, s32[]{:S(2)}) async-start(s8[16777216]{0:T(1024)(128)(4,1)} %bitcast.157), calls=%async_computation.21 | async-start | bytes 8388608
  788.6 25.4 %slice-start.1 = ((s8[16777216]{0:T(1024)(128)(4,1)}), s8[4194304]{0:T(1024)(128)(4,1)S(1)}, s32[]{:S(2)}) async-start(s8[16777216]{0:T(1024)(128)(4,1)} %bitcast.157), calls=%async_computation.22 | async-start | bytes 8388608
  863.0 136.5 %reduce-scatter.15.cloned.1.call-start = ((), (), s32[]{:S(2)}) async-start(), calls=%async_computation.18 | async-start | bytes 1572864 | tf_op jit(solution)/shard_map/reduce_scatter | solution.py:157
  878.8 16.5 %copy-start.51 = (f32[16,1,512]{2,1,0:T(1,128)S(1)}, f32[16,1,512]{2,1,0:T(1,128)}, u32[]{:S(2)}) copy-start(f32[16,1,512]{2,1,0:T(1,128)} %copy-done.50) | copy-start | bytes 98308
  878.8 143.7 %reduce-scatter.13.cloned.1.call-start = ((), (), s32[]{:S(2)}) async-start(), calls=%async_computation.17 | async-start | bytes 1572864 | tf_op jit(solution)/shard_map/reduce_scatter | solution.py:154
  895.0 19.2 %copy-start.4 = (bf16[512,1024]{1,0:T(8,128)(2,1)S(1)}, bf16[512,1024]{1,0:T(8,128)(2,1)}, u32[]{:S(2)}) copy-start(bf16[512,1024]{1,0:T(8,128)(2,1)} %multiply_convert_fusion.3) | copy-start | bytes 3145732
  895.1 19.2 %copy-start.25 = (f32[512,16]{0,1:T(8,128)S(1)}, f32[512,16]{0,1:T(8,128)}, u32[]{:S(2)}) copy-start(f32[512,16]{0,1:T(8,128)} %copy-done.23) | copy-start | bytes 98308
  895.1 19.2 %copy-start.37 = (f32[16,1,512]{2,1,0:T(1,128)S(1)}, f32[16,1,512]{2,1,0:T(1,128)}, u32[]{:S(2)}) copy-start(f32[16,1,512]{2,1,0:T(1,128)} %copy-done.36) | copy-start | bytes 98308
  895.1 150.8 %reduce-scatter.17.cloned.1.call-start = ((), (), s32[]{:S(2)}) async-start(), calls=%async_computation.19 | async-start | bytes 1572864 | tf_op jit(solution)/shard_map/reduce_scatter | solution.py:160
  914.2 257.9 %all-reduce.2.cloned.1.call-start = ((), (), s32[]{:S(2)}) async-start(), calls=%async_computation.15 | async-start | bytes 147456 | tf_op jit(solution)/shard_map/psum | solution.py:216
  924.9 123.0 %copy-start.57 = (f32[512]{0:T(512)S(1)}, f32[512]{0:T(512)}, u32[]{:S(2)}) copy-start(f32[512]{0:T(512)} %get-tuple-element.85) | copy-start | bytes 6148
  925.6 320.8 %all-gather.17.cloned.1.call-start = ((), (), s32[]{:S(2)}) async-start(), calls=%async_computation.16 | async-start | bytes 6488064 | tf_op jit(solution)/shard_map/all_gather | solution.py:215
  (49 other events, 242.4 us)
Sparse Core Ops, SparseCore 0:
  9.6 23.9 all-gather.10
  46.0 129.6 all-gather.6
  177.3 19.4 all-gather.8
  198.1 21.2 all-gather.12
  221.4 126.4 all-gather.14
  420.8 175.5 reduce-scatter.10
  600.5 176.4 reduce-scatter.8
  863.2 114.1 reduce-scatter.18
  980.1 19.3 reduce-scatter.14
  1002.2 20.3 reduce-scatter.12
  1025.4 20.3 reduce-scatter.16
  1051.8 120.2 all-reduce.1
  1175.0 71.3 all-gather.16

commit v2 on v1

--- a/solution.py
+++ b/solution.py
@@ -1,9 +1,11 @@
 import jax
 import jax.numpy as jnp
 from jax import lax
+from jax.sharding import Mesh
 from jax.sharding import PartitionSpec as P
 
 HD = 64
+INNER = 4
 
 
 EPSILON = 1e-05
@@ -73,12 +75,13 @@
     kv_count = w_key.shape[1] // head_dim
     group_size = head_count // kv_count
     experts = router.shape[1]
-    rows_grad = lax.all_gather(grad_out, "wide", axis=0, tiled=True)
-    full_gate, full_up, full_down = (
-        lax.all_gather(w_gate, "narrow", axis=2, tiled=True),
-        lax.all_gather(w_up, "narrow", axis=2, tiled=True),
-        lax.all_gather(w_down, "narrow", axis=1, tiled=True),
-    )
+    outer_count = experts // INNER
+    here = ("inner", "narrow")
+    full_gate = lax.all_gather(w_gate[0], "outer", axis=1, tiled=True)
+    full_up = lax.all_gather(w_up[0], "outer", axis=1, tiled=True)
+    full_down = lax.all_gather(w_down[0], "outer", axis=0, tiled=True)
+    rows_grad = lax.all_gather(grad_out, here, axis=0, tiled=True)
+    part = w_gate.shape[2]
     inputs = hidden_in.astype(f32)
     scale_one = norm_scale(inputs)
     normed = (inputs * scale_one * attn_gain).astype(bf16)
@@ -114,52 +117,57 @@
     masked = jnp.where(member, logits, -jnp.inf)
     powers = jnp.where(member, jnp.exp(masked - jnp.max(masked, axis=-1, keepdims=True)), 0.0)
     gate_probs = powers / jnp.sum(powers, axis=-1, keepdims=True)
-    row_gates = lax.all_to_all(gate_probs.T, "wide", split_axis=0, concat_axis=0, tiled=True)
-    row_gates = row_gates.reshape(-1, 1)
-    rows_in = lax.all_gather(ffn_normed, "wide", axis=0, tiled=True)
-    gate_act = jnp.dot(rows_in, full_gate[0], preferred_element_type=f32)
-    up_act = jnp.dot(rows_in, full_up[0], preferred_element_type=f32)
-    hidden_act = (jax.nn.silu(gate_act) * up_act).astype(bf16)
-    outputs = jnp.dot(hidden_act, full_down[0], preferred_element_type=f32).astype(bf16)
+    gate_table = lax.all_gather(gate_probs.T, here, axis=0, tiled=False)
+    gate_table = gate_table.reshape(-1, outer_count, INNER, length)
+    mine = lax.dynamic_index_in_dim(gate_table, lax.axis_index("inner"), 2, keepdims=False)
+    row_gates = mine.transpose(0, 2, 1).reshape(-1, outer_count)
+    gate_wide = jnp.repeat(row_gates, part, axis=1)
+    rows_in = lax.all_gather(ffn_normed, here, axis=0, tiled=True)
+    gate_act = jnp.dot(rows_in, full_gate, preferred_element_type=f32)
+    up_act = jnp.dot(rows_in, full_up, preferred_element_type=f32)
+    raw_grad = jnp.einsum("rd,fd->rf", rows_grad, full_down, preferred_element_type=f32)
+    sigmoid_gate = jax.nn.sigmoid(gate_act)
+    plain_act = gate_act * sigmoid_gate * up_act
+    hidden_act = (gate_wide * plain_act).astype(bf16)
+    hidden_grad = gate_wide * raw_grad
     moe_rows = lax.psum_scatter(
-        (row_gates * outputs.astype(f32)).astype(bf16), "wide", scatter_dimension=0, tiled=True
+        jnp.dot(hidden_act, full_down, preferred_element_type=f32).astype(bf16),
+        here,
+        scatter_dimension=0,
+        tiled=True,
     )
     hidden_out = (mixed_rows + moe_rows.astype(f32)).astype(bf16)
     cotangent = grad_out.astype(f32)
-    gate_dots = jnp.sum(outputs.astype(f32) * rows_grad.astype(f32), axis=-1)
-    gate_grads = lax.all_to_all(
-        gate_dots.reshape(experts, length), "wide", split_axis=0, concat_axis=0, tiled=True
-    ).T
+    gate_dots = jnp.sum((plain_act * raw_grad).reshape(-1, outer_count, part), axis=-1)
+    lane = jnp.arange(INNER) == lax.axis_index("inner")
+    gate_dots = jnp.where(lane[None, None, :], gate_dots[:, :, None], 0.0).reshape(-1, experts)
+    gate_grads = lax.psum_scatter(gate_dots, here, scatter_dimension=0, tiled=True)
     logit_grads = (
         gate_probs * (gate_grads - jnp.sum(gate_probs * gate_grads, axis=-1, keepdims=True))
     ).astype(bf16)
     router_grad = jnp.einsum("sd,se->de", ffn_normed, logit_grads, preferred_element_type=f32)
     normed_two_grad = jnp.einsum("se,de->sd", logit_grads, router, preferred_element_type=f32)
-    grads_in = (row_gates * rows_grad.astype(f32)).astype(bf16)
-    hidden_grad = jnp.einsum("rd,fd->rf", grads_in, full_down[0], preferred_element_type=f32)
-    down_w_grad = jnp.einsum("rf,rd->fd", hidden_act, grads_in, preferred_element_type=f32)
-    sigmoid_gate = jax.nn.sigmoid(gate_act)
     gate_grad = (
         hidden_grad * up_act * sigmoid_gate * (1.0 + gate_act * (1.0 - sigmoid_gate))
     ).astype(bf16)
     up_grad = (hidden_grad * gate_act * sigmoid_gate).astype(bf16)
+    copy_grads = (
+        jnp.einsum("rf,df->rd", gate_grad, full_gate, preferred_element_type=f32)
+        + jnp.einsum("rf,df->rd", up_grad, full_up, preferred_element_type=f32)
+    ).astype(bf16)
+    rows_back = lax.psum_scatter(copy_grads, here, scatter_dimension=0, tiled=True)
+    down_w_grad = jnp.einsum("rf,rd->fd", hidden_act, rows_grad, preferred_element_type=f32)
     gate_w_grad = jnp.einsum("rd,rf->df", rows_in, gate_grad, preferred_element_type=f32)
     up_w_grad = jnp.einsum("rd,rf->df", rows_in, up_grad, preferred_element_type=f32)
-    copy_grads = (
-        jnp.einsum("rf,df->rd", gate_grad, full_gate[0], preferred_element_type=f32)
-        + jnp.einsum("rf,df->rd", up_grad, full_up[0], preferred_element_type=f32)
-    ).astype(bf16)
-    rows_back = lax.psum_scatter(copy_grads, "wide", scatter_dimension=0, tiled=True)
     gate_w_grad, up_w_grad, down_w_grad = (
-        lax.psum_scatter(
-            gate_w_grad[None].astype(jnp.bfloat16), "narrow", scatter_dimension=2, tiled=True
-        ).astype(jnp.float32),
-        lax.psum_scatter(
-            up_w_grad[None].astype(jnp.bfloat16), "narrow", scatter_dimension=2, tiled=True
-        ).astype(jnp.float32),
-        lax.psum_scatter(
-            down_w_grad[None].astype(jnp.bfloat16), "narrow", scatter_dimension=1, tiled=True
-        ).astype(jnp.float32),
+        lax.psum_scatter(gate_w_grad.astype(bf16), "outer", scatter_dimension=1, tiled=True),
+        lax.psum_scatter(up_w_grad.astype(bf16), "outer", scatter_dimension=1, tiled=True),
+        lax.psum_scatter(down_w_grad.astype(bf16), "outer", scatter_dimension=0, tiled=True),
+    )
+    gate_w_grad, up_w_grad, down_w_grad = (
+        gate_w_grad[None].astype(f32),
+        up_w_grad[None].astype(f32),
+        down_w_grad[None].astype(f32),
     )
     normed_two_grad = normed_two_grad + rows_back.astype(f32)
     mixed_part, ffn_gain_grad = norm_back(mixed_rows, scale_two, ffn_gain, normed_two_grad)
@@ -201,29 +209,28 @@
     )
     input_part, attn_gain_grad = norm_back(inputs, scale_one, attn_gain, normed_one_grad)
     grad_in = (mixed_grad + input_part).astype(bf16)
+    everywhere = ("outer", "inner", "narrow")
     small = jnp.concatenate(
-        [
-            attn_gain_grad.reshape(-1, 128),
-            ffn_gain_grad.reshape(-1, 128),
-            router_grad.reshape(-1, 128),
-        ],
-        axis=0,
-    )
-    everywhere = ("wide", "narrow")
-    columns = jnp.concatenate([query_w_grad, key_w_grad, value_w_grad, out_w_grad], axis=1)
+        [router_grad, attn_gain_grad[:, None], ffn_gain_grad[:, None]], axis=1
+    )
+    small = jnp.pad(small, ((0, 0), (0, 128 - small.shape[1])))
+    columns = jnp.concatenate(
+        [query_w_grad, key_w_grad, value_w_grad, out_w_grad, small], axis=1
+    )
     shares = lax.psum_scatter(columns.astype(bf16), everywhere, scatter_dimension=0, tiled=True)
     columns = lax.all_gather(shares, everywhere, axis=0, tiled=True).astype(f32)
-    small = lax.psum(small, everywhere)
-    gain_rows = model_width // 128
-    query_width, key_width = w_query.shape[1], w_key.shape[1]
+    starts = [0]
+    for width in (w_query.shape[1], w_key.shape[1], w_value.shape[1], model_width, experts, 1, 1):
+        starts.append(starts[-1] + width)
+    pieces = [columns[:, low:high] for low, high in zip(starts[:-1], starts[1:])]
     summed = (
-        small[:gain_rows].reshape(-1),
-        columns[:, :query_width],
-        columns[:, query_width : query_width + key_width],
-        columns[:, query_width + key_width : query_width + 2 * key_width],
-        columns[:, query_width + 2 * key_width :],
-        small[gain_rows : 2 * gain_rows].reshape(-1),
-        small[2 * gain_rows :].reshape(router.shape),
+        pieces[5][:, 0],
+        pieces[0],
+        pieces[1],
+        pieces[2],
+        pieces[3],
+        pieces[6][:, 0],
+        pieces[4],
     )
     return (
         hidden_out,
@@ -242,38 +249,16 @@
 
 
 def solution(mesh):
+    names = ("outer", "inner", "narrow")
+    narrow = mesh.shape["narrow"]
+    cut = Mesh(mesh.devices.reshape(-1, INNER, narrow), names)
+    rows = P(names, None)
+    columns = P(("outer", "inner"), None, "narrow")
+    depths = P(("outer", "inner"), "narrow", None)
     return jax.shard_map(
         on_device,
-        mesh=mesh,
-        in_specs=(
-            P(("wide", "narrow"), None),
-            P(("wide", "narrow"), None),
-            P(("wide", "narrow"), None),
-            P(),
-            P(),
-            P(),
-            P(),
-            P(),
-            P(),
-            P(),
-            P("wide", None, "narrow"),
-            P("wide", None, "narrow"),
-            P("wide", "narrow", None),
-            P(("wide", "narrow"), None),
-        ),
-        out_specs=(
-            P(("wide", "narrow"), None),
-            P(("wide", "narrow"), None),
-            P(),
-            P(),
-            P(),
-            P(),
-            P(),
-            P(),
-            P(),
-            P("wide", None, "narrow"),
-            P("wide", None, "narrow"),
-            P("wide", "narrow", None),
-        ),
+        mesh=cut,
+        in_specs=(rows, rows, rows) + (P(),) * 7 + (columns, columns, depths, rows),
+        out_specs=(rows, rows) + (P(),) * 7 + (columns, columns, depths),
         check_vma=False,
     )

time: 1270 us -> 961 us (0.76)
  waiting for transfers between devices: 885 us -> 592 us
  matrix products: 257 us -> 232 us
    reduce_scatter x5 -> x6, waiting for transfers between devices: 382 us -> 257 us  [the longest x1 71.1 us: on_device(): lax.psum_scatter(jnp.dot(hidden_act, full_down, preferred_element_type=f3...]
    psum x1 -> x0, waiting for transfers between devices: 120 us -> none  [on_device(): small = lax.psum(small, everywhere)]
    all_gather x5, waiting for transfers between devices: 257 us -> 162 us  [the longest x1 54.8 us: on_device(): rows_grad = lax.all_gather(grad_out, here, axis=0, tiled=True)]
    reduce_scatter x1, waiting for transfers between devices: 51.4 us -> 104 us  [on_device(): lax.psum_scatter(columns.astype(bf16), everywhere, scatter_dimension=0, t...]
    all_gather x0 -> x1, blocking collectives: none -> 18.5 us  [on_device(): gate_table = lax.all_gather(gate_probs.T, here, axis=0, tiled=False)]
    reduce_sum x0 -> x1, other arithmetic: none -> 16.8 us  [on_device(): jnp.sum((plain_act * raw_grad).reshape(-1, outer_count, part), axis=-1)]
    dot_general x7, matrix products: 147 us -> 131 us  [the longest x1 34.5 us: on_device(): gate_act = jnp.dot(rows_in, full_gate, preferred_element_type=f32)]
    concatenate x2 -> x1, other arithmetic: 15.8 us -> 0.74 us  [on_device(): jnp.concatenate([query_w_grad, key_w_grad, value_w_grad, out_w_grad, smal...]
  transfers between devices with their start and end apart: 14 -> 13, of which waited for: 12 -> 11; matrix products, arithmetic and copies ran while one was open for 14% -> 19% of each run, Pallas kernels for 0% -> 0%
where the time goes in v2:
time: 961 us; the launch traced here: 957 us
  waiting for transfers between devices  592 us (62%)
  matrix products  232 us (24%)
  other arithmetic  61.9 us (6%)
  local copies, waits for them, and re-layouts  36.6 us (4%)
  blocking collectives  18.5 us (2%)
  between operations  14.7 us (2%)
    reduce_scatter x1, waiting for transfers between devices, on_device(): lax.psum_scatter(columns.astype(bf16), everywhere, scatter_dimension=0, t...  104 us
    reduce_scatter x1, waiting for transfers between devices, on_device(): lax.psum_scatter(jnp.dot(hidden_act, full_down, preferred_element_type=f3...  71.1 us
    all_gather x1, waiting for transfers between devices, on_device(): columns = lax.all_gather(shares, everywhere, axis=0, tiled=True).astype(f32)  66.5 us
    reduce_scatter x1, waiting for transfers between devices, on_device(): lax.psum_scatter(copy_grads, here, scatter_dimension=0, tiled=True)  54.9 us
    all_gather x1, waiting for transfers between devices, on_device(): rows_grad = lax.all_gather(grad_out, here, axis=0, tiled=True)  54.8 us
    reduce_scatter x1, waiting for transfers between devices, on_device(): lax.psum_scatter(up_w_grad.astype(bf16), 'outer', scatter_dimension=1, ti...  44.7 us
    all_gather x1, waiting for transfers between devices, on_device(): rows_in = lax.all_gather(ffn_normed, here, axis=0, tiled=True)  44.6 us
    reduce_scatter x1, waiting for transfers between devices, on_device(): lax.psum_scatter(gate_w_grad.astype(bf16), 'outer', scatter_dimension=1,...  43.7 us
  transfers between devices with their start and end apart: 13, of which 11 were waited for; matrix products, arithmetic and copies ran while one was open for 19% of the time, Pallas kernels for 0%

profile of v2, /device:TPU:0, one launch (start us, length us, event | category | flops | bytes accessed | tf_op | source)
XLA Modules:
  0.0 956.9 jit_solution(1710269945376947296)
XLA Ops:
  16.3 7.7 fusion.75
  24.0 8.3 exponential_reduce_fusion
  33.3 8.7 fusion.31
  48.5 18.5 %all-gather = f32[128,512]{1,0:T(8,128)S(1)} all-gather(f32[16,512]{1,0:T(8,128)S(1)} %fusion.57), channel_id=2, replica_groups=mesh['outer'=4,'inner'=4,'narrow'=2] {'inner','narrow'}, dimensions={0}, use_global_device_ids=true | all-gather | bytes 294912 | tf_op jit(solution)/shard_map/all_gather | solution.py:120
  68.9 44.6 %all-gather.11.cloned.1.call-done = bf16[4096,1024]{1,0:T(8,128)(2,1)} async-done(((bf16[512,1024]{1,0:T(8,128)(2,1)}), bf16[4096,1024]{1,0:T(8,128)(2,1)}) %all-gather.11.cloned.1.call-update) | async-done | bytes 8388624 | tf_op jit(solution)/shard_map/all_gather | solution.py:125
  113.5 16.3 %fusion.23 = f32[4096,1024]{0,1:T(8,128)} fusion(bf16[4096,1024]{1,0:T(8,128)(2,1)} %all-gather.11.cloned.1.call-done, bf16[1,1024,1024]{2,1,0:T(8,128)(2,1)} %all-gather.19.cloned.1.call-done), kind=kOutput, calls=%fused_computation.41 | convolution fusion | flops 8589934592 | bytes 27262976 | tf_op jit(solution)/shard_map/dot_general | solution.py:127
  129.8 30.9 %all-gather.21.cloned.1.call-done = bf16[1,1024,1024]{2,1,0:T(8,128)(2,1)} async-done(((bf16[1,256,1024]{2,1,0:T(8,128)(2,1)}), bf16[1,1024,1024]{2,1,0:T(8,128)(2,1)}) %all-gather.21.cloned.1.call-update) | async-done | bytes 2097168 | tf_op jit(solution)/shard_map/all_gather | solution.py:82
  160.8 54.8 %all-gather.13.cloned.1.call-done = bf16[4096,1024]{1,0:T(8,128)(2,1)} async-done(((bf16[512,1024]{1,0:T(8,128)(2,1)}), bf16[4096,1024]{1,0:T(8,128)(2,1)}) %all-gather.13.cloned.1.call-update) | async-done | bytes 8388624 | tf_op jit(solution)/shard_map/all_gather | solution.py:83
  215.6 16.0 %fusion.19 = f32[4096,1024]{0,1:T(8,128)} fusion(bf16[4096,1024]{1,0:T(8,128)(2,1)} %all-gather.13.cloned.1.call-done, bf16[1,1024,1024]{2,1,0:T(8,128)(2,1)} %all-gather.21.cloned.1.call-done), kind=kOutput, calls=%fused_computation.37 | convolution fusion | flops 8589934592 | bytes 27262976 | tf_op jit(solution)/shard_map/rd,fd->rf/dot_general | solution.py:128
  231.6 31.7 %all-gather.17.cloned.1.call-done = bf16[1,1024,1024]{2,1,0:T(8,128)(2,1)} async-done(((bf16[1,1024,256]{2,1,0:T(8,128)(2,1)}), bf16[1,1024,1024]{2,1,0:T(8,128)(2,1)}) %all-gather.17.cloned.1.call-update) | async-done | bytes 2097168 | tf_op jit(solution)/shard_map/all_gather | solution.py:80
  263.3 34.5 %multiply_convert_fusion = (bf16[4096,1024]{0,1:T(8,128)(2,1)}, bf16[4096,1024]{0,1:T(8,128)(2,1)}, bf16[4096,1024]{0,1:T(8,128)(2,1)}, f32[4096,1024]{0,1:T(8,128)}) fusion(f32[4096,1024]{0,1:T(8,128)} %fusion.19, f32[4096,4]{0,1:T(4,128)S(1)} %bitcast.180, f32[4096,1024]{0,1:T(8,128)} %fusion.23, bf16[4096,1024]{1,0:T(8,128)(2,1)} %all-gather.11.cloned.1.call-done, ...), kind=kOutput, calls=%fused_computation.11 | convolution fusion | flops 8665432064 | bytes 86048768 | tf_op jit(solution)/shard_map/dot_general | solution.py:126
  297.8 16.8 %bitcast_reduce_fusion = f32[4096,4]{0,1:T(4,128)S(1)} fusion(f32[4096,1024]{0,1:T(8,128)} %fusion.19, f32[4096,1024]{0,1:T(8,128)} %fusion.23, f32[4096,1024]{0,1:T(8,128)} %get-tuple-element.108), kind=kLoop, calls=%fused_computation.8 | loop fusion | flops 29343744 | bytes 50397184 | tf_op jit(solution)/shard_map/reduce_sum | solution.py:141
  317.3 16.8 %fusion.25 = f32[4096,1024]{1,0:T(8,128)} fusion(bf16[4096,1024]{0,1:T(8,128)(2,1)} %get-tuple-element.79, bf16[1,1024,1024]{2,1,0:T(8,128)(2,1)} %all-gather.17.cloned.1.call-done), kind=kOutput, calls=%fused_computation.43 | convolution fusion | flops 8589934592 | bytes 27262976 | tf_op jit(solution)/shard_map/rf,df->rd/dot_general | solution.py:155
  334.2 17.2 %add_convert_fusion = bf16[4096,1024]{1,0:T(8,128)(2,1)} fusion(f32[4096,1024]{1,0:T(8,128)} %fusion.25, bf16[4096,1024]{0,1:T(8,128)(2,1)} %get-tuple-element.78, bf16[1,1024,1024]{2,1,0:T(8,128)(2,1)S(1)} %copy-done.41), kind=kOutput, calls=%fused_computation.10 | convolution fusion | flops 8598323200 | bytes 35651584 | tf_op jit(solution)/shard_map/rf,df->rd/dot_general | solution.py:156
  351.5 15.3 %convolution_convert_fusion = bf16[4096,1024]{1,0:T(8,128)(2,1)} fusion(bf16[4096,1024]{0,1:T(8,128)(2,1)} %get-tuple-element.80, bf16[1,1024,1024]{2,1,0:T(8,128)(2,1)} %all-gather.21.cloned.1.call-done), kind=kOutput, calls=%fused_computation.18 | convolution fusion | flops 8594128896 | bytes 18874368 | tf_op jit(solution)/shard_map/dot_general | solution.py:134
  369.3 54.9 %reduce-scatter.14.cloned.1.call-done = bf16[512,1024]{1,0:T(8,128)(2,1)} async-done(((bf16[4096,1024]{1,0:T(8,128)(2,1)}), bf16[512,1024]{1,0:T(8,128)(2,1)}) %reduce-scatter.14.cloned.1.call-update) | async-done | bytes 1048592 | tf_op jit(solution)/shard_map/reduce_scatter | solution.py:158
  428.2 71.1 %reduce-scatter.10.cloned.1.call-done = bf16[512,1024]{1,0:T(8,128)(2,1)} async-done(((bf16[4096,1024]{1,0:T(8,128)(2,1)}), bf16[512,1024]{1,0:T(8,128)(2,1)}) %reduce-scatter.10.cloned.1.call-update) | async-done | bytes 1048592 | tf_op jit(solution)/shard_map/reduce_scatter | solution.py:133
  499.2 4.1 subtract_add_fusion
  507.1 15.2 %fusion.1 = (f32[8,2,512]{2,1,0:T(2,128)S(1)}, f32[8,512,512,2]{2,1,3,0:T(8,128)}) fusion(f32[8,2,512,512]{2,3,1,0:T(8,128)} %get-tuple-element.103, f32[8,2,512]{2,1,0:T(2,128)S(1)} %bitcast.177, bf16[512,8,64,1]{0,2,3,1:T(8,128)(2,1)S(1)} %bitcast.163, bf16[512,8,2,64]{0,3,2,1:T(8,128)(2,1)S(1)} %bitcast.157), kind=kOutput, calls=%fused_computation.5 | convolution fusion | flops 549445632 | bytes 35192832 | tf_op jit(solution)/shard_map/qngd,knd->ngqk/dot_general | solution.py:186
  523.1 8.3 fusion.3
  537.6 6.0 fusion.38
  565.6 9.6 %copy.90 = bf16[1024,3200]{1,0:T(8,128)(2,1)} copy(bf16[1024,3200]{0,1:T(8,128)(2,1)} %fusion.50) | data formatting | bytes 13107200
  575.3 15.2 %convolution_convert_fusion.2 = bf16[1024,1024]{1,0:T(8,128)(2,1)} fusion(bf16[4096,1024]{1,0:T(8,128)(2,1)} %all-gather.11.cloned.1.call-done, bf16[4096,1024]{0,1:T(8,128)(2,1)} %get-tuple-element.78), kind=kOutput, calls=%fused_computation.58 | convolution fusion | flops 8590983168 | bytes 18874368 | tf_op jit(solution)/shard_map/rd,rf->df/dot_general | solution.py:161
  590.6 14.8 %convolution_convert_fusion.3 = bf16[1024,1024]{1,0:T(8,128)(2,1)} fusion(bf16[4096,1024]{1,0:T(8,128)(2,1)} %all-gather.11.cloned.1.call-done, bf16[4096,1024]{0,1:T(8,128)(2,1)} %get-tuple-element.79), kind=kOutput, calls=%fused_computation.59 | convolution fusion | flops 8590983168 | bytes 18874368 | tf_op jit(solution)/shard_map/rd,rf->df/dot_general | solution.py:160
  605.4 15.0 %convolution_convert_fusion.1 = bf16[1024,1024]{1,0:T(8,128)(2,1)} fusion(bf16[4096,1024]{0,1:T(8,128)(2,1)} %get-tuple-element.80, bf16[4096,1024]{1,0:T(8,128)(2,1)} %all-gather.13.cloned.1.call-done), kind=kOutput, calls=%fused_computation.57 | convolution fusion | flops 8590983168 | bytes 18874368 | tf_op jit(solution)/shard_map/rf,rd->fd/dot_general | solution.py:159
  620.5 104.0 %reduce-scatter.22.cloned.1.call-done = bf16[32,3200]{1,0:T(8,128)(2,1)} async-done(((bf16[1024,3200]{1,0:T(8,128)(2,1)}), bf16[32,3200]{1,0:T(8,128)(2,1)}) %reduce-scatter.22.cloned.1.call-update) | async-done | bytes 204816 | tf_op jit(solution)/shard_map/reduce_scatter | solution.py:220
  724.6 44.7 %reduce-scatter.18.cloned.1.call-done = bf16[1024,256]{1,0:T(8,128)(2,1)} async-done(((bf16[1024,1024]{1,0:T(8,128)(2,1)}), bf16[1024,256]{1,0:T(8,128)(2,1)}) %reduce-scatter.18.cloned.1.call-update) | async-done | bytes 524304 | tf_op jit(solution)/shard_map/reduce_scatter | solution.py:164
  771.3 43.7 %reduce-scatter.16.cloned.1.call-done = bf16[1024,256]{1,0:T(8,128)(2,1)} async-done(((bf16[1024,1024]{1,0:T(8,128)(2,1)}), bf16[1024,256]{1,0:T(8,128)(2,1)}) %reduce-scatter.16.cloned.1.call-update) | async-done | bytes 524304 | tf_op jit(solution)/shard_map/reduce_scatter | solution.py:163
  817.1 42.9 %reduce-scatter.20.cloned.1.call-done = bf16[256,1024]{1,0:T(8,128)(2,1)} async-done(((bf16[1024,1024]{1,0:T(8,128)(2,1)}), bf16[256,1024]{1,0:T(8,128)(2,1)}) %reduce-scatter.20.cloned.1.call-update) | async-done | bytes 524304 | tf_op jit(solution)/shard_map/reduce_scatter | solution.py:165
  865.9 66.5 %all-gather.15.cloned.1.call-done = bf16[1024,3200]{1,0:T(8,128)(2,1)} async-done(((bf16[32,3200]{1,0:T(8,128)(2,1)}), bf16[1024,3200]{1,0:T(8,128)(2,1)}) %all-gather.15.cloned.1.call-update) | async-done | bytes 6553616 | tf_op jit(solution)/shard_map/all_gather | solution.py:221
  939.2 6.7 fusion.73
  945.8 4.3 fusion.74
  (180 shorter events, 76.8 us)
Async XLA Ops:
  7.2 34.9 %copy-start = (bf16[1024,1024]{1,0:T(8,128)(2,1)S(1)}, bf16[1024,1024]{1,0:T(8,128)(2,1)}, u32[]{:S(2)}) copy-start(bf16[1024,1024]{1,0:T(8,128)(2,1)} %param.21) | copy-start | bytes 6291460
  7.2 61.7 %all-gather.19.cloned.1.call-start = ((), (), s32[]{:S(2)}) async-start(), calls=%async_computation.17 | async-start | bytes 2621440 | tf_op jit(solution)/shard_map/all_gather | solution.py:81
  7.9 105.6 %all-gather.11.cloned.1.call-start = ((), (), s32[]{:S(2)}) async-start(), calls=%async_computation.7 | async-start | bytes 9437184 | tf_op jit(solution)/shard_map/all_gather | solution.py:125
  10.1 22.3 %copy-start.33 = (f32[512]{0:T(512)}, f32[512]{0:T(512)S(1)}, u32[]{:S(2)}) copy-start(f32[512]{0:T(512)S(1)} %get-tuple-element.96) | copy-start | bytes 6148
  11.0 4.8 copy-start.18
  15.8 8.2 copy-start.14
  15.8 8.2 copy-start.16
  16.0 8.0 copy-start.22
  16.0 8.0 copy-start.24
  24.0 8.4 copy-start.26
  32.4 489.8 %copy-start.28 = (f32[2,8,512]{2,1,0:T(8,128)}, f32[2,8,512]{2,1,0:T(8,128)S(1)}, u32[]{:S(2)}) copy-start(f32[2,8,512]{2,1,0:T(8,128)S(1)} %log_add_fusion) | copy-start | bytes 98308
  33.3 8.7 copy-start.12
  46.0 114.8 %all-gather.21.cloned.1.call-start = ((), (), s32[]{:S(2)}) async-start(), calls=%async_computation.18 | async-start | bytes 2621440 | tf_op jit(solution)/shard_map/all_gather | solution.py:82
  46.7 168.9 %all-gather.13.cloned.1.call-start = ((), (), s32[]{:S(2)}) async-start(), calls=%async_computation.9 | async-start | bytes 9437184 | tf_op jit(solution)/shard_map/all_gather | solution.py:83
  47.3 216.0 %all-gather.17.cloned.1.call-start = ((), (), s32[]{:S(2)}) async-start(), calls=%async_computation.16 | async-start | bytes 2621440 | tf_op jit(solution)/shard_map/all_gather | solution.py:80
  47.9 319.0 %reduce-scatter.12.cloned.1.call-start = ((), (), s32[]{:S(2)}) async-start(), calls=%async_computation.10 | async-start | bytes 294912 | tf_op jit(solution)/shard_map/reduce_scatter | solution.py:144
  317.3 107.0 %reduce-scatter.14.cloned.1.call-start = ((), (), s32[]{:S(2)}) async-start(), calls=%async_computation.11 | async-start | bytes 9437184 | tf_op jit(solution)/shard_map/reduce_scatter | solution.py:158
  317.3 16.9 %copy-start.41 = (bf16[1,1024,1024]{2,1,0:T(8,128)(2,1)S(1)}, bf16[1,1024,1024]{2,1,0:T(8,128)(2,1)}, u32[]{:S(2)}) copy-start(bf16[1,1024,1024]{2,1,0:T(8,128)(2,1)} %all-gather.19.cloned.1.call-done) | copy-start | bytes 6291460
  351.4 147.8 %reduce-scatter.10.cloned.1.call-start = ((), (), s32[]{:S(2)}) async-start(), calls=%async_computation.8 | async-start | bytes 9437184 | tf_op jit(solution)/shard_map/reduce_scatter | solution.py:133
  366.8 357.7 %reduce-scatter.22.cloned.1.call-start = ((), (), s32[]{:S(2)}) async-start(), calls=%async_computation.19 | async-start | bytes 6758400 | tf_op jit(solution)/shard_map/reduce_scatter | solution.py:220
  369.3 129.9 %copy-start.9 = (bf16[512,1024]{1,0:T(8,128)(2,1)S(1)}, bf16[512,1024]{1,0:T(8,128)(2,1)}, u32[]{:S(2)}) copy-start(bf16[512,1024]{1,0:T(8,128)(2,1)} %param.27) | copy-start | bytes 3145732
  506.8 15.4 %slice-start = ((s8[16777216]{0:T(1024)(128)(4,1)}), s8[4194304]{0:T(1024)(128)(4,1)S(1)}, s32[]{:S(2)}) async-start(s8[16777216]{0:T(1024)(128)(4,1)} %bitcast.155), calls=%async_computation.20 | async-start | bytes 8388608
  507.1 15.2 %slice-start.1 = ((s8[16777216]{0:T(1024)(128)(4,1)}), s8[4194304]{0:T(1024)(128)(4,1)S(1)}, s32[]{:S(2)}) async-start(s8[16777216]{0:T(1024)(128)(4,1)} %bitcast.155), calls=%async_computation.21 | async-start | bytes 8388608
  507.1 15.2 %slice-start.2 = ((s8[16777216]{0:T(1024)(128)(4,1)}), s8[4194304]{0:T(1024)(128)(4,1)S(1)}, s32[]{:S(2)}) async-start(s8[16777216]{0:T(1024)(128)(4,1)} %bitcast.155), calls=%async_computation.22 | async-start | bytes 8388608
  507.1 16.0 %slice-start.3 = ((s8[16777216]{0:T(1024)(128)(4,1)}), s8[4194304]{0:T(1024)(128)(4,1)S(1)}, s32[]{:S(2)}) async-start(s8[16777216]{0:T(1024)(128)(4,1)} %bitcast.155), calls=%async_computation.23 | async-start | bytes 8388608
  523.1 11.6 %copy-start.23 = (bf16[512,8,32]{0,2,1:T(8,128)(2,1)S(1)}, bf16[512,8,32]{0,2,1:T(8,128)(2,1)}, u32[]{:S(2)}) copy-start(bf16[512,8,32]{0,2,1:T(8,128)(2,1)} %copy-done.22) | copy-start | bytes 786436
  523.1 11.6 %copy-start.25 = (bf16[512,8,32]{0,2,1:T(8,128)(2,1)S(1)}, bf16[512,8,32]{0,2,1:T(8,128)(2,1)}, u32[]{:S(2)}) copy-start(bf16[512,8,32]{0,2,1:T(8,128)(2,1)} %copy-done.24) | copy-start | bytes 786436
  575.2 194.0 %reduce-scatter.18.cloned.1.call-start = ((), (), s32[]{:S(2)}) async-start(), calls=%async_computation.14 | async-start | bytes 2621440 | tf_op jit(solution)/shard_map/reduce_scatter | solution.py:164
  590.5 224.5 %reduce-scatter.16.cloned.1.call-start = ((), (), s32[]{:S(2)}) async-start(), calls=%async_computation.13 | async-start | bytes 2621440 | tf_op jit(solution)/shard_map/reduce_scatter | solution.py:163
  605.4 254.6 %reduce-scatter.20.cloned.1.call-start = ((), (), s32[]{:S(2)}) async-start(), calls=%async_computation.15 | async-start | bytes 2621440 | tf_op jit(solution)/shard_map/reduce_scatter | solution.py:165
  620.5 312.0 %all-gather.15.cloned.1.call-start = ((), (), s32[]{:S(2)}) async-start(), calls=%async_computation.12 | async-start | bytes 6758400 | tf_op jit(solution)/shard_map/all_gather | solution.py:221
  724.6 137.6 %copy-start.39 = (f32[512]{0:T(512)S(1)}, f32[512]{0:T(512)}, u32[]{:S(2)}) copy-start(f32[512]{0:T(512)} %get-tuple-element.95) | copy-start | bytes 6148
  (27 other events, 60.4 us)
Sparse Core Ops, SparseCore 0:
  9.6 48.9 all-gather.18
  61.0 52.4 all-gather.10
  115.1 45.6 all-gather.20
  162.5 53.0 all-gather.12
  217.0 46.2 all-gather.16
  317.4 31.8 reduce-scatter.11
  352.7 71.4 reduce-scatter.13
  427.7 71.4 reduce-scatter.9
  575.3 149.1 reduce-scatter.21
  727.3 41.9 reduce-scatter.17
  772.1 42.8 reduce-scatter.15
  817.1 42.8 reduce-scatter.19
  862.9 69.4 all-gather.14

commit v3 on v2

--- a/solution.py
+++ b/solution.py
@@ -1,6 +1,10 @@
+import functools
+
 import jax
 import jax.numpy as jnp
 from jax import lax
+from jax.experimental import pallas as pl
+from jax.experimental.pallas import tpu as pltpu
 from jax.sharding import Mesh
 from jax.sharding import PartitionSpec as P
 
@@ -49,6 +53,468 @@
         "qngd,knd->ngqk", grouped, key_rows, preferred_element_type=jnp.float32
     ) * head_dim ** (-0.5)
     return jnp.where(allowed, scores, -1e30)
+
+
+def dot_nn(left, right):
+    return lax.dot_general(left, right, (((1,), (0,)), ((), ())), preferred_element_type=jnp.float32)
+
+
+def dot_nt(left, right):
+    return lax.dot_general(left, right, (((1,), (1,)), ((), ())), preferred_element_type=jnp.float32)
+
+
+def dot_tn(left, right):
+    return lax.dot_general(left, right, (((0,), (0,)), ((), ())), preferred_element_type=jnp.float32)
+
+
+def expert_kernel(
+    outer_count,
+    x_hbm,
+    gate_hbm,
+    grad_hbm,
+    pair_own,
+    down_own,
+    pair_next,
+    down_next,
+    dx_hbm,
+    y_hbm,
+    dots_ref,
+    first_hbm,
+    last_hbm,
+    rows,
+    gates,
+    act,
+    both,
+    wide,
+    down,
+    grads,
+    total,
+    stage_a,
+    stage_b,
+    ring,
+    core_in,
+    relay_in,
+    last_in,
+    dots,
+    dots_in,
+    local_sem,
+    grad_sem,
+    y_sem,
+    gather_send,
+    gather_recv,
+    weight_send,
+    weight_recv,
+    ring_send,
+    ring_recv,
+    dots_send,
+    dots_recv,
+    back_send,
+    back_recv,
+):
+    f32 = jnp.float32
+    bf16 = jnp.bfloat16
+    length, part = rows.shape[1], down.shape[1]
+    half = length // 2
+    outer, inner, narrow = lax.axis_index("outer"), lax.axis_index("inner"), lax.axis_index("narrow")
+    side, core = inner // 2, inner % 2
+    core_at = {"inner": side * 2 + (1 - core)}
+    x_at = {"narrow": 1 - narrow}
+    y_at = {"inner": (1 - side) * 2 + core}
+    next_at = {"outer": lax.rem(outer + 1, outer_count)}
+    before_at = {"outer": lax.rem(outer + outer_count - 1, outer_count)}
+
+    def device_of(slot):
+        there = slot // 2
+        return {
+            "inner": ((side + there // 2) % 2) * 2 + (core + slot % 2) % 2,
+            "narrow": (narrow + there % 2) % 2,
+        }
+
+    def place_of(slot):
+        there = slot // 2
+        at_inner = ((side + there // 2) % 2) * 2 + (core + slot % 2) % 2
+        return at_inner * 2 + (narrow + there % 2) % 2
+
+    def remote(source, target, sends, recvs, index, device):
+        return pltpu.make_async_remote_copy(
+            src_ref=source,
+            dst_ref=target,
+            send_sem=sends.at[index],
+            recv_sem=recvs.at[index],
+            device_id=device,
+            device_id_type=pl.DeviceIdType.MESH,
+        )
+
+    def local(source, target, index):
+        return pltpu.make_async_copy(source, target, local_sem.at[index])
+
+    low, high = pl.ds(0, half), pl.ds(half, half)
+    dx_ref = total.at[pl.ds(0, length)]
+
+    def gather(index):
+        source, target, device = (
+            (rows.at[0], rows.at[1], core_at),
+            (rows.at[0], rows.at[2], x_at),
+            (rows.at[0], rows.at[4], y_at),
+            (rows.at[2, low], rows.at[6, low], y_at),
+            (rows.at[4, high], rows.at[6, high], x_at),
+            (rows.at[2], rows.at[3], core_at),
+            (rows.at[4], rows.at[5], core_at),
+            (rows.at[6], rows.at[7], core_at),
+            (gates.at[0], gates.at[1], core_at),
+            (gates.at[0], gates.at[2], x_at),
+            (gates.at[0], gates.at[4], y_at),
+            (gates.at[0], gates.at[6], device_of(6)),
+            (gates.at[2], gates.at[3], core_at),
+            (gates.at[4], gates.at[5], core_at),
+            (gates.at[6], gates.at[7], core_at),
+        )[index]
+        return remote(source, target, gather_send, gather_recv, index, device)
+
+    def wide_at(slot):
+        return wide.at[:, pl.ds(slot * 2 * part, 2 * part)]
+
+    def weight(index):
+        slot = 1 + index // 2
+        if index % 2 == 0:
+            return remote(
+                wide_at(slot), wide_at(slot + 1), weight_send, weight_recv, index, next_at
+            )
+        return remote(
+            down.at[slot], down.at[slot + 1], weight_send, weight_recv, index, next_at
+        )
+
+    def ring_copy(index):
+        source = (stage_a, stage_b)[index]
+        return remote(source, ring.at[index], ring_send, ring_recv, index, next_at)
+
+    def dots_copy(slot):
+        return remote(
+            dots.at[slot], dots_in.at[slot], dots_send, dots_recv, slot, device_of(slot)
+        )
+
+    def back(index):
+        source, target, device = (
+            (rows.at[1], core_in.at[0], core_at),
+            (rows.at[3], core_in.at[1], core_at),
+            (rows.at[5], core_in.at[2], core_at),
+            (rows.at[7], core_in.at[3], core_at),
+            (rows.at[6, low], relay_in.at[0], x_at),
+            (rows.at[6, high], relay_in.at[1], y_at),
+            (rows.at[2], last_in.at[0], x_at),
+            (rows.at[4], last_in.at[1], y_at),
+        )[index]
+        return remote(source, target, back_send, back_recv, index, device)
+
+    own_copies = (
+        local(x_hbm, rows.at[0], 0),
+        local(gate_hbm, gates.at[0], 1),
+        local(pair_next, wide_at(1), 2),
+        local(down_next, down.at[1], 3),
+        local(pair_own, wide_at(0), 4),
+        local(down_own, down.at[0], 5),
+    )
+    for copy in own_copies:
+        copy.start()
+
+    def fetch(step):
+        order = step % 8
+        slot = jnp.where(order == 3, 4, jnp.where(order == 4, 3, order))
+        return pltpu.make_async_copy(
+            grad_hbm.at[place_of(slot)], grads.at[step % 2], grad_sem.at[step % 2]
+        )
+
+    fetch(0).start()
+    barrier = pltpu.get_barrier_semaphore()
+    for slot in range(1, 8):
+        pl.semaphore_signal(
+            barrier, inc=1, device_id=device_of(slot), device_id_type=pl.DeviceIdType.MESH
+        )
+    for device in (next_at, before_at):
+        pl.semaphore_signal(
+            barrier, inc=1, device_id=device, device_id_type=pl.DeviceIdType.MESH
+        )
+    pl.semaphore_wait(barrier, 9)
+    own_copies[0].wait()
+    own_copies[1].wait()
+    for index in (1, 2, 9, 10, 11, 0, 8):
+        gather(index).start()
+    for copy in own_copies[2:]:
+        copy.wait()
+    weight(0).start()
+    weight(1).start()
+
+    def first_step(step, carry):
+        turn, order = step // 8, step % 8
+        slot = jnp.where(order == 3, 4, jnp.where(order == 4, 3, order))
+        block = jnp.where(turn == 0, 1, jnp.where(turn == 1, 2, jnp.where(turn == 2, 0, 3)))
+
+        @pl.when(step + 1 < 8 * outer_count)
+        def _():
+            fetch(step + 1).start()
+
+        @pl.when(step == 1)
+        def _():
+            gather(0).wait_recv()
+            gather(8).wait_recv()
+
+        @pl.when(step == 2)
+        def _():
+            gather(1).wait_recv()
+            gather(3).start()
+            gather(5).start()
+            gather(2).wait_recv()
+            gather(4).start()
+            gather(6).start()
+            gather(9).wait_recv()
+            gather(12).start()
+            gather(10).wait_recv()
+            gather(13).start()
+
+        @pl.when(step == 4)
+        def _():
+            gather(5).wait_recv()
+            gather(12).wait_recv()
+
+        @pl.when(step == 5)
+        def _():
+            gather(6).wait_recv()
+            gather(13).wait_recv()
+
+        @pl.when(step == 6)
+        def _():
+            gather(3).wait_recv()
+            gather(4).wait_recv()
+            gather(7).start()
+            gather(11).wait_recv()
+            gather(14).start()
+
+        @pl.when(step == 7)
+        def _():
+            gather(7).wait_recv()
+            gather(14).wait_recv()
+
+        @pl.when(step == 8)
+        def _():
+            weight(0).wait_recv()
+            weight(1).wait_recv()
+            weight(2).start()
+            weight(3).start()
+
+        @pl.when(step == 24)
+        def _():
+            weight(2).wait_recv()
+            weight(3).wait_recv()
+
+        fetch(step).wait()
+        here = rows[slot]
+        grad_rows = grads[step % 2]
+        products = dot_nn(here, wide[:, pl.ds(block * 2 * part, 2 * part)])
+        gate_act, up_act = products[:, :part], products[:, part:]
+        raw = dot_nt(grad_rows, down[block])
+        expert = lax.rem(outer + outer_count - block, outer_count) * INNER + inner
+        count = gates.shape[1] // 3
+        place = lax.broadcasted_iota(jnp.int32, (gates.shape[1], part), 0) % count
+        chosen = jnp.where(place == expert, 1.0, 0.0).astype(bf16)
+        weights = dot_tn(gates[slot], chosen)
+        sigmoid = 1.0 / (1.0 + jnp.exp(-gate_act))
+        silu = gate_act * sigmoid
+        plain = silu * up_act
+        act[slot, :, pl.ds(block * part, part)] = (weights * plain).astype(bf16)
+        products = (plain * raw).astype(bf16)
+        dots[slot, pl.ds(block, 1), :] = dot_nt(jnp.ones((8, part), bf16), products)[:1]
+        hidden = weights * raw
+        both[slot, :, pl.ds(block * 2 * part, part)] = (
+            hidden * up_act * sigmoid * (1.0 + gate_act * (1.0 - sigmoid))
+        ).astype(bf16)
+        both[slot, :, pl.ds(block * 2 * part + part, part)] = (hidden * silu).astype(bf16)
+        pair_grad = dot_tn(both[slot, :, pl.ds(block * 2 * part, 2 * part)], here)
+        down_grad = dot_tn(act[slot, :, pl.ds(block * part, part)], grad_rows)
+
+        @pl.when(order == 0)
+        def _():
+            total[: 2 * part] = pair_grad
+            total[2 * part :] = down_grad
+
+        @pl.when(order > 0)
+        def _():
+            total[: 2 * part] += pair_grad
+            total[2 * part :] += down_grad
+
+        @pl.when(step == 7)
+        def _():
+            stage_a[...] = total[...].astype(bf16)
+            ring_copy(0).start()
+
+        @pl.when(step == 15)
+        def _():
+            stage_b[...] = total[...].astype(bf16)
+
+        @pl.when(step == 23)
+        def _():
+            ring_copy(0).wait()
+            stage_b[...] = (stage_b[...].astype(f32) + ring[0].astype(f32)).astype(bf16)
+            ring_copy(1).start()
+            stage_a[...] = total[...].astype(bf16)
+            local(stage_a, first_hbm, 0).start()
+
+        @pl.when(step == 31)
+        def _():
+            local(stage_a, first_hbm, 0).wait()
+            stage_a[...] = total[...].astype(bf16)
+
+        return carry
+
+    lax.fori_loop(0, 8 * outer_count, first_step, 0)
+    for slot in range(1, 8):
+        dots_copy(slot).start()
+    for index in range(15):
+        gather(index).wait_send()
+
+    def second_step(order, carry):
+        turn = order // 2
+        there = jnp.where(turn == 0, 3, jnp.where(turn == 3, 0, turn))
+        slot = there * 2 + 1 - order % 2
+        dx_ref[...] = dot_nt(both[slot], wide[...])
+
+        @pl.when(order % 2 == 0)
+        def _():
+            rows[slot] = dx_ref[...].astype(bf16)
+
+        for index in range(4):
+
+            @pl.when((order % 2 == 0) & (there == index))
+            def _():
+                back(index).start()
+
+        @pl.when(order == 1)
+        def _():
+            back(3).wait_recv()
+            rows[6] = (dx_ref[...] + core_in[3].astype(f32)).astype(bf16)
+            back(4).start()
+            back(5).start()
+
+        @pl.when(order == 3)
+        def _():
+            back(1).wait_recv()
+            back(5).wait_recv()
+            rows[2, :half] = (dx_ref[:half] + core_in[1, :half].astype(f32)).astype(bf16)
+            rows[2, half:] = (
+                dx_ref[half:] + core_in[1, half:].astype(f32) + relay_in[1].astype(f32)
+            ).astype(bf16)
+            back(6).start()
+
+        @pl.when(order == 5)
+        def _():
+            back(2).wait_recv()
+            back(4).wait_recv()
+            rows[4, :half] = (
+                dx_ref[:half] + core_in[2, :half].astype(f32) + relay_in[0].astype(f32)
+            ).astype(bf16)
+            rows[4, half:] = (dx_ref[half:] + core_in[2, half:].astype(f32)).astype(bf16)
+            back(7).start()
+
+        return carry
+
+    lax.fori_loop(0, 8, second_step, 0)
+
+    def third_step(slot, carry):
+        act[slot] = dot_nn(act[slot], down[...].reshape(outer_count * part, -1)).astype(bf16)
+        pltpu.make_async_copy(act.at[slot], y_hbm.at[place_of(slot)], y_sem.at[slot]).start()
+        return carry
+
+    lax.fori_loop(0, 8, third_step, 0)
+    ring_copy(1).wait()
+    stage_a[...] = (stage_a[...].astype(f32) + ring[1].astype(f32)).astype(bf16)
+    local(stage_a, last_hbm, 0).start()
+    back(0).wait_recv()
+    back(6).wait_recv()
+    back(7).wait_recv()
+    dx_ref[...] = (
+        dx_ref[...]
+        + core_in[0].astype(f32)
+        + (last_in[0].astype(f32) + last_in[1].astype(f32))
+    )
+    local(dx_ref, dx_hbm, 1).start()
+    dots_ref[0] = dots[0]
+    for slot in range(1, 8):
+        dots_copy(slot).wait()
+        dots_ref[slot] = dots_in[slot]
+    for index in range(8):
+        back(index).wait_send()
+    for index in range(4):
+        weight(index).wait_send()
+    for slot in range(8):
+        pltpu.make_async_copy(act.at[slot], y_hbm.at[place_of(slot)], y_sem.at[slot]).wait()
+    local(stage_a, last_hbm, 0).wait()
+    local(dx_ref, dx_hbm, 1).wait()
+
+
+def expert_layer(rows_own, gate_table, rows_grad, pair_own, down_own, outer_count):
+    f32 = jnp.float32
+    bf16 = jnp.bfloat16
+    length, width = rows_own.shape
+    part = down_own.shape[0]
+    ahead = [(place, (place + 1) % outer_count) for place in range(outer_count)]
+    pair_next = lax.ppermute(pair_own, "outer", ahead)
+    down_next = lax.ppermute(down_own, "outer", ahead)
+    anywhere = pl.BlockSpec(memory_space=pl.ANY)
+    inside = pl.BlockSpec(memory_space=pltpu.VMEM)
+    vmem, dma = pltpu.VMEM, pltpu.SemaphoreType.DMA
+    hidden = outer_count * part
+    share = jax.ShapeDtypeStruct((3 * part, width), bf16)
+    dx, y_rows, dots, first, last = pl.pallas_call(
+        functools.partial(expert_kernel, outer_count),
+        out_shape=(
+            jax.ShapeDtypeStruct((length, width), f32),
+            jax.ShapeDtypeStruct((8, length, width), bf16),
+            jax.ShapeDtypeStruct((8, 8, length), f32),
+            share,
+            share,
+        ),
+        in_specs=[anywhere] * 7,
+        out_specs=(anywhere, anywhere, inside, anywhere, anywhere),
+        scratch_shapes=[
+            vmem((8, length, width), bf16),
+            vmem((8,) + gate_table.shape, bf16),
+            vmem((8, length, hidden), bf16),
+            vmem((8, length, 2 * hidden), bf16),
+            vmem((width, 2 * hidden), bf16),
+            vmem((outer_count, part, width), bf16),
+            vmem((2, length, width), bf16),
+            vmem((3 * part, width), f32),
+            vmem((3 * part, width), bf16),
+            vmem((3 * part, width), bf16),
+            vmem((2, 3 * part, width), bf16),
+            vmem((4, length, width), bf16),
+            vmem((2, length // 2, width), bf16),
+            vmem((2, length, width), bf16),
+            vmem((8, 8, length), f32),
+            vmem((8, 8, length), f32),
+            dma((6,)),
+            dma((2,)),
+            dma((8,)),
+            dma((15,)),
+            dma((15,)),
+            dma((4,)),
+            dma((4,)),
+            dma((2,)),
+            dma((2,)),
+            dma((8,)),
+            dma((8,)),
+            dma((8,)),
+            dma((8,)),
+        ],
+        compiler_params=pltpu.CompilerParams(
+            collective_id=0, has_side_effects=True, vmem_limit_bytes=67043328
+        ),
+        cost_estimate=pl.CostEstimate(
+            flops=18 * 8 * length * width * hidden, bytes_accessed=1 << 26, transcendentals=0
+        ),
+        name="expert_layer",
+    )(rows_own, gate_table, rows_grad.reshape(8, length, width), pair_own, down_own, pair_next, down_next)
+    last = lax.ppermute(last, "outer", ahead)
+    return dx, y_rows.reshape(8 * length, width), dots, first, last
 
 
 def on_device(
@@ -77,9 +543,7 @@
     experts = router.shape[1]
     outer_count = experts // INNER
     here = ("inner", "narrow")
-    full_gate = lax.all_gather(w_gate[0], "outer", axis=1, tiled=True)
-    full_up = lax.all_gather(w_up[0], "outer", axis=1, tiled=True)
-    full_down = lax.all_gather(w_down[0], "outer", axis=0, tiled=True)
+    fused = outer_count == 4 and lax.axis_size("narrow") == 2
     rows_grad = lax.all_gather(grad_out, here, axis=0, tiled=True)
     part = w_gate.shape[2]
     inputs = hidden_in.astype(f32)
@@ -117,58 +581,79 @@
     masked = jnp.where(member, logits, -jnp.inf)
     powers = jnp.where(member, jnp.exp(masked - jnp.max(masked, axis=-1, keepdims=True)), 0.0)
     gate_probs = powers / jnp.sum(powers, axis=-1, keepdims=True)
-    gate_table = lax.all_gather(gate_probs.T, here, axis=0, tiled=False)
-    gate_table = gate_table.reshape(-1, outer_count, INNER, length)
-    mine = lax.dynamic_index_in_dim(gate_table, lax.axis_index("inner"), 2, keepdims=False)
-    row_gates = mine.transpose(0, 2, 1).reshape(-1, outer_count)
-    gate_wide = jnp.repeat(row_gates, part, axis=1)
-    rows_in = lax.all_gather(ffn_normed, here, axis=0, tiled=True)
-    gate_act = jnp.dot(rows_in, full_gate, preferred_element_type=f32)
-    up_act = jnp.dot(rows_in, full_up, preferred_element_type=f32)
-    raw_grad = jnp.einsum("rd,fd->rf", rows_grad, full_down, preferred_element_type=f32)
-    sigmoid_gate = jax.nn.sigmoid(gate_act)
-    plain_act = gate_act * sigmoid_gate * up_act
-    hidden_act = (gate_wide * plain_act).astype(bf16)
-    hidden_grad = gate_wide * raw_grad
-    moe_rows = lax.psum_scatter(
-        jnp.dot(hidden_act, full_down, preferred_element_type=f32).astype(bf16),
-        here,
-        scatter_dimension=0,
-        tiled=True,
-    )
-    hidden_out = (mixed_rows + moe_rows.astype(f32)).astype(bf16)
+    if fused:
+        table = gate_probs.T
+        part_one = lax.reduce_precision(table, 8, 7)
+        part_two = lax.reduce_precision(table - part_one, 8, 7)
+        part_three = table - part_one - part_two
+        table = jnp.concatenate([part_one, part_two, part_three], axis=0).astype(bf16)
+        pair_own = jnp.concatenate([w_gate[0], w_up[0]], axis=1)
+        rows_back, y_rows, dots, weight_first, weight_last = expert_layer(
+            ffn_normed, table, rows_grad, pair_own, w_down[0], outer_count
+        )
+        moe_rows = lax.psum_scatter(y_rows, here, scatter_dimension=0, tiled=True)
+        dots = dots[:, :outer_count].reshape(2, 2, 2, outer_count, length).sum(axis=1)
+        each = jnp.arange(experts, dtype=jnp.int32)
+        outer, inner = lax.axis_index("outer"), lax.axis_index("inner")
+        side = (each % INNER // 2 + inner // 2) % 2
+        core = (each + inner) % 2
+        block = (outer + outer_count - each // INNER) % outer_count
+        gate_grads = dots.reshape(experts, length)[(side * 2 + core) * outer_count + block].T
+    else:
+        full_gate = lax.all_gather(w_gate[0], "outer", axis=1, tiled=True)
+        full_up = lax.all_gather(w_up[0], "outer", axis=1, tiled=True)
+        full_down = lax.all_gather(w_down[0], "outer", axis=0, tiled=True)
+        gate_table = lax.all_gather(gate_probs.T, here, axis=0, tiled=False)
+        gate_table = gate_table.reshape(-1, outer_count, INNER, length)
+        mine = lax.dynamic_index_in_dim(gate_table, lax.axis_index("inner"), 2, keepdims=False)
+        row_gates = mine.transpose(0, 2, 1).reshape(-1, outer_count)
+        gate_wide = jnp.repeat(row_gates, part, axis=1)
+        rows_in = lax.all_gather(ffn_normed, here, axis=0, tiled=True)
+        gate_act = jnp.dot(rows_in, full_gate, preferred_element_type=f32)
+        up_act = jnp.dot(rows_in, full_up, preferred_element_type=f32)
+        raw_grad = jnp.einsum("rd,fd->rf", rows_grad, full_down, preferred_element_type=f32)
+        sigmoid_gate = jax.nn.sigmoid(gate_act)
+        plain_act = gate_act * sigmoid_gate * up_act
+        hidden_act = (gate_wide * plain_act).astype(bf16)
+        hidden_grad = gate_wide * raw_grad
+        moe_rows = lax.psum_scatter(
+            jnp.dot(hidden_act, full_down, preferred_element_type=f32).astype(bf16),
+            here,
+            scatter_dimension=0,
+            tiled=True,
+        )
+        gate_dots = jnp.sum((plain_act * raw_grad).reshape(-1, outer_count, part), axis=-1)
+        lane = jnp.arange(INNER) == lax.axis_index("inner")
+        gate_dots = jnp.where(lane[None, None, :], gate_dots[:, :, None], 0.0).reshape(-1, experts)
+        gate_grads = lax.psum_scatter(gate_dots, here, scatter_dimension=0, tiled=True)
+        gate_grad = (
+            hidden_grad * up_act * sigmoid_gate * (1.0 + gate_act * (1.0 - sigmoid_gate))
+        ).astype(bf16)
+        up_grad = (hidden_grad * gate_act * sigmoid_gate).astype(bf16)
+        copy_grads = (
+            jnp.einsum("rf,df->rd", gate_grad, full_gate, preferred_element_type=f32)
+            + jnp.einsum("rf,df->rd", up_grad, full_up, preferred_element_type=f32)
+        ).astype(bf16)
+        rows_back = lax.psum_scatter(copy_grads, here, scatter_dimension=0, tiled=True)
+        down_w_grad = jnp.einsum("rf,rd->fd", hidden_act, rows_grad, preferred_element_type=f32)
+        gate_w_grad = jnp.einsum("rd,rf->df", rows_in, gate_grad, preferred_element_type=f32)
+        up_w_grad = jnp.einsum("rd,rf->df", rows_in, up_grad, preferred_element_type=f32)
+        gate_w_grad, up_w_grad, down_w_grad = (
+            lax.psum_scatter(gate_w_grad.astype(bf16), "outer", scatter_dimension=1, tiled=True),
+            lax.psum_scatter(up_w_grad.astype(bf16), "outer", scatter_dimension=1, tiled=True),
+            lax.psum_scatter(down_w_grad.astype(bf16), "outer", scatter_dimension=0, tiled=True),
+        )
+        gate_w_grad, up_w_grad, down_w_grad = (
+            gate_w_grad[None].astype(f32),
+            up_w_grad[None].astype(f32),
+            down_w_grad[None].astype(f32),
+        )
     cotangent = grad_out.astype(f32)
-    gate_dots = jnp.sum((plain_act * raw_grad).reshape(-1, outer_count, part), axis=-1)
-    lane = jnp.arange(INNER) == lax.axis_index("inner")
-    gate_dots = jnp.where(lane[None, None, :], gate_dots[:, :, None], 0.0).reshape(-1, experts)
-    gate_grads = lax.psum_scatter(gate_dots, here, scatter_dimension=0, tiled=True)
     logit_grads = (
         gate_probs * (gate_grads - jnp.sum(gate_probs * gate_grads, axis=-1, keepdims=True))
     ).astype(bf16)
     router_grad = jnp.einsum("sd,se->de", ffn_normed, logit_grads, preferred_element_type=f32)
     normed_two_grad = jnp.einsum("se,de->sd", logit_grads, router, preferred_element_type=f32)
-    gate_grad = (
-        hidden_grad * up_act * sigmoid_gate * (1.0 + gate_act * (1.0 - sigmoid_gate))
-    ).astype(bf16)
-    up_grad = (hidden_grad * gate_act * sigmoid_gate).astype(bf16)
-    copy_grads = (
-        jnp.einsum("rf,df->rd", gate_grad, full_gate, preferred_element_type=f32)
-        + jnp.einsum("rf,df->rd", up_grad, full_up, preferred_element_type=f32)
-    ).astype(bf16)
-    rows_back = lax.psum_scatter(copy_grads, here, scatter_dimension=0, tiled=True)
-    down_w_grad = jnp.einsum("rf,rd->fd", hidden_act, rows_grad, preferred_element_type=f32)
-    gate_w_grad = jnp.einsum("rd,rf->df", rows_in, gate_grad, preferred_element_type=f32)
-    up_w_grad = jnp.einsum("rd,rf->df", rows_in, up_grad, preferred_element_type=f32)
-    gate_w_grad, up_w_grad, down_w_grad = (
-        lax.psum_scatter(gate_w_grad.astype(bf16), "outer", scatter_dimension=1, tiled=True),
-        lax.psum_scatter(up_w_grad.astype(bf16), "outer", scatter_dimension=1, tiled=True),
-        lax.psum_scatter(down_w_grad.astype(bf16), "outer", scatter_dimension=0, tiled=True),
-    )
-    gate_w_grad, up_w_grad, down_w_grad = (
-        gate_w_grad[None].astype(f32),
-        up_w_grad[None].astype(f32),
-        down_w_grad[None].astype(f32),
-    )
     normed_two_grad = normed_two_grad + rows_back.astype(f32)
     mixed_part, ffn_gain_grad = norm_back(mixed_rows, scale_two, ffn_gain, normed_two_grad)
     mixed_grad = cotangent + mixed_part
@@ -216,8 +701,18 @@
     small = jnp.pad(small, ((0, 0), (0, 128 - small.shape[1])))
     columns = jnp.concatenate(
         [query_w_grad, key_w_grad, value_w_grad, out_w_grad, small], axis=1
-    )
-    shares = lax.psum_scatter(columns.astype(bf16), everywhere, scatter_dimension=0, tiled=True)
+    ).astype(bf16)
+    mixed_late, columns = lax.optimization_barrier((mixed_rows, columns))
+    hidden_out = (mixed_late + moe_rows.astype(f32)).astype(bf16)
+    if fused:
+        columns, hidden_out, weight_last = lax.optimization_barrier(
+            (columns, hidden_out, weight_last)
+        )
+        weight_sum = weight_first.astype(f32) + weight_last.astype(f32)
+        gate_w_grad = weight_sum[:part].T[None]
+        up_w_grad = weight_sum[part : 2 * part].T[None]
+        down_w_grad = weight_sum[2 * part :][None]
+    shares = lax.psum_scatter(columns, everywhere, scatter_dimension=0, tiled=True)
     columns = lax.all_gather(shares, everywhere, axis=0, tiled=True).astype(f32)
     starts = [0]
     for width in (w_query.shape[1], w_key.shape[1], w_value.shape[1], model_width, experts, 1, 1):

time: 961 us -> 606 us (0.63)
  waiting for transfers between devices: 592 us -> 227 us
  Pallas kernels: 0 us -> 194 us
  matrix products: 232 us -> 78.9 us
  blocking collectives: 18.5 us -> 0 us
  other arithmetic: 61.9 us -> 43.6 us
    reduce_scatter x7 -> x2, waiting for transfers between devices: 361 us -> 149 us  [the longest x1 149 us: on_device(): lax.psum_scatter(columns, everywhere, scatter_dimension=0, tiled=True)]
    pallas_call x0 -> x1, Pallas kernels: none -> 194 us  [expert_layer(): pl.pallas_call(functools.partial(expert_kernel, outer_count), out_shape=(...]
    dot_general x9 -> x0, matrix products: 161 us -> none  [the longest x1 34.5 us: on_device(): gate_act = jnp.dot(rows_in, full_gate, preferred_element_type=f32)]
    all_gather x4 -> x0, waiting for transfers between devices: 107 us -> none  [the longest x1 44.6 us: on_device(): rows_in = lax.all_gather(ffn_normed, here, axis=0, tiled=True)]
    all_gather x1, waiting for transfers between devices: 54.8 us -> 15.2 us  [on_device(): rows_grad = lax.all_gather(grad_out, here, axis=0, tiled=True)]
    all_gather x1 -> x0, blocking collectives: 18.5 us -> none  [on_device(): gate_table = lax.all_gather(gate_probs.T, here, axis=0, tiled=False)]
    reduce_sum x1, other arithmetic: 16.8 us -> 0.02 us  [on_device(): dots[:, :outer_count].reshape(2, 2, 2, outer_count, length).sum(axis=1)]
    unnamed x95 -> x150, local copies, waits for them, and re-layouts: 19 us -> 22.6 us
  transfers between devices with their start and end apart: 13 -> 7, of which waited for: 11 -> 3; matrix products, arithmetic and copies ran while one was open for 19% -> 20% of each run, Pallas kernels for 0% -> 0%
where the time goes in v3:
time: 606 us; the launch traced here: 602 us
  waiting for transfers between devices  227 us (37%)
  Pallas kernels  194 us (32%)
  matrix products  78.9 us (13%)
  other arithmetic  43.6 us (7%)
  local copies, waits for them, and re-layouts  37.6 us (6%)
  between operations  15 us (2%)
    pallas_call x1, Pallas kernels, expert_layer(): pl.pallas_call(functools.partial(expert_kernel, outer_count), out_shape=(...  194 us
    reduce_scatter x1, waiting for transfers between devices, on_device(): lax.psum_scatter(columns, everywhere, scatter_dimension=0, tiled=True)  149 us
    all_gather x1, waiting for transfers between devices, on_device(): columns = lax.all_gather(shares, everywhere, axis=0, tiled=True).astype(f32)  62.1 us
    unnamed x150, local copies, waits for them, and re-layouts  22.6 us
    all_gather x1, waiting for transfers between devices, on_device(): rows_grad = lax.all_gather(grad_out, here, axis=0, tiled=True)  15.2 us
    dot_general x1, matrix products, on_device(): jnp.einsum('qngd,knd->ngqk', attended_grad, value_rows, preferred_element...  14.8 us
  transfers between devices with their start and end apart: 7, of which 3 were waited for; matrix products, arithmetic and copies ran while one was open for 20% of the time, Pallas kernels for 0%

profile of v3, /device:TPU:0, one launch (start us, length us, event | category | flops | bytes accessed | tf_op | source)
XLA Modules:
  0.0 601.6 jit_solution(10153964943004948197)
XLA Ops:
  8.0 3.1 collective-permute-start.1
  12.4 1.6 collective-permute-start
  19.5 7.8 %fusion.75 = (f32[8,2,512]{2,1,0:T(2,128)S(1)}, f32[8,2,512,512]{2,3,1,0:T(8,128)}) fusion(bf16[512,8,2,32]{0,3,2,1:T(8,128)(2,1)S(1)} %bitcast.152, bf16[512,8,2,32]{0,3,2,1:T(8,128)(2,1)S(1)} %bitcast.150, bf16[512,8,32]{0,2,1:T(8,128)(2,1)S(1)} %get-tuple-element.112, bf16[512,8,32]{0,2,1:T(8,128)(2,1)S(1)} %get-tuple-element.111, ...), kind=kOutput, calls=%fused_computation.150 | convolution fusion | flops 552591360 | bytes 18644992 | tf_op jit(solution)/shard_map/qngd,knd->ngqk/dot_general | solution.py:52
  27.4 8.3 %exponential_reduce_fusion = f32[8,2,512]{2,1,0:T(2,128)S(1)} fusion(f32[8,2,512,512]{2,3,1,0:T(8,128)} %get-tuple-element.124, f32[8,2,512]{2,1,0:T(2,128)S(1)} %get-tuple-element.123), kind=kLoop, calls=%fused_computation.8 | loop fusion | flops 8380416 | bytes 16842752 | tf_op jit(solution)/shard_map/reduce_sum | solution.py:569
  36.6 10.1 %fusion.20 = bf16[8,64,2,512]{3,1,2,0:T(8,128)(2,1)S(1)} fusion(bf16[512,8,64,1]{0,2,3,1:T(8,128)(2,1)S(1)} %bitcast.148, f32[8,2,512,512]{2,3,1,0:T(8,128)} %get-tuple-element.124, f32[8,2,512]{2,1,0:T(2,128)S(1)} %bitcast.162), kind=kOutput, calls=%fused_computation.44 | convolution fusion | flops 545783808 | bytes 18382848 | tf_op jit(solution)/shard_map/ngqk,knd->qngd/dot_general | solution.py:571
  51.7 15.2 %all-gather.3.cloned.1.call-done = bf16[4096,1024]{1,0:T(8,128)(2,1)} async-done(((bf16[512,1024]{1,0:T(8,128)(2,1)}), bf16[4096,1024]{1,0:T(8,128)(2,1)}) %all-gather.3.cloned.1.call-update) | async-done | bytes 8388624 | tf_op jit(solution)/shard_map/all_gather | solution.py:547
  66.9 194.4 %expert_layer.1 = (f32[512,1024]{1,0:T(8,128)}, bf16[8,512,1024]{2,1,0:T(8,128)(2,1)}, f32[8,8,512]{2,1,0:T(8,128)}, bf16[768,1024]{1,0:T(8,128)(2,1)}, bf16[768,1024]{1,0:T(8,128)(2,1)}) custom-call(bf16[512,1024]{1,0:T(8,128)(2,1)} %copy-done.5, bf16[48,512]{1,0:T(8,128)(2,1)} %pad_maximum_fusion.6.gate_hbm, bf16[8,512,1024]{2,1,0:T(8,128)(2,1)} %bitcast.172, ...), custom_call_target="tpu_custom_call" | custom-call | flops 77309411328 | bytes 67108864 | tf_op jit(solution)/shard_map/expert_layer/pallas_call | solution.py:466
  263.1 3.2 multiply_reduce_fusion
  269.0 2.3 convolution_convert_fusion
  271.3 2.6 copy.83
  273.9 14.8 %fusion = (f32[8,2,512]{2,1,0:T(2,128)}, f32[8,512,512,2]{2,1,3,0:T(8,128)}) fusion(f32[8,2,512,512]{2,3,1,0:T(8,128)} %get-tuple-element.124, f32[8,2,512]{2,1,0:T(2,128)} %bitcast.163, bf16[512,8,64,1]{0,2,3,1:T(8,128)(2,1)S(1)} %bitcast.149, bf16[512,8,2,64]{0,3,2,1:T(8,128)(2,1)} %bitcast.142), kind=kOutput, calls=%fused_computation.3 | convolution fusion | flops 549445632 | bytes 35192832 | tf_op jit(solution)/shard_map/qngd,knd->ngqk/dot_general | solution.py:671
  291.1 11.3 %fusion.2 = bf16[8,2,512,512]{2,3,1,0:T(8,128)(2,1)} fusion(f32[8,512,512,2]{2,1,3,0:T(8,128)} %get-tuple-element.131, f32[8,2,512,512]{2,3,1,0:T(8,128)S(1)} %bitcast.139, f32[8,2,512]{2,1,0:T(2,128)} %get-tuple-element.130, f32[8,2,512]{2,1,0:T(2,128)} %bitcast.164), kind=kLoop, calls=%fused_computation.5 | loop fusion | flops 16777216 | bytes 42008576 | tf_op jit(solution)/shard_map/convert_element_type | solution.py:674
  302.4 6.1 %fusion.27 = f32[512,8,64]{0,2,1:T(8,128)S(1)} fusion(bf16[8,2,512,512]{2,3,1,0:T(8,128)(2,1)} %fusion.2, bf16[512,8,2,32]{0,3,2,1:T(8,128)(2,1)S(1)} %bitcast.153, bf16[512,8,2,32]{0,3,2,1:T(8,128)(2,1)S(1)} %bitcast.151), kind=kOutput, calls=%fused_computation.48 | convolution fusion | flops 539230208 | bytes 10485760 | tf_op jit(solution)/shard_map/ngqk,qngd->knd/dot_general | solution.py:678
  309.6 5.1 convolution_multiply_fusion
  316.4 2.1 fusion.77
  318.5 2.6 fusion.76
  321.1 4.4 fusion.28
  325.6 6.2 %fusion.17 = (f32[512]{0:T(512)}, bf16[1024]{0:T(1024)(128)(2,1)S(1)}, f32[512,1024]{1,0:T(8,128)}) fusion(bf16[512,1024]{1,0:T(8,128)(2,1)} %param.14, f32[1024]{0:T(1024)} %param.17, f32[512]{0:T(512)S(1)} %copy-done.55, bf16[512,512]{0,1:T(8,128)(2,1)S(1)} %bitcast.154, bf16[1024,512]{1,0:T(8,128)(2,1)} %param.20, f32[512,1024]{1,0:T(8,128)} %fusion.76, ...), kind=kOutput, calls=%fused_computation.28 | convolution fusion | flops 541587968 | bytes 8923136 | tf_op jit(solution)/shard_map/sh,dh->sd/dot_general | solution.py:693
  331.8 2.8 convert_dynamic-update-slice_fusion.1
  334.8 1.8 fusion.19
  336.6 1.8 fusion.18
  338.6 2.7 convert_dynamic-update-slice_fusion
  342.1 2.6 add_convert_fusion
  344.7 9.6 %copy.100 = bf16[1024,3200]{1,0:T(8,128)(2,1)} copy(bf16[1024,3200]{0,1:T(8,128)(2,1)} %fusion.39) | data formatting | bytes 13107200
  354.4 149.1 %reduce-scatter.7.cloned.1.call-done = bf16[32,3200]{1,0:T(8,128)(2,1)} async-done(((bf16[1024,3200]{1,0:T(8,128)(2,1)}), bf16[32,3200]{1,0:T(8,128)(2,1)}) %reduce-scatter.7.cloned.1.call-update) | async-done | bytes 204816 | tf_op jit(solution)/shard_map/reduce_scatter | solution.py:715
  503.6 3.3 fusion.16
  506.9 2.0 convert_add_fusion.1
  512.7 62.1 %all-gather.5.cloned.1.call-done = bf16[1024,3200]{1,0:T(8,128)(2,1)} async-done(((bf16[32,3200]{1,0:T(8,128)(2,1)}), bf16[1024,3200]{1,0:T(8,128)(2,1)}) %all-gather.5.cloned.1.call-update) | async-done | bytes 6553616 | tf_op jit(solution)/shard_map/all_gather | solution.py:716
  576.6 8.6 %convert_element_type.103 = f32[1024,3200]{1,0:T(8,128)} convert(bf16[1024,3200]{1,0:T(8,128)(2,1)} %all-gather.5.cloned.1.call-done) | non-fusion elementwise | flops 3276800 | bytes 19660800 | tf_op jit(solution)/shard_map/convert_element_type | solution.py:716
  585.2 2.4 slice_reduce_fusion
  587.7 2.6 fusion.74
  590.3 4.5 fusion.73
  (205 shorter events, 29.4 us)
Async XLA Ops:
  7.2 6.9 %copy-start.2 = (bf16[512,1024]{1,0:T(8,128)(2,1)S(1)}, bf16[512,1024]{1,0:T(8,128)(2,1)}, u32[]{:S(2)}) copy-start(bf16[512,1024]{1,0:T(8,128)(2,1)} %param.14) | copy-start | bytes 3145732
  7.2 8.7 %copy-start.60 = (s32[1,512]{1,0:T(1,128)S(1)}, s32[1,512]{1,0:T(1,128)}, u32[]{:S(2)}) copy-start(s32[1,512]{1,0:T(1,128)} %param.15) | copy-start | bytes 6148
  7.2 8.9 %copy-start.57 = (f32[1024]{0:T(1024)S(1)}, f32[1024]{0:T(1024)}, u32[]{:S(2)}) copy-start(f32[1024]{0:T(1024)} %param.17) | copy-start | bytes 12292
  7.2 8.9 %copy-start.27 = (bf16[1024,512]{1,0:T(8,128)(2,1)S(1)}, bf16[1024,512]{1,0:T(8,128)(2,1)}, u32[]{:S(2)}) copy-start(bf16[1024,512]{1,0:T(8,128)(2,1)} %param.19) | copy-start | bytes 3145732
  7.2 59.7 %all-gather.3.cloned.1.call-start = ((), (), s32[]{:S(2)}) async-start(), calls=%async_computation.2 | async-start | bytes 9437184 | tf_op jit(solution)/shard_map/all_gather | solution.py:547
  8.0 334.2 %reduce-scatter.5.cloned.1.call-start = ((), (), s32[]{:S(2)}) async-start(), calls=%async_computation.3 | async-start | bytes 9437184 | tf_op jit(solution)/shard_map/reduce_scatter | solution.py:594
  8.0 42.7 %collective-permute-start.1 = (bf16[256,1024]{1,0:T(8,128)(2,1)}, bf16[256,1024]{1,0:T(8,128)(2,1)}, u32[]{:S(2)}, u32[]{:S(2)}) collective-permute-start(bf16[256,1024]{1,0:T(8,128)(2,1)} %bitcast.173), channel_id=1, source_target_pairs={{0,8},{8,16},{16,24},{24,0},{1,9},{9,17},{17,25},{25,1},{2,10},{10... | collective-permute-start | bytes 1572872 | tf_op jit(solution)/shard_map/ppermute | solution.py:460
  12.4 38.4 %collective-permute-start = (bf16[1024,512]{1,0:T(8,128)(2,1)S(1)}, bf16[1024,512]{1,0:T(8,128)(2,1)S(1)}, u32[]{:S(2)}, u32[]{:S(2)}) collective-permute-start(bf16[1024,512]{1,0:T(8,128)(2,1)S(1)} %pad_maximum_fusion.1.pair_own), channel_id=1, source_target_pairs={{0,8},{8,16},{16,24},{24,0},{1,9},{9,17},{17,25},{25,1},{2,10},{10... | collective-permute-start | bytes 3145736 | tf_op jit(solution)/shard_map/ppermute | solution.py:459
  14.9 20.8 %copy-start.54 = (f32[512]{0:T(512)}, f32[512]{0:T(512)S(1)}, u32[]{:S(2)}) copy-start(f32[512]{0:T(512)S(1)} %get-tuple-element.117) | copy-start | bytes 6148
  19.5 7.9 %copy-start.16 = (bf16[512,16,32]{0,2,1:T(8,128)(2,1)}, bf16[512,16,32]{0,2,1:T(8,128)(2,1)S(1)}, u32[]{:S(2)}) copy-start(bf16[512,16,32]{0,2,1:T(8,128)(2,1)S(1)} %get-tuple-element.107) | copy-start | bytes 1572868
  19.5 7.9 %copy-start.18 = (bf16[512,16,32]{0,2,1:T(8,128)(2,1)}, bf16[512,16,32]{0,2,1:T(8,128)(2,1)S(1)}, u32[]{:S(2)}) copy-start(bf16[512,16,32]{0,2,1:T(8,128)(2,1)S(1)} %get-tuple-element.108) | copy-start | bytes 1572868
  27.4 8.3 %copy-start.36 = (bf16[1024,512]{1,0:T(8,128)(2,1)S(1)}, bf16[1024,512]{1,0:T(8,128)(2,1)}, u32[]{:S(2)}) copy-start(bf16[1024,512]{1,0:T(8,128)(2,1)} %param.20) | copy-start | bytes 3145732
  35.7 11.0 %copy-start.39 = (f32[2,8,512]{2,1,0:T(8,128)}, f32[2,8,512]{2,1,0:T(8,128)S(1)}, u32[]{:S(2)}) copy-start(f32[2,8,512]{2,1,0:T(8,128)S(1)} %log_add_fusion) | copy-start | bytes 98308
  36.6 10.1 %copy-start.14 = (bf16[512,512]{0,1:T(8,128)(2,1)}, bf16[512,512]{0,1:T(8,128)(2,1)S(1)}, u32[]{:S(2)}) copy-start(bf16[512,512]{0,1:T(8,128)(2,1)S(1)} %convolution_convert_fusion.3) | copy-start | bytes 1572868
  36.6 10.1 %copy-start.22 = (bf16[1024,1024]{1,0:T(8,128)(2,1)S(1)}, bf16[1024,1024]{1,0:T(8,128)(2,1)}, u32[]{:S(2)}) copy-start(bf16[1024,1024]{1,0:T(8,128)(2,1)} %param.21) | copy-start | bytes 6291460
  261.4 242.1 %reduce-scatter.7.cloned.1.call-start = ((), (), s32[]{:S(2)}) async-start(), calls=%async_computation.5 | async-start | bytes 6758400 | tf_op jit(solution)/shard_map/reduce_scatter | solution.py:715
  262.3 82.4 %collective-permute-start.2 = (bf16[768,1024]{1,0:T(8,128)(2,1)}, bf16[768,1024]{1,0:T(8,128)(2,1)}, u32[]{:S(2)}, u32[]{:S(2)}) collective-permute-start(bf16[768,1024]{1,0:T(8,128)(2,1)} %get-tuple-element.27), channel_id=1, source_target_pairs={{0,8},{8,16},{16,24},{24,0},{1,9},{9,17},{17,25},{25,1},{2,10},{10... | collective-permute-start | bytes 4718600 | tf_op jit(solution)/shard_map/ppermute | solution.py:516
  273.9 14.8 %slice-start = ((s8[16777216]{0:T(1024)(128)(4,1)}), s8[4194304]{0:T(1024)(128)(4,1)S(1)}, s32[]{:S(2)}) async-start(s8[16777216]{0:T(1024)(128)(4,1)} %bitcast.138), calls=%async_computation.6 | async-start | bytes 8388608
  273.9 14.8 %slice-start.1 = ((s8[16777216]{0:T(1024)(128)(4,1)}), s8[4194304]{0:T(1024)(128)(4,1)S(1)}, s32[]{:S(2)}) async-start(s8[16777216]{0:T(1024)(128)(4,1)} %bitcast.138), calls=%async_computation.7 | async-start | bytes 8388608
  273.9 16.0 %slice-start.2 = ((s8[16777216]{0:T(1024)(128)(4,1)}), s8[4194304]{0:T(1024)(128)(4,1)S(1)}, s32[]{:S(2)}) async-start(s8[16777216]{0:T(1024)(128)(4,1)} %bitcast.138), calls=%async_computation.8 | async-start | bytes 8388608
  273.9 17.2 %slice-start.3 = ((s8[16777216]{0:T(1024)(128)(4,1)}), s8[4194304]{0:T(1024)(128)(4,1)S(1)}, s32[]{:S(2)}) async-start(s8[16777216]{0:T(1024)(128)(4,1)} %bitcast.138), calls=%async_computation.9 | async-start | bytes 8388608
  291.1 11.3 %copy-start.17 = (bf16[512,16,32]{0,2,1:T(8,128)(2,1)S(1)}, bf16[512,16,32]{0,2,1:T(8,128)(2,1)}, u32[]{:S(2)}) copy-start(bf16[512,16,32]{0,2,1:T(8,128)(2,1)} %copy-done.16) | copy-start | bytes 1572868
  291.1 11.3 %copy-start.19 = (bf16[512,16,32]{0,2,1:T(8,128)(2,1)S(1)}, bf16[512,16,32]{0,2,1:T(8,128)(2,1)}, u32[]{:S(2)}) copy-start(bf16[512,16,32]{0,2,1:T(8,128)(2,1)} %copy-done.18) | copy-start | bytes 1572868
  325.5 6.2 %copy-start.3 = (bf16[512,1024]{1,0:T(8,128)(2,1)S(1)}, bf16[512,1024]{1,0:T(8,128)(2,1)}, u32[]{:S(2)}) copy-start(bf16[512,1024]{1,0:T(8,128)(2,1)} %param.14) | copy-start | bytes 3145732
  354.3 149.3 %copy-start.63 = (f32[512]{0:T(512)S(1)}, f32[512]{0:T(512)}, u32[]{:S(2)}) copy-start(f32[512]{0:T(512)} %get-tuple-element.96) | copy-start | bytes 6148
  354.3 149.3 %copy-start.4 = (bf16[512,1024]{1,0:T(8,128)(2,1)S(1)}, bf16[512,1024]{1,0:T(8,128)(2,1)}, u32[]{:S(2)}) copy-start(bf16[512,1024]{1,0:T(8,128)(2,1)} %param.14) | copy-start | bytes 3145732
  354.3 149.3 %copy-start.9 = (f32[512,1024]{1,0:T(8,128)S(1)}, f32[512,1024]{1,0:T(8,128)}, u32[]{:S(2)}) copy-start(f32[512,1024]{1,0:T(8,128)} %copy-done.7) | copy-start | bytes 6291460
  354.3 149.3 %copy-start.59 = (f32[1024]{0:T(1024)S(1)}, f32[1024]{0:T(1024)}, u32[]{:S(2)}) copy-start(f32[1024]{0:T(1024)} %param.17) | copy-start | bytes 12292
  354.3 149.3 %copy-start.61 = (f32[512]{0:T(512)S(1)}, f32[512]{0:T(512)}, u32[]{:S(2)}) copy-start(f32[512]{0:T(512)} %get-tuple-element.116) | copy-start | bytes 6148
  354.3 220.5 %all-gather.5.cloned.1.call-start = ((), (), s32[]{:S(2)}) async-start(), calls=%async_computation.4 | async-start | bytes 6758400 | tf_op jit(solution)/shard_map/all_gather | solution.py:716
  575.8 11.9 %slice-start.4 = ((s8[6553600]{0:T(1024)(128)(4,1)}), s8[2359296]{0:T(1024)(128)(4,1)S(1)}, s32[]{:S(2)}) async-start(s8[6553600]{0:T(1024)(128)(4,1)} %bitcast.140), calls=%async_computation.10 | async-start | bytes 4718592
  576.6 11.1 %slice-start.5 = ((s8[6553600]{0:T(1024)(128)(4,1)}), s8[4194304]{0:T(1024)(128)(4,1)S(1)}, s32[]{:S(2)}) async-start(s8[6553600]{0:T(1024)(128)(4,1)} %bitcast.140), calls=%async_computation.11 | async-start | bytes 8388608
  (48 other events, 115.7 us)
Sparse Core Ops, SparseCore 0:
  9.9 56.9 all-gather.2
  261.5 68.7 reduce-scatter.4
  354.4 149.0 reduce-scatter.6
  506.3 68.5 all-gather.4

commit v4 on v3

--- a/solution.py
+++ b/solution.py
@@ -517,6 +517,218 @@
     return dx, y_rows.reshape(8 * length, width), dots, first, last
 
 
+def reduce_kernel(
+    outer_count,
+    normed_ref,
+    turned_ref,
+    attended_ref,
+    branch_ref,
+    small_ref,
+    out_one,
+    out_two,
+    out_three,
+    out_four,
+    work_one,
+    work_two,
+    work_three,
+    work_four,
+    core_one,
+    core_two,
+    core_three,
+    core_four,
+    near_one,
+    near_two,
+    near_three,
+    near_four,
+    far_one,
+    far_two,
+    far_three,
+    far_four,
+    deep_one,
+    deep_two,
+    deep_three,
+    deep_four,
+    sends,
+    recvs,
+    deep_sends,
+    deep_recvs,
+):
+    f32 = jnp.float32
+    bf16 = jnp.bfloat16
+    outer, inner, narrow = lax.axis_index("outer"), lax.axis_index("inner"), lax.axis_index("narrow")
+    side, core = inner // 2, inner % 2
+    core_at = {"inner": side * 2 + (1 - core)}
+    x_at = {"narrow": 1 - narrow}
+    y_at = {"inner": (1 - side) * 2 + core}
+    outs = (out_one, out_two, out_three, out_four)
+    works = (work_one, work_two, work_three, work_four)
+    cores = (core_one, core_two, core_three, core_four)
+    nears = (near_one, near_two, near_three, near_four)
+    fars = (far_one, far_two, far_three, far_four)
+    deeps = (deep_one, deep_two, deep_three, deep_four)
+    rows = work_one.shape[0]
+    halves, quarters, eighths = rows // 2, rows // 4, rows // 8
+    pieces = eighths // outer_count
+
+    def span(start, size):
+        return pl.ds(pl.multiple_of(start, pieces), size)
+
+    def remote(source, target, chunk, stage, device):
+        return pltpu.make_async_remote_copy(
+            src_ref=source,
+            dst_ref=target,
+            send_sem=sends.at[chunk * 8 + stage],
+            recv_sem=recvs.at[chunk * 8 + stage],
+            device_id=device,
+            device_id_type=pl.DeviceIdType.MESH,
+        )
+
+    def places(chunk):
+        first, second = (narrow, side) if chunk % 2 == 0 else (side, narrow)
+        devices = (x_at, y_at) if chunk % 2 == 0 else (y_at, x_at)
+        at_core = core * halves
+        at_near = at_core + first * quarters
+        at_far = at_near + second * eighths
+        return first, second, devices, at_core, at_near, at_far
+
+    def copies(chunk, stage):
+        first, second, devices, at_core, at_near, at_far = places(chunk)
+        work, out = works[chunk], outs[chunk]
+        if stage == 0:
+            source = work.at[span((1 - core) * halves, halves)]
+            return [remote(source, cores[chunk], chunk, 0, core_at)]
+        if stage == 1:
+            source = work.at[span(at_core + (1 - first) * quarters, quarters)]
+            return [remote(source, nears[chunk], chunk, 1, devices[0])]
+        if stage == 2:
+            source = work.at[span(at_near + (1 - second) * eighths, eighths)]
+            return [remote(source, fars[chunk], chunk, 2, devices[1])]
+        if stage in (3, 4):
+            found = []
+            for step in range(1, outer_count):
+                there = lax.rem(outer + step, outer_count)
+                index = (chunk * 2 + stage - 3) * (outer_count - 1) + step - 1
+                if stage == 3:
+                    source = work.at[span(at_far + there * pieces, pieces)]
+                    target = deeps[chunk].at[step - 1]
+                else:
+                    source = out.at[span(at_far + outer * pieces, pieces)]
+                    target = source
+                found.append(
+                    pltpu.make_async_remote_copy(
+                        src_ref=source,
+                        dst_ref=target,
+                        send_sem=deep_sends.at[index],
+                        recv_sem=deep_recvs.at[index],
+                        device_id={"outer": there},
+                        device_id_type=pl.DeviceIdType.MESH,
+                    )
+                )
+            return found
+        start, size, device = (
+            (at_far, eighths, devices[1]),
+            (at_near, quarters, devices[0]),
+            (at_core, halves, core_at),
+        )[stage - 5]
+        source = out.at[span(start, size)]
+        return [remote(source, source, chunk, stage, device)]
+
+    def arrive(chunk, stage):
+        first, second, devices, at_core, at_near, at_far = places(chunk)
+        work, out = works[chunk], outs[chunk]
+        for copy in copies(chunk, stage):
+            copy.wait_recv()
+        if stage < 3:
+            start, size, box = (
+                (at_core, halves, cores[chunk]),
+                (at_near, quarters, nears[chunk]),
+                (at_far, eighths, fars[chunk]),
+            )[stage]
+            held = work[span(start, size)].astype(f32) + box[...].astype(f32)
+            work[span(start, size)] = held.astype(bf16)
+        elif stage == 3:
+            held = work[span(at_far + outer * pieces, pieces)].astype(f32)
+            for step in range(outer_count - 1):
+                held = held + deeps[chunk][step].astype(f32)
+            out[span(at_far + outer * pieces, pieces)] = held.astype(bf16)
+
+    barrier = pltpu.get_barrier_semaphore()
+    others = [core_at, x_at, y_at]
+    for step in range(1, outer_count):
+        others.append({"outer": lax.rem(outer + step, outer_count)})
+    for device in others:
+        pl.semaphore_signal(
+            barrier, inc=1, device_id=device, device_id_type=pl.DeviceIdType.MESH
+        )
+    width = small_ref.shape[1]
+    model = normed_ref.shape[1]
+    heads = attended_ref.shape[1]
+    kept = (turned_ref.shape[1] - heads) // 2
+
+    def product(chunk):
+        if chunk == 0:
+            work_one[...] = dot_tn(attended_ref[...], branch_ref[...]).astype(bf16)
+        elif chunk == 1:
+            work_two[...] = dot_tn(normed_ref[...], turned_ref[:, :heads]).astype(bf16)
+        elif chunk == 2:
+            work_three[...] = dot_tn(
+                normed_ref[...], turned_ref[:, heads : heads + kept]
+            ).astype(bf16)
+        else:
+            work_four[:, :kept] = dot_tn(
+                normed_ref[...], turned_ref[:, heads + kept :]
+            ).astype(bf16)
+            work_four[:, kept:] = small_ref[...].astype(bf16)
+
+    product(0)
+    pl.semaphore_wait(barrier, 2 + outer_count)
+    for slot in range(8 + 4):
+        for chunk in range(4):
+            stage = slot - chunk
+            if stage > 0 and stage <= 8:
+                arrive(chunk, stage - 1)
+            if stage == 0 and chunk > 0:
+                product(chunk)
+            if 0 <= stage < 8:
+                for copy in copies(chunk, stage):
+                    copy.start()
+    for chunk in range(4):
+        for stage in range(8):
+            for copy in copies(chunk, stage):
+                copy.wait_send()
+
+
+def reduce_layer(normed, turned, attended, branch, small, outer_count):
+    bf16 = jnp.bfloat16
+    model, heads = normed.shape[1], attended.shape[1]
+    kept = (turned.shape[1] - heads) // 2
+    tops = [heads, model, model, model]
+    widths = [model, heads, kept, kept + small.shape[1]]
+    vmem, dma = pltpu.VMEM, pltpu.SemaphoreType.DMA
+    inside = pl.BlockSpec(memory_space=pltpu.VMEM)
+    scratch = []
+    for cut in (1, 2, 4, 8):
+        scratch += [vmem((top // cut, width), bf16) for top, width in zip(tops, widths)]
+    scratch += [
+        vmem((outer_count - 1, top // 8 // outer_count, width), bf16)
+        for top, width in zip(tops, widths)
+    ]
+    return pl.pallas_call(
+        functools.partial(reduce_kernel, outer_count),
+        out_shape=tuple(
+            jax.ShapeDtypeStruct((top, width), bf16) for top, width in zip(tops, widths)
+        ),
+        in_specs=[inside] * 5,
+        out_specs=(inside,) * 4,
+        scratch_shapes=scratch
+        + [dma((32,)), dma((32,)), dma((8 * (outer_count - 1),)), dma((8 * (outer_count - 1),))],
+        compiler_params=pltpu.CompilerParams(
+            collective_id=1, has_side_effects=True, vmem_limit_bytes=60 << 20
+        ),
+        name="reduce_layer",
+    )(normed, turned, attended, branch, small)
+
+
 def on_device(
     hidden_in,
     segment_ids,
@@ -699,34 +911,51 @@
         [router_grad, attn_gain_grad[:, None], ffn_gain_grad[:, None]], axis=1
     )
     small = jnp.pad(small, ((0, 0), (0, 128 - small.shape[1])))
-    columns = jnp.concatenate(
-        [query_w_grad, key_w_grad, value_w_grad, out_w_grad, small], axis=1
-    ).astype(bf16)
-    mixed_late, columns = lax.optimization_barrier((mixed_rows, columns))
-    hidden_out = (mixed_late + moe_rows.astype(f32)).astype(bf16)
     if fused:
-        columns, hidden_out, weight_last = lax.optimization_barrier(
-            (columns, hidden_out, weight_last)
+        turned = jnp.concatenate([query_grad, key_grad, value_grad], axis=1)
+        mixed_late, turned = lax.optimization_barrier((mixed_rows, turned))
+        hidden_out = (mixed_late + moe_rows.astype(f32)).astype(bf16)
+        small, hidden_out, weight_last = lax.optimization_barrier(
+            (small, hidden_out, weight_last)
         )
         weight_sum = weight_first.astype(f32) + weight_last.astype(f32)
         gate_w_grad = weight_sum[:part].T[None]
         up_w_grad = weight_sum[part : 2 * part].T[None]
         down_w_grad = weight_sum[2 * part :][None]
-    shares = lax.psum_scatter(columns, everywhere, scatter_dimension=0, tiled=True)
-    columns = lax.all_gather(shares, everywhere, axis=0, tiled=True).astype(f32)
-    starts = [0]
-    for width in (w_query.shape[1], w_key.shape[1], w_value.shape[1], model_width, experts, 1, 1):
-        starts.append(starts[-1] + width)
-    pieces = [columns[:, low:high] for low, high in zip(starts[:-1], starts[1:])]
-    summed = (
-        pieces[5][:, 0],
-        pieces[0],
-        pieces[1],
-        pieces[2],
-        pieces[3],
-        pieces[6][:, 0],
-        pieces[4],
-    )
+        out_sum, query_sum, key_sum, value_sum = reduce_layer(
+            normed, turned, attended, branch_grad, small, outer_count
+        )
+        key_width = w_key.shape[1]
+        small = value_sum[:, key_width:].astype(f32)
+        summed = (
+            small[:, experts],
+            query_sum.astype(f32),
+            key_sum.astype(f32),
+            value_sum[:, :key_width].astype(f32),
+            out_sum.astype(f32),
+            small[:, experts + 1],
+            small[:, :experts],
+        )
+    else:
+        columns = jnp.concatenate(
+            [query_w_grad, key_w_grad, value_w_grad, out_w_grad, small], axis=1
+        ).astype(bf16)
+        hidden_out = (mixed_rows + moe_rows.astype(f32)).astype(bf16)
+        shares = lax.psum_scatter(columns, everywhere, scatter_dimension=0, tiled=True)
+        columns = lax.all_gather(shares, everywhere, axis=0, tiled=True).astype(f32)
+        starts = [0]
+        for width in (w_query.shape[1], w_key.shape[1], w_value.shape[1], model_width, experts, 1, 1):
+            starts.append(starts[-1] + width)
+        pieces = [columns[:, low:high] for low, high in zip(starts[:-1], starts[1:])]
+        summed = (
+            pieces[5][:, 0],
+            pieces[0],
+            pieces[1],
+            pieces[2],
+            pieces[3],
+            pieces[6][:, 0],
+            pieces[4],
+        )
     return (
         hidden_out,
         grad_in,

time: 606 us -> 485 us (0.80)
  waiting for transfers between devices: 227 us -> 19.9 us
  Pallas kernels: 194 us -> 315 us
  matrix products: 78.9 us -> 57.8 us
  local copies, waits for them, and re-layouts: 37.6 us -> 20.3 us
    reduce_scatter x1 -> x0, waiting for transfers between devices: 149 us -> none  [on_device(): lax.psum_scatter(columns, everywhere, scatter_dimension=0, tiled=True)]
    pallas_call x0 -> x1, Pallas kernels: none -> 121 us  [reduce_layer(): pl.pallas_call(functools.partial(reduce_kernel, outer_count), out_shape=t...]
    all_gather x1 -> x0, waiting for transfers between devices: 62.1 us -> none  [on_device(): columns = lax.all_gather(shares, everywhere, axis=0, tiled=True).astype(f32)]
    unnamed x150 -> x141, local copies, waits for them, and re-layouts: 22.6 us -> 11.1 us
    slice x4 -> x1, local copies, waits for them, and re-layouts: 10.5 us -> 1.23 us  [on_device(): small[:, experts + 1]]
    dot_general x4 -> x0, matrix products: 9.13 us -> none  [the longest x1 2.78 us: on_device(): jnp.einsum('sd,sh->dh', normed, query_grad, preferred_element_type=f32)]
    dot_general x1, matrix products: 14.8 us -> 7.93 us  [on_device(): jnp.einsum('qngd,knd->ngqk', attended_grad, value_rows, preferred_element...]
    convert_element_type x1 -> x7, other arithmetic: 8.61 us -> 12.8 us  [the longest x1 2.95 us: on_device(): value_sum[:, :key_width].astype(f32)]
  transfers between devices with their start and end apart: 7 -> 5, of which waited for: 3 -> 2; matrix products, arithmetic and copies ran while one was open for 20% -> 21% of each run, Pallas kernels for 0% -> 0%
where the time goes in v4:
time: 485 us; the launch traced here: 481 us
  Pallas kernels  315 us (65%)
  matrix products  57.8 us (12%)
  other arithmetic  47.2 us (10%)
  local copies, waits for them, and re-layouts  20.3 us (4%)
  waiting for transfers between devices  19.9 us (4%)
  between operations  15.2 us (3%)
  starting transfers between devices  4.87 us (1%)
    pallas_call x1, Pallas kernels, expert_layer(): pl.pallas_call(functools.partial(expert_kernel, outer_count), out_shape=(...  194 us
    pallas_call x1, Pallas kernels, reduce_layer(): pl.pallas_call(functools.partial(reduce_kernel, outer_count), out_shape=t...  121 us
    all_gather x1, waiting for transfers between devices, on_device(): rows_grad = lax.all_gather(grad_out, here, axis=0, tiled=True)  16 us
    unnamed x141, local copies, waits for them, and re-layouts  11.1 us
    dot_general x1, matrix products, on_device(): jnp.einsum('ngqk,knd->qngd', weights_prob.astype(bf16), value_rows, prefe...  10.1 us
  transfers between devices with their start and end apart: 5, of which 2 were waited for; matrix products, arithmetic and copies ran while one was open for 21% of the time, Pallas kernels for 0%

profile of v4, /device:TPU:0, one launch (start us, length us, event | category | flops | bytes accessed | tf_op | source)
XLA Modules:
  0.0 480.5 jit_solution(7472846437890678252)
XLA Ops:
  8.0 3.1 collective-permute-start.1
  12.4 1.6 collective-permute-start
  18.4 1.3 fusion.58
  20.1 7.5 %fusion.56 = (f32[8,2,512]{2,1,0:T(2,128)S(1)}, f32[8,2,512,512]{2,3,1,0:T(8,128)}) fusion(bf16[512,8,2,32]{0,3,2,1:T(8,128)(2,1)S(1)} %bitcast.157, bf16[512,8,2,32]{0,3,2,1:T(8,128)(2,1)S(1)} %bitcast.155, bf16[512,8,32]{0,2,1:T(8,128)(2,1)S(1)} %get-tuple-element.106, bf16[512,8,32]{0,2,1:T(8,128)(2,1)S(1)} %get-tuple-element.105, ...), kind=kOutput, calls=%fused_computation.135 | convolution fusion | flops 552591360 | bytes 18644992 | tf_op jit(solution)/shard_map/qngd,knd->ngqk/dot_general | solution.py:52
  27.6 8.3 %exponential_reduce_fusion = f32[8,2,512]{2,1,0:T(2,128)S(1)} fusion(f32[8,2,512,512]{2,3,1,0:T(8,128)} %get-tuple-element.118, f32[8,2,512]{2,1,0:T(2,128)S(1)} %get-tuple-element.117), kind=kLoop, calls=%fused_computation.8 | loop fusion | flops 8380416 | bytes 16842752 | tf_op jit(solution)/shard_map/reduce_sum | solution.py:781
  36.8 10.1 %fusion.18 = bf16[8,64,2,512]{3,1,2,0:T(8,128)(2,1)S(1)} fusion(bf16[512,8,64,1]{0,2,3,1:T(8,128)(2,1)S(1)} %bitcast.153, f32[8,2,512,512]{2,3,1,0:T(8,128)} %get-tuple-element.118, f32[8,2,512]{2,1,0:T(2,128)S(1)} %bitcast.161), kind=kOutput, calls=%fused_computation.39 | convolution fusion | flops 545783808 | bytes 18382848 | tf_op jit(solution)/shard_map/ngqk,knd->qngd/dot_general | solution.py:783
  46.9 1.4 multiply_reduce_fusion.2
  51.0 16.0 %all-gather.2.cloned.1.call-done = bf16[4096,1024]{1,0:T(8,128)(2,1)} async-done(((bf16[512,1024]{1,0:T(8,128)(2,1)}), bf16[4096,1024]{1,0:T(8,128)(2,1)}) %all-gather.2.cloned.1.call-update) | async-done | bytes 8388624 | tf_op jit(solution)/shard_map/all_gather | solution.py:759
  66.9 194.4 %expert_layer.1 = (f32[512,1024]{1,0:T(8,128)}, bf16[8,512,1024]{2,1,0:T(8,128)(2,1)}, f32[8,8,512]{2,1,0:T(8,128)}, bf16[768,1024]{1,0:T(8,128)(2,1)}, bf16[768,1024]{1,0:T(8,128)(2,1)}) custom-call(bf16[512,1024]{1,0:T(8,128)(2,1)} %copy-done.7, bf16[48,512]{1,0:T(8,128)(2,1)} %pad_maximum_fusion.8.gate_hbm, bf16[8,512,1024]{2,1,0:T(8,128)(2,1)} %bitcast.173, ...), custom_call_target="tpu_custom_call" | custom-call | flops 77309411328 | bytes 67108864 | tf_op jit(solution)/shard_map/expert_layer/pallas_call | solution.py:466
  262.5 1.3 copy.89.attended_ref
  264.8 3.2 multiply_reduce_fusion.1
  268.0 2.0 fusion.55
  271.0 1.3 convolution_convert_fusion
  273.4 9.2 %fusion.26 = bf16[8,64,512]{2,1,0:T(8,128)(2,1)S(1)} fusion(bf16[512,8,2,64]{0,3,2,1:T(8,128)(2,1)S(1)} %bitcast.140, f32[8,2,512,512]{2,3,1,0:T(8,128)} %get-tuple-element.118, f32[8,2,512]{2,1,0:T(2,128)S(1)} %bitcast.162), kind=kOutput, calls=%fused_computation.44 | convolution fusion | flops 545521664 | bytes 18382848 | tf_op jit(solution)/shard_map/ngqk,qngd->knd/dot_general | solution.py:880
  284.4 7.9 %fusion = (f32[8,2,512]{2,1,0:T(2,128)S(1)}, f32[8,512,512,2]{2,1,3,0:T(8,128)S(1)}) fusion(f32[8,2,512,512]{2,3,1,0:T(8,128)} %get-tuple-element.118, f32[8,2,512]{2,1,0:T(2,128)S(1)} %bitcast.163, bf16[512,8,64,1]{0,2,3,1:T(8,128)(2,1)S(1)} %bitcast.154, bf16[512,8,2,64]{0,3,2,1:T(8,128)(2,1)} %bitcast.141), kind=kOutput, calls=%fused_computation.3 | convolution fusion | flops 549445632 | bytes 35192832 | tf_op jit(solution)/shard_map/qngd,knd->ngqk/dot_general | solution.py:883
  292.3 8.7 %fusion.2 = bf16[8,2,512,512]{2,3,1,0:T(8,128)(2,1)S(1)} fusion(f32[8,512,512,2]{2,1,3,0:T(8,128)S(1)} %get-tuple-element.125, f32[8,2,512,512]{2,3,1,0:T(8,128)} %get-tuple-element.118, f32[8,2,512]{2,1,0:T(2,128)S(1)} %get-tuple-element.124, f32[8,2,512]{2,1,0:T(2,128)S(1)} %bitcast.164), kind=kLoop, calls=%fused_computation.5 | loop fusion | flops 16777216 | bytes 42008576 | tf_op jit(solution)/shard_map/convert_element_type | solution.py:886
  301.1 4.2 fusion.25
  306.6 5.0 %convolution_multiply_fusion = f32[8,64,2,512]{3,1,2,0:T(8,128)S(1)} fusion(bf16[8,2,512,512]{2,3,1,0:T(8,128)(2,1)} %copy-done, bf16[512,8,32]{0,2,1:T(8,128)(2,1)S(1)} %copy-done.39, bf16[512,8,32]{0,2,1:T(8,128)(2,1)S(1)} %copy-done.37), kind=kOutput, calls=%fused_computation.37 | convolution fusion | flops 538443776 | bytes 11010048 | tf_op jit(solution)/shard_map/ngqk,knd->qngd/dot_general | solution.py:887
  313.0 2.7 pad_maximum_fusion.turned_ref
  317.4 1.3 fusion.59
  319.4 2.6 fusion.17
  323.1 4.0 fusion.16
  327.0 3.2 reduce-scatter.2.cloned.1.call-done
  330.2 2.5 add_convert_fusion
  332.8 120.9 %reduce_layer.1 = (bf16[1024,1024]{1,0:T(8,128)(2,1)}, bf16[1024,1024]{1,0:T(8,128)(2,1)}, bf16[1024,512]{1,0:T(8,128)(2,1)}, bf16[1024,640]{1,0:T(8,128)(2,1)}) custom-call(bf16[512,1024]{1,0:T(8,128)(2,1)} %copy-done.16, bf16[512,2048]{1,0:T(8,128)(2,1)} %pad_maximum_fusion.turned_ref, bf16[512,1024]{1,0:T(8,128)(2,1)} %copy.89.attended_ref, ...), custom_call_target="tpu_custom_call" | custom-call | tf_op jit(solution)/shard_map/reduce_layer/pallas_call | solution.py:716
  454.7 3.0 slice_convert_fusion
  459.7 2.0 convert_add_fusion.1
  462.9 1.3 copy.92
  464.2 1.3 copy.91
  466.2 2.5 convert_element_type.113
  468.7 1.6 convert_element_type.114
  471.0 2.5 convert_element_type.116
  (192 shorter events, 27.5 us)
Async XLA Ops:
  7.2 6.9 %copy-start.4 = (bf16[512,1024]{1,0:T(8,128)(2,1)S(1)}, bf16[512,1024]{1,0:T(8,128)(2,1)}, u32[]{:S(2)}) copy-start(bf16[512,1024]{1,0:T(8,128)(2,1)} %param.14) | copy-start | bytes 3145732
  7.2 8.7 %copy-start.64 = (s32[1,512]{1,0:T(1,128)S(1)}, s32[1,512]{1,0:T(1,128)}, u32[]{:S(2)}) copy-start(s32[1,512]{1,0:T(1,128)} %param.15) | copy-start | bytes 6148
  7.2 8.9 %copy-start.53 = (f32[1024]{0:T(1024)S(1)}, f32[1024]{0:T(1024)}, u32[]{:S(2)}) copy-start(f32[1024]{0:T(1024)} %param.17) | copy-start | bytes 12292
  7.2 59.7 %all-gather.2.cloned.1.call-start = ((), (), s32[]{:S(2)}) async-start(), calls=%async_computation.1 | async-start | bytes 9437184 | tf_op jit(solution)/shard_map/all_gather | solution.py:759
  7.9 322.3 %reduce-scatter.2.cloned.1.call-start = ((), (), s32[]{:S(2)}) async-start(), calls=%async_computation.2 | async-start | bytes 9437184 | tf_op jit(solution)/shard_map/reduce_scatter | solution.py:806
  8.0 42.9 %collective-permute-start.1 = (bf16[256,1024]{1,0:T(8,128)(2,1)}, bf16[256,1024]{1,0:T(8,128)(2,1)}, u32[]{:S(2)}, u32[]{:S(2)}) collective-permute-start(bf16[256,1024]{1,0:T(8,128)(2,1)} %bitcast.174), channel_id=1, source_target_pairs={{0,8},{8,16},{16,24},{24,0},{1,9},{9,17},{17,25},{25,1},{2,10},{10... | collective-permute-start | bytes 1572872 | tf_op jit(solution)/shard_map/ppermute | solution.py:460
  12.4 4.8 %copy-start.35 = (bf16[1024,512]{1,0:T(8,128)(2,1)}, bf16[1024,512]{1,0:T(8,128)(2,1)S(1)}, u32[]{:S(2)}) copy-start(bf16[1024,512]{1,0:T(8,128)(2,1)S(1)} %pad_maximum_fusion.2.pair_own) | copy-start | bytes 3145732
  12.4 4.0 copy-start.30
  12.4 38.5 %collective-permute-start = (bf16[1024,512]{1,0:T(8,128)(2,1)S(1)}, bf16[1024,512]{1,0:T(8,128)(2,1)}, u32[]{:S(2)}, u32[]{:S(2)}) collective-permute-start(bf16[1024,512]{1,0:T(8,128)(2,1)S(1)} %pad_maximum_fusion.2.pair_own), channel_id=1, source_target_pairs={{0,8},{8,16},{16,24},{24,0},{1,9},{9,17},{17,25},{25,1},{2,10},{10... | collective-permute-start | bytes 3145736 | tf_op jit(solution)/shard_map/ppermute | solution.py:459
  15.9 3.8 copy-start.27
  16.4 19.5 %copy-start.16 = (bf16[512,1024]{1,0:T(8,128)(2,1)}, bf16[512,1024]{1,0:T(8,128)(2,1)S(1)}, u32[]{:S(2)}) copy-start(bf16[512,1024]{1,0:T(8,128)(2,1)S(1)} %fusion.10.normed_ref) | copy-start | bytes 3145732
  20.1 7.5 %copy-start.21 = (bf16[512,16,32]{0,2,1:T(8,128)(2,1)}, bf16[512,16,32]{0,2,1:T(8,128)(2,1)S(1)}, u32[]{:S(2)}) copy-start(bf16[512,16,32]{0,2,1:T(8,128)(2,1)S(1)} %get-tuple-element.101) | copy-start | bytes 1572868
  20.1 7.5 %copy-start.23 = (bf16[512,16,32]{0,2,1:T(8,128)(2,1)}, bf16[512,16,32]{0,2,1:T(8,128)(2,1)S(1)}, u32[]{:S(2)}) copy-start(bf16[512,16,32]{0,2,1:T(8,128)(2,1)S(1)} %get-tuple-element.102) | copy-start | bytes 1572868
  27.6 8.3 %copy-start.32 = (bf16[1024,512]{1,0:T(8,128)(2,1)S(1)}, bf16[1024,512]{1,0:T(8,128)(2,1)}, u32[]{:S(2)}) copy-start(bf16[1024,512]{1,0:T(8,128)(2,1)} %param.20) | copy-start | bytes 3145732
  36.0 10.9 %copy-start.42 = (f32[2,8,512]{2,1,0:T(8,128)}, f32[2,8,512]{2,1,0:T(8,128)S(1)}, u32[]{:S(2)}) copy-start(f32[2,8,512]{2,1,0:T(8,128)S(1)} %log_add_fusion) | copy-start | bytes 98308
  36.7 10.1 %copy-start.17 = (bf16[512,512]{0,1:T(8,128)(2,1)}, bf16[512,512]{0,1:T(8,128)(2,1)S(1)}, u32[]{:S(2)}) copy-start(bf16[512,512]{0,1:T(8,128)(2,1)S(1)} %convolution_convert_fusion.1) | copy-start | bytes 1572868
  36.8 10.1 %copy-start.24 = (bf16[1024,1024]{1,0:T(8,128)(2,1)S(1)}, bf16[1024,1024]{1,0:T(8,128)(2,1)}, u32[]{:S(2)}) copy-start(bf16[1024,1024]{1,0:T(8,128)(2,1)} %param.21) | copy-start | bytes 6291460
  261.3 3.3 copy-start.41
  261.4 3.4 copy-start.2
  261.4 3.4 copy-start.48
  261.4 3.3 copy-start.52
  261.4 3.3 copy-start.61
  264.0 68.8 %collective-permute-start.2 = (bf16[768,1024]{1,0:T(8,128)(2,1)}, bf16[768,1024]{1,0:T(8,128)(2,1)}, u32[]{:S(2)}, u32[]{:S(2)}) collective-permute-start(bf16[768,1024]{1,0:T(8,128)(2,1)} %get-tuple-element.30), channel_id=1, source_target_pairs={{0,8},{8,16},{16,24},{24,0},{1,9},{9,17},{17,25},{25,1},{2,10},{10... | collective-permute-start | bytes 4718600 | tf_op jit(solution)/shard_map/ppermute | solution.py:516
  273.4 9.2 %copy-start.6 = (bf16[512,1024]{0,1:T(8,128)(2,1)}, bf16[512,1024]{0,1:T(8,128)(2,1)S(1)}, u32[]{:S(2)}) copy-start(bf16[512,1024]{0,1:T(8,128)(2,1)S(1)} %copy.81) | copy-start | bytes 3145732
  273.4 11.0 %copy-start.18 = (bf16[512,512]{0,1:T(8,128)(2,1)S(1)}, bf16[512,512]{0,1:T(8,128)(2,1)}, u32[]{:S(2)}) copy-start(bf16[512,512]{0,1:T(8,128)(2,1)} %copy-done.17) | copy-start | bytes 1572868
  292.3 8.7 %copy-start.22 = (bf16[512,16,32]{0,2,1:T(8,128)(2,1)S(1)}, bf16[512,16,32]{0,2,1:T(8,128)(2,1)}, u32[]{:S(2)}) copy-start(bf16[512,16,32]{0,2,1:T(8,128)(2,1)} %copy-done.21) | copy-start | bytes 1572868
  301.1 4.3 copy-start
  301.1 4.3 copy-start.28
  301.1 4.3 copy-start.44
  319.4 3.7 copy-start.65
  323.1 7.2 %copy-start.3 = (f32[512,1024]{1,0:T(8,128)S(1)}, f32[512,1024]{1,0:T(8,128)}, u32[]{:S(2)}) copy-start(f32[512,1024]{1,0:T(8,128)} %copy-done.1) | copy-start | bytes 6291460
  454.7 5.0 %copy-start.29 = (bf16[768,1024]{1,0:T(8,128)(2,1)S(1)}, bf16[768,1024]{1,0:T(8,128)(2,1)}, u32[]{:S(2)}) copy-start(bf16[768,1024]{1,0:T(8,128)(2,1)} %get-tuple-element.38) | copy-start | bytes 4718596
  (42 other events, 78.0 us)
Sparse Core Ops, SparseCore 0:
  9.9 56.9 all-gather.1
  261.5 68.7 reduce-scatter.1

commit v5 on v4

--- a/solution.py
+++ b/solution.py
@@ -175,13 +175,13 @@
         return wide.at[:, pl.ds(slot * 2 * part, 2 * part)]
 
     def weight(index):
-        slot = 1 + index // 2
+        source, target, device = ((1, 2, next_at), (0, 3, before_at))[index // 2]
         if index % 2 == 0:
             return remote(
-                wide_at(slot), wide_at(slot + 1), weight_send, weight_recv, index, next_at
+                wide_at(source), wide_at(target), weight_send, weight_recv, index, device
             )
         return remote(
-            down.at[slot], down.at[slot + 1], weight_send, weight_recv, index, next_at
+            down.at[source], down.at[target], weight_send, weight_recv, index, device
         )
 
     def ring_copy(index):
@@ -301,10 +301,11 @@
             weight(2).start()
             weight(3).start()
 
-        @pl.when(step == 24)
+        @pl.when(step == 20)
         def _():
             weight(2).wait_recv()
             weight(3).wait_recv()
+            ring_copy(0).start()
 
         fetch(step).wait()
         here = rows[slot]
@@ -331,20 +332,12 @@
         pair_grad = dot_tn(both[slot, :, pl.ds(block * 2 * part, 2 * part)], here)
         down_grad = dot_tn(act[slot, :, pl.ds(block * part, part)], grad_rows)
 
-        @pl.when(order == 0)
-        def _():
-            total[: 2 * part] = pair_grad
-            total[2 * part :] = down_grad
-
-        @pl.when(order > 0)
-        def _():
-            total[: 2 * part] += pair_grad
-            total[2 * part :] += down_grad
+        total[: 2 * part] = jnp.where(order == 0, pair_grad, total[: 2 * part] + pair_grad)
+        total[2 * part :] = jnp.where(order == 0, down_grad, total[2 * part :] + down_grad)
 
         @pl.when(step == 7)
         def _():
             stage_a[...] = total[...].astype(bf16)
-            ring_copy(0).start()
 
         @pl.when(step == 15)
         def _():
@@ -352,20 +345,17 @@
 
         @pl.when(step == 23)
         def _():
-            ring_copy(0).wait()
-            stage_b[...] = (stage_b[...].astype(f32) + ring[0].astype(f32)).astype(bf16)
-            ring_copy(1).start()
-            stage_a[...] = total[...].astype(bf16)
-            local(stage_a, first_hbm, 0).start()
-
-        @pl.when(step == 31)
-        def _():
-            local(stage_a, first_hbm, 0).wait()
-            stage_a[...] = total[...].astype(bf16)
+            copy = local(total, first_hbm, 0)
+            copy.start()
+            copy.wait()
 
         return carry
 
     lax.fori_loop(0, 8 * outer_count, first_step, 0)
+    ring_copy(0).wait()
+    stage_a[...] = total[...].astype(bf16)
+    stage_b[...] = (stage_b[...].astype(f32) + ring[0].astype(f32)).astype(bf16)
+    ring_copy(1).start()
     for slot in range(1, 8):
         dots_copy(slot).start()
     for index in range(15):
@@ -469,7 +459,7 @@
             jax.ShapeDtypeStruct((length, width), f32),
             jax.ShapeDtypeStruct((8, length, width), bf16),
             jax.ShapeDtypeStruct((8, 8, length), f32),
-            share,
+            jax.ShapeDtypeStruct((3 * part, width), f32),
             share,
         ),
         in_specs=[anywhere] * 7,
@@ -512,7 +502,15 @@
             flops=18 * 8 * length * width * hidden, bytes_accessed=1 << 26, transcendentals=0
         ),
         name="expert_layer",
-    )(rows_own, gate_table, rows_grad.reshape(8, length, width), pair_own, down_own, pair_next, down_next)
+    )(
+        rows_own,
+        gate_table,
+        rows_grad.reshape(8, length, width),
+        pair_own,
+        down_own,
+        pair_next,
+        down_next,
+    )
     last = lax.ppermute(last, "outer", ahead)
     return dx, y_rows.reshape(8 * length, width), dots, first, last
 
@@ -682,10 +680,10 @@
 
     product(0)
     pl.semaphore_wait(barrier, 2 + outer_count)
-    for slot in range(8 + 4):
+    for slot in range(8 + 2):
         for chunk in range(4):
-            stage = slot - chunk
-            if stage > 0 and stage <= 8:
+            stage = slot - chunk // 2
+            if 0 < stage <= 8:
                 arrive(chunk, stage - 1)
             if stage == 0 and chunk > 0:
                 product(chunk)
@@ -918,7 +916,7 @@
         small, hidden_out, weight_last = lax.optimization_barrier(
             (small, hidden_out, weight_last)
         )
-        weight_sum = weight_first.astype(f32) + weight_last.astype(f32)
+        weight_sum = weight_first + weight_last.astype(f32)
         gate_w_grad = weight_sum[:part].T[None]
         up_w_grad = weight_sum[part : 2 * part].T[None]
         down_w_grad = weight_sum[2 * part :][None]

time: 485 us -> 432 us (0.89)
  Pallas kernels: 315 us -> 261 us
    pallas_call x1, Pallas kernels: 121 us -> 89.3 us  [reduce_layer(): pl.pallas_call(functools.partial(reduce_kernel, outer_count), out_shape=t...]
    pallas_call x1, Pallas kernels: 194 us -> 171 us  [expert_layer(): pl.pallas_call(functools.partial(expert_kernel, outer_count), out_shape=(...]
    unnamed x141 -> x139, local copies, waits for them, and re-layouts: 11.1 us -> 10.4 us
  transfers between devices with their start and end apart: 5 -> 5, of which waited for: 2 -> 2; matrix products, arithmetic and copies ran while one was open for 21% -> 23% of each run, Pallas kernels for 0% -> 0%
where the time goes in v5:
time: 432 us; the launch traced here: 427 us
  Pallas kernels  261 us (60%)
  matrix products  57.9 us (13%)
  other arithmetic  49 us (11%)
  waiting for transfers between devices  19.9 us (5%)
  local copies, waits for them, and re-layouts  19.6 us (5%)
  between operations  15.2 us (4%)
  starting transfers between devices  4.87 us (1%)
    pallas_call x1, Pallas kernels, expert_layer(): pl.pallas_call(functools.partial(expert_kernel, outer_count), out_shape=(...  171 us
    pallas_call x1, Pallas kernels, reduce_layer(): pl.pallas_call(functools.partial(reduce_kernel, outer_count), out_shape=t...  89.3 us
    all_gather x1, waiting for transfers between devices, on_device(): rows_grad = lax.all_gather(grad_out, here, axis=0, tiled=True)  16 us
    unnamed x139, local copies, waits for them, and re-layouts  10.4 us
    dot_general x1, matrix products, on_device(): jnp.einsum('ngqk,knd->qngd', weights_prob.astype(bf16), value_rows, prefe...  10.1 us
    dot_general x1, matrix products, on_device(): jnp.einsum('ngqk,qngd->knd', weights_prob.astype(bf16), attended_grad, pr...  9.2 us
    convert_element_type x1, other arithmetic, on_device(): score_grad = (weights_prob * (prob_grad - jnp.sum(weights_prob * prob_gra...  8.71 us
  transfers between devices with their start and end apart: 5, of which 2 were waited for; matrix products, arithmetic and copies ran while one was open for 23% of the time, Pallas kernels for 0%

profile of v5, /device:TPU:0, one launch (start us, length us, event | category | flops | bytes accessed | tf_op | source)
XLA Modules:
  0.0 427.1 jit_solution(16774830944195491861)
XLA Ops:
  8.0 3.1 collective-permute-start.1
  12.4 1.6 collective-permute-start
  18.4 1.3 fusion.58
  20.1 7.4 %fusion.56 = (f32[8,2,512]{2,1,0:T(2,128)S(1)}, f32[8,2,512,512]{2,3,1,0:T(8,128)}) fusion(bf16[512,8,2,32]{0,3,2,1:T(8,128)(2,1)S(1)} %bitcast.157, bf16[512,8,2,32]{0,3,2,1:T(8,128)(2,1)S(1)} %bitcast.155, bf16[512,8,32]{0,2,1:T(8,128)(2,1)S(1)} %get-tuple-element.106, bf16[512,8,32]{0,2,1:T(8,128)(2,1)S(1)} %get-tuple-element.105, ...), kind=kOutput, calls=%fused_computation.135 | convolution fusion | flops 552591360 | bytes 18644992 | tf_op jit(solution)/shard_map/qngd,knd->ngqk/dot_general | solution.py:52
  27.6 8.3 %exponential_reduce_fusion = f32[8,2,512]{2,1,0:T(2,128)S(1)} fusion(f32[8,2,512,512]{2,3,1,0:T(8,128)} %get-tuple-element.118, f32[8,2,512]{2,1,0:T(2,128)S(1)} %get-tuple-element.117), kind=kLoop, calls=%fused_computation.8 | loop fusion | flops 8380416 | bytes 16842752 | tf_op jit(solution)/shard_map/reduce_sum | solution.py:779
  36.7 10.1 %fusion.18 = bf16[8,64,2,512]{3,1,2,0:T(8,128)(2,1)S(1)} fusion(bf16[512,8,64,1]{0,2,3,1:T(8,128)(2,1)S(1)} %bitcast.153, f32[8,2,512,512]{2,3,1,0:T(8,128)} %get-tuple-element.118, f32[8,2,512]{2,1,0:T(2,128)S(1)} %bitcast.161), kind=kOutput, calls=%fused_computation.39 | convolution fusion | flops 545783808 | bytes 18382848 | tf_op jit(solution)/shard_map/ngqk,knd->qngd/dot_general | solution.py:781
  46.9 1.4 multiply_reduce_fusion.2
  50.9 16.0 %all-gather.2.cloned.1.call-done = bf16[4096,1024]{1,0:T(8,128)(2,1)} async-done(((bf16[512,1024]{1,0:T(8,128)(2,1)}), bf16[4096,1024]{1,0:T(8,128)(2,1)}) %all-gather.2.cloned.1.call-update) | async-done | bytes 8388624 | tf_op jit(solution)/shard_map/all_gather | solution.py:757
  66.9 171.4 %expert_layer.1 = (f32[512,1024]{1,0:T(8,128)}, bf16[8,512,1024]{2,1,0:T(8,128)(2,1)}, f32[8,8,512]{2,1,0:T(8,128)}, f32[768,1024]{1,0:T(8,128)}, bf16[768,1024]{1,0:T(8,128)(2,1)}) custom-call(bf16[512,1024]{1,0:T(8,128)(2,1)} %copy-done.7, bf16[48,512]{1,0:T(8,128)(2,1)} %pad_maximum_fusion.8.gate_hbm, bf16[8,512,1024]{2,1,0:T(8,128)(2,1)} %bitcast.173, ...), custom_call_target="tpu_custom_call" | custom-call | flops 77309411328 | bytes 67108864 | tf_op jit(solution)/shard_map/expert_layer/pallas_call | solution.py:456
  239.6 1.3 copy.89.attended_ref
  241.9 3.2 multiply_reduce_fusion.1
  245.1 2.0 fusion.55
  248.1 1.3 convolution_convert_fusion
  250.4 9.2 %fusion.26 = bf16[8,64,512]{2,1,0:T(8,128)(2,1)S(1)} fusion(bf16[512,8,2,64]{0,3,2,1:T(8,128)(2,1)S(1)} %bitcast.140, f32[8,2,512,512]{2,3,1,0:T(8,128)} %get-tuple-element.118, f32[8,2,512]{2,1,0:T(2,128)S(1)} %bitcast.162), kind=kOutput, calls=%fused_computation.44 | convolution fusion | flops 545521664 | bytes 18382848 | tf_op jit(solution)/shard_map/ngqk,qngd->knd/dot_general | solution.py:878
  261.4 7.9 %fusion = (f32[8,2,512]{2,1,0:T(2,128)S(1)}, f32[8,512,512,2]{2,1,3,0:T(8,128)S(1)}) fusion(f32[8,2,512,512]{2,3,1,0:T(8,128)} %get-tuple-element.118, f32[8,2,512]{2,1,0:T(2,128)S(1)} %bitcast.163, bf16[512,8,64,1]{0,2,3,1:T(8,128)(2,1)S(1)} %bitcast.154, bf16[512,8,2,64]{0,3,2,1:T(8,128)(2,1)} %bitcast.141), kind=kOutput, calls=%fused_computation.3 | convolution fusion | flops 549445632 | bytes 35192832 | tf_op jit(solution)/shard_map/qngd,knd->ngqk/dot_general | solution.py:881
  269.4 8.7 %fusion.2 = bf16[8,2,512,512]{2,3,1,0:T(8,128)(2,1)S(1)} fusion(f32[8,512,512,2]{2,1,3,0:T(8,128)S(1)} %get-tuple-element.125, f32[8,2,512,512]{2,3,1,0:T(8,128)} %get-tuple-element.118, f32[8,2,512]{2,1,0:T(2,128)S(1)} %get-tuple-element.124, f32[8,2,512]{2,1,0:T(2,128)S(1)} %bitcast.164), kind=kLoop, calls=%fused_computation.5 | loop fusion | flops 16777216 | bytes 42008576 | tf_op jit(solution)/shard_map/convert_element_type | solution.py:884
  278.1 4.3 fusion.25
  283.7 5.0 %convolution_multiply_fusion = f32[8,64,2,512]{3,1,2,0:T(8,128)S(1)} fusion(bf16[8,2,512,512]{2,3,1,0:T(8,128)(2,1)} %copy-done, bf16[512,8,32]{0,2,1:T(8,128)(2,1)S(1)} %copy-done.38, bf16[512,8,32]{0,2,1:T(8,128)(2,1)S(1)} %copy-done.36), kind=kOutput, calls=%fused_computation.37 | convolution fusion | flops 538443776 | bytes 11010048 | tf_op jit(solution)/shard_map/ngqk,knd->qngd/dot_general | solution.py:885
  290.1 2.7 pad_maximum_fusion.turned_ref
  294.5 1.3 fusion.59
  296.5 2.6 fusion.17
  300.1 4.0 fusion.16
  304.1 3.1 reduce-scatter.2.cloned.1.call-done
  307.3 2.5 add_convert_fusion
  309.8 89.3 %reduce_layer.1 = (bf16[1024,1024]{1,0:T(8,128)(2,1)}, bf16[1024,1024]{1,0:T(8,128)(2,1)}, bf16[1024,512]{1,0:T(8,128)(2,1)}, bf16[1024,640]{1,0:T(8,128)(2,1)}) custom-call(bf16[512,1024]{1,0:T(8,128)(2,1)} %copy-done.16, bf16[512,2048]{1,0:T(8,128)(2,1)} %pad_maximum_fusion.turned_ref, bf16[512,1024]{1,0:T(8,128)(2,1)} %copy.89.attended_ref, ...), custom_call_target="tpu_custom_call" | custom-call | tf_op jit(solution)/shard_map/reduce_layer/pallas_call | solution.py:714
  400.2 2.8 slice_convert_fusion
  403.1 2.1 convert_add_fusion.1
  406.4 1.3 copy.92
  407.8 1.3 copy.91
  411.1 4.2 convert_element_type.110
  415.2 1.6 convert_element_type.111
  417.6 2.5 convert_element_type.113
  (190 shorter events, 26.9 us)
Async XLA Ops:
  7.2 6.9 %copy-start.4 = (bf16[512,1024]{1,0:T(8,128)(2,1)S(1)}, bf16[512,1024]{1,0:T(8,128)(2,1)}, u32[]{:S(2)}) copy-start(bf16[512,1024]{1,0:T(8,128)(2,1)} %param.14) | copy-start | bytes 3145732
  7.2 8.7 %copy-start.63 = (s32[1,512]{1,0:T(1,128)S(1)}, s32[1,512]{1,0:T(1,128)}, u32[]{:S(2)}) copy-start(s32[1,512]{1,0:T(1,128)} %param.15) | copy-start | bytes 6148
  7.2 8.9 %copy-start.52 = (f32[1024]{0:T(1024)S(1)}, f32[1024]{0:T(1024)}, u32[]{:S(2)}) copy-start(f32[1024]{0:T(1024)} %param.17) | copy-start | bytes 12292
  7.2 59.7 %all-gather.2.cloned.1.call-start = ((), (), s32[]{:S(2)}) async-start(), calls=%async_computation.1 | async-start | bytes 9437184 | tf_op jit(solution)/shard_map/all_gather | solution.py:757
  7.9 299.3 %reduce-scatter.2.cloned.1.call-start = ((), (), s32[]{:S(2)}) async-start(), calls=%async_computation.2 | async-start | bytes 9437184 | tf_op jit(solution)/shard_map/reduce_scatter | solution.py:804
  8.0 42.9 %collective-permute-start.1 = (bf16[256,1024]{1,0:T(8,128)(2,1)}, bf16[256,1024]{1,0:T(8,128)(2,1)}, u32[]{:S(2)}, u32[]{:S(2)}) collective-permute-start(bf16[256,1024]{1,0:T(8,128)(2,1)} %bitcast.174), channel_id=1, source_target_pairs={{0,8},{8,16},{16,24},{24,0},{1,9},{9,17},{17,25},{25,1},{2,10},{10... | collective-permute-start | bytes 1572872 | tf_op jit(solution)/shard_map/ppermute | solution.py:450
  12.4 4.8 %copy-start.34 = (bf16[1024,512]{1,0:T(8,128)(2,1)}, bf16[1024,512]{1,0:T(8,128)(2,1)S(1)}, u32[]{:S(2)}) copy-start(bf16[1024,512]{1,0:T(8,128)(2,1)S(1)} %pad_maximum_fusion.2.pair_own) | copy-start | bytes 3145732
  12.4 4.0 copy-start.29
  12.4 38.5 %collective-permute-start = (bf16[1024,512]{1,0:T(8,128)(2,1)S(1)}, bf16[1024,512]{1,0:T(8,128)(2,1)}, u32[]{:S(2)}, u32[]{:S(2)}) collective-permute-start(bf16[1024,512]{1,0:T(8,128)(2,1)S(1)} %pad_maximum_fusion.2.pair_own), channel_id=1, source_target_pairs={{0,8},{8,16},{16,24},{24,0},{1,9},{9,17},{17,25},{25,1},{2,10},{10... | collective-permute-start | bytes 3145736 | tf_op jit(solution)/shard_map/ppermute | solution.py:449
  15.9 3.8 copy-start.27
  16.4 19.5 %copy-start.16 = (bf16[512,1024]{1,0:T(8,128)(2,1)}, bf16[512,1024]{1,0:T(8,128)(2,1)S(1)}, u32[]{:S(2)}) copy-start(bf16[512,1024]{1,0:T(8,128)(2,1)S(1)} %fusion.10.normed_ref) | copy-start | bytes 3145732
  20.1 7.5 %copy-start.21 = (bf16[512,16,32]{0,2,1:T(8,128)(2,1)}, bf16[512,16,32]{0,2,1:T(8,128)(2,1)S(1)}, u32[]{:S(2)}) copy-start(bf16[512,16,32]{0,2,1:T(8,128)(2,1)S(1)} %get-tuple-element.101) | copy-start | bytes 1572868
  20.1 7.5 %copy-start.23 = (bf16[512,16,32]{0,2,1:T(8,128)(2,1)}, bf16[512,16,32]{0,2,1:T(8,128)(2,1)S(1)}, u32[]{:S(2)}) copy-start(bf16[512,16,32]{0,2,1:T(8,128)(2,1)S(1)} %get-tuple-element.102) | copy-start | bytes 1572868
  27.6 8.3 %copy-start.31 = (bf16[1024,512]{1,0:T(8,128)(2,1)S(1)}, bf16[1024,512]{1,0:T(8,128)(2,1)}, u32[]{:S(2)}) copy-start(bf16[1024,512]{1,0:T(8,128)(2,1)} %param.20) | copy-start | bytes 3145732
  35.9 10.9 %copy-start.41 = (f32[2,8,512]{2,1,0:T(8,128)}, f32[2,8,512]{2,1,0:T(8,128)S(1)}, u32[]{:S(2)}) copy-start(f32[2,8,512]{2,1,0:T(8,128)S(1)} %log_add_fusion) | copy-start | bytes 98308
  36.7 10.1 %copy-start.18 = (bf16[512,512]{0,1:T(8,128)(2,1)}, bf16[512,512]{0,1:T(8,128)(2,1)S(1)}, u32[]{:S(2)}) copy-start(bf16[512,512]{0,1:T(8,128)(2,1)S(1)} %convolution_convert_fusion.1) | copy-start | bytes 1572868
  36.7 10.1 %copy-start.24 = (bf16[1024,1024]{1,0:T(8,128)(2,1)S(1)}, bf16[1024,1024]{1,0:T(8,128)(2,1)}, u32[]{:S(2)}) copy-start(bf16[1024,1024]{1,0:T(8,128)(2,1)} %param.21) | copy-start | bytes 6291460
  238.5 3.4 copy-start.2
  238.5 3.3 copy-start.47
  238.5 3.3 copy-start.51
  238.5 3.3 copy-start.60
  241.0 68.8 %collective-permute-start.2 = (bf16[768,1024]{1,0:T(8,128)(2,1)}, bf16[768,1024]{1,0:T(8,128)(2,1)}, u32[]{:S(2)}, u32[]{:S(2)}) collective-permute-start(bf16[768,1024]{1,0:T(8,128)(2,1)} %get-tuple-element.30), channel_id=1, source_target_pairs={{0,8},{8,16},{16,24},{24,0},{1,9},{9,17},{17,25},{25,1},{2,10},{10... | collective-permute-start | bytes 4718600 | tf_op jit(solution)/shard_map/ppermute | solution.py:514
  250.3 9.2 %copy-start.6 = (bf16[512,1024]{0,1:T(8,128)(2,1)}, bf16[512,1024]{0,1:T(8,128)(2,1)S(1)}, u32[]{:S(2)}) copy-start(bf16[512,1024]{0,1:T(8,128)(2,1)S(1)} %copy.81) | copy-start | bytes 3145732
  250.3 11.1 %copy-start.19 = (bf16[512,512]{0,1:T(8,128)(2,1)S(1)}, bf16[512,512]{0,1:T(8,128)(2,1)}, u32[]{:S(2)}) copy-start(bf16[512,512]{0,1:T(8,128)(2,1)} %copy-done.18) | copy-start | bytes 1572868
  269.3 8.7 %copy-start.22 = (bf16[512,16,32]{0,2,1:T(8,128)(2,1)S(1)}, bf16[512,16,32]{0,2,1:T(8,128)(2,1)}, u32[]{:S(2)}) copy-start(bf16[512,16,32]{0,2,1:T(8,128)(2,1)} %copy-done.21) | copy-start | bytes 1572868
  278.1 4.3 %copy-start = (bf16[8,2,512,512]{2,3,1,0:T(8,128)(2,1)}, bf16[8,2,512,512]{2,3,1,0:T(8,128)(2,1)S(1)}, u32[]{:S(2)}) copy-start(bf16[8,2,512,512]{2,3,1,0:T(8,128)(2,1)S(1)} %fusion.2) | copy-start | bytes 25165828
  278.1 4.3 %copy-start.28 = (f32[512,32]{0,1:T(8,128)S(1)}, f32[512,32]{0,1:T(8,128)}, u32[]{:S(2)}) copy-start(f32[512,32]{0,1:T(8,128)} %copy-done.27) | copy-start | bytes 196612
  278.1 4.3 %copy-start.43 = (f32[512,32]{0,1:T(8,128)S(1)}, f32[512,32]{0,1:T(8,128)}, u32[]{:S(2)}) copy-start(f32[512,32]{0,1:T(8,128)} %get-tuple-element.114) | copy-start | bytes 196612
  296.5 3.7 copy-start.64
  300.1 7.1 %copy-start.3 = (f32[512,1024]{1,0:T(8,128)S(1)}, f32[512,1024]{1,0:T(8,128)}, u32[]{:S(2)}) copy-start(f32[512,1024]{1,0:T(8,128)} %copy-done.1) | copy-start | bytes 6291460
  399.1 4.0 copy-start.17
  411.1 4.2 copy-start.33
  (41 other events, 76.6 us)
Sparse Core Ops, SparseCore 0:
  9.9 56.9 all-gather.1
  238.5 68.6 reduce-scatter.1

commit v6 on v5

--- a/solution.py
+++ b/solution.py
@@ -71,7 +71,10 @@
     outer_count,
     x_hbm,
     gate_hbm,
-    grad_hbm,
+    grad_own,
+    grad_x,
+    grad_y,
+    grad_far,
     pair_own,
     down_own,
     pair_next,
@@ -81,6 +84,8 @@
     dots_ref,
     first_hbm,
     last_hbm,
+    grad_other,
+    ring_hbm,
     rows,
     gates,
     act,
@@ -110,6 +115,8 @@
     dots_recv,
     back_send,
     back_recv,
+    swap_send,
+    swap_recv,
 ):
     f32 = jnp.float32
     bf16 = jnp.bfloat16
@@ -185,8 +192,8 @@
         )
 
     def ring_copy(index):
-        source = (stage_a, stage_b)[index]
-        return remote(source, ring.at[index], ring_send, ring_recv, index, next_at)
+        source, target = ((stage_a, ring), (stage_b, ring_hbm))[index]
+        return remote(source, target, ring_send, ring_recv, index, next_at)
 
     def dots_copy(slot):
         return remote(
@@ -217,14 +224,33 @@
     for copy in own_copies:
         copy.start()
 
+    grad_same = (grad_own, grad_x, grad_y, grad_far)
+
+    def swap(index):
+        return remote(
+            grad_same[index], grad_other.at[index], swap_send, swap_recv, index, core_at
+        )
+
+    def slot_at(step):
+        order = step % 8
+        return jnp.where(order == 3, 4, jnp.where(order == 4, 3, order))
+
+    def fetch_from(source, step):
+        return pltpu.make_async_copy(source, grads.at[step % 2], grad_sem.at[step % 2])
+
     def fetch(step):
-        order = step % 8
-        slot = jnp.where(order == 3, 4, jnp.where(order == 4, 3, order))
-        return pltpu.make_async_copy(
-            grad_hbm.at[place_of(slot)], grads.at[step % 2], grad_sem.at[step % 2]
-        )
-
-    fetch(0).start()
+        slot = slot_at(step)
+        for index in range(4):
+
+            @pl.when(slot == 2 * index)
+            def _():
+                fetch_from(grad_same[index], step).start()
+
+        @pl.when(slot % 2 == 1)
+        def _():
+            fetch_from(grad_other.at[slot // 2], step).start()
+
+    fetch_from(grad_own, 0).start()
     barrier = pltpu.get_barrier_semaphore()
     for slot in range(1, 8):
         pl.semaphore_signal(
@@ -243,74 +269,11 @@
         copy.wait()
     weight(0).start()
     weight(1).start()
-
-    def first_step(step, carry):
-        turn, order = step // 8, step % 8
-        slot = jnp.where(order == 3, 4, jnp.where(order == 4, 3, order))
-        block = jnp.where(turn == 0, 1, jnp.where(turn == 1, 2, jnp.where(turn == 2, 0, 3)))
-
-        @pl.when(step + 1 < 8 * outer_count)
-        def _():
-            fetch(step + 1).start()
-
-        @pl.when(step == 1)
-        def _():
-            gather(0).wait_recv()
-            gather(8).wait_recv()
-
-        @pl.when(step == 2)
-        def _():
-            gather(1).wait_recv()
-            gather(3).start()
-            gather(5).start()
-            gather(2).wait_recv()
-            gather(4).start()
-            gather(6).start()
-            gather(9).wait_recv()
-            gather(12).start()
-            gather(10).wait_recv()
-            gather(13).start()
-
-        @pl.when(step == 4)
-        def _():
-            gather(5).wait_recv()
-            gather(12).wait_recv()
-
-        @pl.when(step == 5)
-        def _():
-            gather(6).wait_recv()
-            gather(13).wait_recv()
-
-        @pl.when(step == 6)
-        def _():
-            gather(3).wait_recv()
-            gather(4).wait_recv()
-            gather(7).start()
-            gather(11).wait_recv()
-            gather(14).start()
-
-        @pl.when(step == 7)
-        def _():
-            gather(7).wait_recv()
-            gather(14).wait_recv()
-
-        @pl.when(step == 8)
-        def _():
-            weight(0).wait_recv()
-            weight(1).wait_recv()
-            weight(2).start()
-            weight(3).start()
-
-        @pl.when(step == 20)
-        def _():
-            weight(2).wait_recv()
-            weight(3).wait_recv()
-            ring_copy(0).start()
-
-        fetch(step).wait()
-        here = rows[slot]
-        grad_rows = grads[step % 2]
-        products = dot_nn(here, wide[:, pl.ds(block * 2 * part, 2 * part)])
+    for index in range(4):
+        swap(index).start()
+
+    def forward(slot, block, grad_rows):
+        products = dot_nn(rows[slot], wide[:, pl.ds(block * 2 * part, 2 * part)])
         gate_act, up_act = products[:, :part], products[:, part:]
         raw = dot_nt(grad_rows, down[block])
         expert = lax.rem(outer + outer_count - block, outer_count) * INNER + inner
@@ -329,15 +292,100 @@
             hidden * up_act * sigmoid * (1.0 + gate_act * (1.0 - sigmoid))
         ).astype(bf16)
         both[slot, :, pl.ds(block * 2 * part + part, part)] = (hidden * silu).astype(bf16)
-        pair_grad = dot_tn(both[slot, :, pl.ds(block * 2 * part, 2 * part)], here)
+
+    def gather_weights(slot, block, order, grad_rows):
+        pair_grad = dot_tn(both[slot, :, pl.ds(block * 2 * part, 2 * part)], rows[slot])
         down_grad = dot_tn(act[slot, :, pl.ds(block * part, part)], grad_rows)
-
         total[: 2 * part] = jnp.where(order == 0, pair_grad, total[: 2 * part] + pair_grad)
         total[2 * part :] = jnp.where(order == 0, down_grad, total[2 * part :] + down_grad)
 
+    def open_step(step, carry):
+        slot = slot_at(step)
+
+        @pl.when(step == 0)
+        def _():
+            swap(0).wait_recv()
+
+        @pl.when(step == 1)
+        def _():
+            gather(0).wait_recv()
+            gather(8).wait_recv()
+
+        @pl.when(step == 2)
+        def _():
+            gather(1).wait_recv()
+            gather(3).start()
+            gather(5).start()
+            gather(2).wait_recv()
+            gather(4).start()
+            gather(6).start()
+            gather(9).wait_recv()
+            gather(12).start()
+            gather(10).wait_recv()
+            gather(13).start()
+
+        @pl.when(step == 3)
+        def _():
+            swap(1).wait_recv()
+
+        @pl.when(step == 4)
+        def _():
+            gather(5).wait_recv()
+            gather(12).wait_recv()
+            swap(2).wait_recv()
+
+        @pl.when(step == 5)
+        def _():
+            weight(2).start()
+            weight(3).start()
+            gather(6).wait_recv()
+            gather(13).wait_recv()
+
+        @pl.when(step == 6)
+        def _():
+            swap(3).wait_recv()
+            gather(3).wait_recv()
+            gather(4).wait_recv()
+            gather(7).start()
+            gather(11).wait_recv()
+            gather(14).start()
+
         @pl.when(step == 7)
         def _():
-            stage_a[...] = total[...].astype(bf16)
+            gather(7).wait_recv()
+            gather(14).wait_recv()
+
+        fetch(step + 1)
+        fetch_from(grad_own, step).wait()
+        grad_rows = grads[step % 2]
+        forward(slot, 1, grad_rows)
+        forward(slot, 0, grad_rows)
+        gather_weights(slot, 1, step, grad_rows)
+        return carry
+
+    def first_step(step, carry):
+        turn, order = step // 8, step % 8
+        slot = slot_at(step)
+        block = jnp.where(turn == 1, 2, jnp.where(turn == 2, 0, 3))
+
+        @pl.when(step + 1 < 8 * outer_count)
+        def _():
+            fetch(step + 1)
+
+        @pl.when(step == 20)
+        def _():
+            weight(2).wait_recv()
+            weight(3).wait_recv()
+            ring_copy(0).start()
+
+        fetch_from(grad_own, step).wait()
+        grad_rows = grads[step % 2]
+
+        @pl.when(turn != 2)
+        def _():
+            forward(slot, block, grad_rows)
+
+        gather_weights(slot, block, order, grad_rows)
 
         @pl.when(step == 15)
         def _():
@@ -351,10 +399,14 @@
 
         return carry
 
-    lax.fori_loop(0, 8 * outer_count, first_step, 0)
+    lax.fori_loop(0, 8, open_step, 0)
+    stage_a[...] = total[...].astype(bf16)
+    weight(0).wait_recv()
+    weight(1).wait_recv()
+    lax.fori_loop(8, 8 * outer_count, first_step, 0)
     ring_copy(0).wait()
     stage_a[...] = total[...].astype(bf16)
-    stage_b[...] = (stage_b[...].astype(f32) + ring[0].astype(f32)).astype(bf16)
+    stage_b[...] = (stage_b[...].astype(f32) + ring[...].astype(f32)).astype(bf16)
     ring_copy(1).start()
     for slot in range(1, 8):
         dots_copy(slot).start()
@@ -362,29 +414,29 @@
         gather(index).wait_send()
 
     def second_step(order, carry):
-        turn = order // 2
-        there = jnp.where(turn == 0, 3, jnp.where(turn == 3, 0, turn))
-        slot = there * 2 + 1 - order % 2
+        slot = jnp.where(order < 2, 7 - order, jnp.where(order > 5, 7 - order, 0))
+        for index, found in ((2, 3), (3, 5), (4, 2), (5, 4)):
+            slot = jnp.where(order == index, found, slot)
         dx_ref[...] = dot_nt(both[slot], wide[...])
 
-        @pl.when(order % 2 == 0)
+        @pl.when(slot % 2 == 1)
         def _():
             rows[slot] = dx_ref[...].astype(bf16)
 
         for index in range(4):
 
-            @pl.when((order % 2 == 0) & (there == index))
+            @pl.when(slot == 2 * index + 1)
             def _():
                 back(index).start()
 
-        @pl.when(order == 1)
+        @pl.when(slot == 6)
         def _():
             back(3).wait_recv()
             rows[6] = (dx_ref[...] + core_in[3].astype(f32)).astype(bf16)
             back(4).start()
             back(5).start()
 
-        @pl.when(order == 3)
+        @pl.when(slot == 2)
         def _():
             back(1).wait_recv()
             back(5).wait_recv()
@@ -394,7 +446,7 @@
             ).astype(bf16)
             back(6).start()
 
-        @pl.when(order == 5)
+        @pl.when(slot == 4)
         def _():
             back(2).wait_recv()
             back(4).wait_recv()
@@ -415,7 +467,10 @@
 
     lax.fori_loop(0, 8, third_step, 0)
     ring_copy(1).wait()
-    stage_a[...] = (stage_a[...].astype(f32) + ring[1].astype(f32)).astype(bf16)
+    arrived = local(ring_hbm, ring, 2)
+    arrived.start()
+    arrived.wait()
+    stage_a[...] = (stage_a[...].astype(f32) + ring[...].astype(f32)).astype(bf16)
     local(stage_a, last_hbm, 0).start()
     back(0).wait_recv()
     back(6).wait_recv()
@@ -434,18 +489,23 @@
         back(index).wait_send()
     for index in range(4):
         weight(index).wait_send()
+        swap(index).wait_send()
     for slot in range(8):
         pltpu.make_async_copy(act.at[slot], y_hbm.at[place_of(slot)], y_sem.at[slot]).wait()
     local(stage_a, last_hbm, 0).wait()
     local(dx_ref, dx_hbm, 1).wait()
 
 
-def expert_layer(rows_own, gate_table, rows_grad, pair_own, down_own, outer_count):
+def expert_layer(rows_own, gate_table, grad_own, pair_own, down_own, outer_count):
     f32 = jnp.float32
     bf16 = jnp.bfloat16
     length, width = rows_own.shape
     part = down_own.shape[0]
     ahead = [(place, (place + 1) % outer_count) for place in range(outer_count)]
+    grad_x = lax.ppermute(grad_own, "narrow", [(0, 1), (1, 0)])
+    grad_y = lax.ppermute(grad_own, "inner", [(place, (place + 2) % 4) for place in range(4)])
+    across = [(place, (place // 2 + 2) % 4 * 2 + 1 - place % 2) for place in range(8)]
+    grad_far = lax.ppermute(grad_own, ("inner", "narrow"), across)
     pair_next = lax.ppermute(pair_own, "outer", ahead)
     down_next = lax.ppermute(down_own, "outer", ahead)
     anywhere = pl.BlockSpec(memory_space=pl.ANY)
@@ -453,7 +513,7 @@
     vmem, dma = pltpu.VMEM, pltpu.SemaphoreType.DMA
     hidden = outer_count * part
     share = jax.ShapeDtypeStruct((3 * part, width), bf16)
-    dx, y_rows, dots, first, last = pl.pallas_call(
+    dx, y_rows, dots, first, last, _, _ = pl.pallas_call(
         functools.partial(expert_kernel, outer_count),
         out_shape=(
             jax.ShapeDtypeStruct((length, width), f32),
@@ -461,9 +521,11 @@
             jax.ShapeDtypeStruct((8, 8, length), f32),
             jax.ShapeDtypeStruct((3 * part, width), f32),
             share,
+            jax.ShapeDtypeStruct((4, length, width), bf16),
+            share,
         ),
-        in_specs=[anywhere] * 7,
-        out_specs=(anywhere, anywhere, inside, anywhere, anywhere),
+        in_specs=[anywhere] * 10,
+        out_specs=(anywhere, anywhere, inside, anywhere, anywhere, anywhere, anywhere),
         scratch_shapes=[
             vmem((8, length, width), bf16),
             vmem((8,) + gate_table.shape, bf16),
@@ -475,7 +537,7 @@
             vmem((3 * part, width), f32),
             vmem((3 * part, width), bf16),
             vmem((3 * part, width), bf16),
-            vmem((2, 3 * part, width), bf16),
+            vmem((3 * part, width), bf16),
             vmem((4, length, width), bf16),
             vmem((2, length // 2, width), bf16),
             vmem((2, length, width), bf16),
@@ -494,6 +556,8 @@
             dma((8,)),
             dma((8,)),
             dma((8,)),
+            dma((4,)),
+            dma((4,)),
         ],
         compiler_params=pltpu.CompilerParams(
             collective_id=0, has_side_effects=True, vmem_limit_bytes=67043328
@@ -505,7 +569,10 @@
     )(
         rows_own,
         gate_table,
-        rows_grad.reshape(8, length, width),
+        grad_own,
+        grad_x,
+        grad_y,
+        grad_far,
         pair_own,
         down_own,
         pair_next,
@@ -754,7 +821,6 @@
     outer_count = experts // INNER
     here = ("inner", "narrow")
     fused = outer_count == 4 and lax.axis_size("narrow") == 2
-    rows_grad = lax.all_gather(grad_out, here, axis=0, tiled=True)
     part = w_gate.shape[2]
     inputs = hidden_in.astype(f32)
     scale_one = norm_scale(inputs)
@@ -799,7 +865,7 @@
         table = jnp.concatenate([part_one, part_two, part_three], axis=0).astype(bf16)
         pair_own = jnp.concatenate([w_gate[0], w_up[0]], axis=1)
         rows_back, y_rows, dots, weight_first, weight_last = expert_layer(
-            ffn_normed, table, rows_grad, pair_own, w_down[0], outer_count
+            ffn_normed, table, grad_out, pair_own, w_down[0], outer_count
         )
         moe_rows = lax.psum_scatter(y_rows, here, scatter_dimension=0, tiled=True)
         dots = dots[:, :outer_count].reshape(2, 2, 2, outer_count, length).sum(axis=1)
@@ -810,6 +876,7 @@
         block = (outer + outer_count - each // INNER) % outer_count
         gate_grads = dots.reshape(experts, length)[(side * 2 + core) * outer_count + block].T
     else:
+        rows_grad = lax.all_gather(grad_out, here, axis=0, tiled=True)
         full_gate = lax.all_gather(w_gate[0], "outer", axis=1, tiled=True)
         full_up = lax.all_gather(w_up[0], "outer", axis=1, tiled=True)
         full_down = lax.all_gather(w_down[0], "outer", axis=0, tiled=True)

time: 432 us -> 415 us (0.961)
  waiting for transfers between devices: 19.9 us -> 6.57 us
  Pallas kernels: 261 us -> 252 us
    all_gather x1 -> x0, waiting for transfers between devices: 16 us -> none  [on_device(): rows_grad = lax.all_gather(grad_out, here, axis=0, tiled=True)]
    pallas_call x1, Pallas kernels: 171 us -> 163 us  [expert_layer(): pl.pallas_call(functools.partial(expert_kernel, outer_count), out_shape=(...]
    ppermute x0 -> x3, starting transfers between devices: none -> 4.63 us  [the longest x1 3.99 us: expert_layer(): grad_far = lax.ppermute(grad_own, ('inner', 'narrow'), across)]
    unnamed x139 -> x141, local copies, waits for them, and re-layouts: 10.4 us -> 11.1 us
  transfers between devices with their start and end apart: 5 -> 7, of which waited for: 2 -> 3; matrix products, arithmetic and copies ran while one was open for 23% -> 24% of each run, Pallas kernels for 0% -> 0%
where the time goes in v6:
time: 415 us; the launch traced here: 409 us
  Pallas kernels  252 us (61%)
  matrix products  57.1 us (14%)
  other arithmetic  49 us (12%)
  local copies, waits for them, and re-layouts  20 us (5%)
  between operations  15.5 us (4%)
  starting transfers between devices  9.15 us (2%)
  waiting for transfers between devices  6.57 us (2%)
    pallas_call x1, Pallas kernels, expert_layer(): pl.pallas_call(functools.partial(expert_kernel, outer_count), out_shape=(...  163 us
    pallas_call x1, Pallas kernels, reduce_layer(): pl.pallas_call(functools.partial(reduce_kernel, outer_count), out_shape=t...  89.3 us
    unnamed x141, local copies, waits for them, and re-layouts  11.1 us
    dot_general x1, matrix products, on_device(): jnp.einsum('ngqk,qngd->knd', weights_prob.astype(bf16), attended_grad, pr...  9.03 us
    convert_element_type x1, other arithmetic, on_device(): score_grad = (weights_prob * (prob_grad - jnp.sum(weights_prob * prob_gra...  8.74 us
    dot_general x1, matrix products, on_device(): jnp.einsum('ngqk,knd->qngd', weights_prob.astype(bf16), value_rows, prefe...  8.65 us
  transfers between devices with their start and end apart: 7, of which 3 were waited for; matrix products, arithmetic and copies ran while one was open for 24% of the time, Pallas kernels for 0%

profile of v6, /device:TPU:0, one launch (start us, length us, event | category | flops | bytes accessed | tf_op | source)
XLA Modules:
  0.0 409.2 jit_solution(4219543620651506533)
XLA Ops:
  7.3 4.0 collective-permute-start.2
  11.9 2.0 collective-permute-start.4
  15.2 1.6 collective-permute-start.3
  22.6 1.3 fusion.58
  24.5 7.7 %fusion.56 = (f32[8,2,512]{2,1,0:T(2,128)S(1)}, f32[8,2,512,512]{2,3,1,0:T(8,128)}) fusion(bf16[512,8,2,32]{0,3,2,1:T(8,128)(2,1)S(1)} %bitcast.156, bf16[512,8,2,32]{0,3,2,1:T(8,128)(2,1)S(1)} %bitcast.154, bf16[512,8,32]{0,2,1:T(8,128)(2,1)S(1)} %get-tuple-element.106, bf16[512,8,32]{0,2,1:T(8,128)(2,1)S(1)} %get-tuple-element.105, ...), kind=kOutput, calls=%fused_computation.135 | convolution fusion | flops 552591360 | bytes 18644992 | tf_op jit(solution)/shard_map/qngd,knd->ngqk/dot_general | solution.py:52
  32.3 8.2 %exponential_reduce_fusion = f32[8,2,512]{2,1,0:T(2,128)S(1)} fusion(f32[8,2,512,512]{2,3,1,0:T(8,128)} %get-tuple-element.118, f32[8,2,512]{2,1,0:T(2,128)S(1)} %get-tuple-element.117), kind=kLoop, calls=%fused_computation.8 | loop fusion | flops 8380416 | bytes 16842752 | tf_op jit(solution)/shard_map/reduce_sum | solution.py:845
  40.5 8.7 %fusion.18 = bf16[8,64,2,512]{3,1,2,0:T(8,128)(2,1)S(1)} fusion(bf16[512,8,64,1]{0,2,3,1:T(8,128)(2,1)S(1)} %bitcast.152, f32[8,2,512,512]{2,3,1,0:T(8,128)} %get-tuple-element.118, f32[8,2,512]{2,1,0:T(2,128)S(1)} %bitcast.160), kind=kOutput, calls=%fused_computation.39 | convolution fusion | flops 545783808 | bytes 18382848 | tf_op jit(solution)/shard_map/ngqk,knd->qngd/dot_general | solution.py:847
  49.2 1.4 multiply_reduce_fusion.2
  53.3 3.9 collective-permute-done.1.grad_y
  57.5 162.6 %expert_layer.1 = (f32[512,1024]{1,0:T(8,128)}, bf16[8,512,1024]{2,1,0:T(8,128)(2,1)}, f32[8,8,512]{2,1,0:T(8,128)}, f32[768,1024]{1,0:T(8,128)}, bf16[768,1024]...) custom-call(bf16[512,1024]{1,0:T(8,128)(2,1)} %copy-done.7, ...), custom_call_target="tpu_custom_call" | custom-call | flops 77309411328 | bytes 67108864 | tf_op jit(solution)/shard_map/expert_layer/pallas_call | solution.py:516
  221.3 1.3 copy.89.attended_ref
  224.4 3.6 multiply_reduce_fusion.1
  228.0 2.0 fusion.55
  233.1 9.0 %fusion.26 = bf16[8,64,512]{2,1,0:T(8,128)(2,1)S(1)} fusion(bf16[512,8,2,64]{0,3,2,1:T(8,128)(2,1)S(1)} %bitcast.139, f32[8,2,512,512]{2,3,1,0:T(8,128)} %get-tuple-element.118, f32[8,2,512]{2,1,0:T(2,128)S(1)} %bitcast.161), kind=kOutput, calls=%fused_computation.44 | convolution fusion | flops 545521664 | bytes 18382848 | tf_op jit(solution)/shard_map/ngqk,qngd->knd/dot_general | solution.py:945
  244.0 8.1 %fusion = (f32[8,2,512]{2,1,0:T(2,128)S(1)}, f32[8,512,512,2]{2,1,3,0:T(8,128)S(1)}) fusion(f32[8,2,512,512]{2,3,1,0:T(8,128)} %get-tuple-element.118, f32[8,2,512]{2,1,0:T(2,128)S(1)} %bitcast.162, bf16[512,8,64,1]{0,2,3,1:T(8,128)(2,1)S(1)} %bitcast.153, bf16[512,8,2,64]{0,3,2,1:T(8,128)(2,1)} %bitcast.140), kind=kOutput, calls=%fused_computation.3 | convolution fusion | flops 549445632 | bytes 35192832 | tf_op jit(solution)/shard_map/qngd,knd->ngqk/dot_general | solution.py:948
  252.1 8.7 %fusion.2 = bf16[8,2,512,512]{2,3,1,0:T(8,128)(2,1)S(1)} fusion(f32[8,512,512,2]{2,1,3,0:T(8,128)S(1)} %get-tuple-element.125, f32[8,2,512,512]{2,3,1,0:T(8,128)} %get-tuple-element.118, f32[8,2,512]{2,1,0:T(2,128)S(1)} %get-tuple-element.124, f32[8,2,512]{2,1,0:T(2,128)S(1)} %bitcast.163), kind=kLoop, calls=%fused_computation.5 | loop fusion | flops 16777216 | bytes 42008576 | tf_op jit(solution)/shard_map/convert_element_type | solution.py:951
  260.9 4.2 %fusion.25 = f32[512,8,64]{0,2,1:T(8,128)S(1)} fusion(bf16[8,2,512,512]{2,3,1,0:T(8,128)(2,1)S(1)} %fusion.2, bf16[512,8,2,32]{0,3,2,1:T(8,128)(2,1)} %bitcast.157, bf16[512,8,2,32]{0,3,2,1:T(8,128)(2,1)S(1)} %bitcast.155), kind=kOutput, calls=%fused_computation.43 | convolution fusion | flops 539230208 | bytes 10485760 | tf_op jit(solution)/shard_map/ngqk,qngd->knd/dot_general | solution.py:955
  266.4 5.0 %convolution_multiply_fusion = f32[8,64,2,512]{3,1,2,0:T(8,128)S(1)} fusion(bf16[8,2,512,512]{2,3,1,0:T(8,128)(2,1)} %copy-done, bf16[512,8,32]{0,2,1:T(8,128)(2,1)S(1)} %copy-done.38, bf16[512,8,32]{0,2,1:T(8,128)(2,1)S(1)} %copy-done.36), kind=kOutput, calls=%fused_computation.37 | convolution fusion | flops 538443776 | bytes 11010048 | tf_op jit(solution)/shard_map/ngqk,knd->qngd/dot_general | solution.py:952
  272.8 2.7 pad_maximum_fusion.turned_ref
  277.1 1.3 fusion.59
  279.1 2.6 fusion.17
  282.7 4.0 fusion.16
  286.7 2.3 reduce-scatter.2.cloned.1.call-done
  289.1 2.5 add_convert_fusion
  291.6 89.3 %reduce_layer.1 = (bf16[1024,1024]{1,0:T(8,128)(2,1)}, bf16[1024,1024]{1,0:T(8,128)(2,1)}, bf16[1024,512]{1,0:T(8,128)(2,1)}, bf16[1024,640]{1,0:T(8,128)(2,1)}) custom-call(bf16[512,1024]{1,0:T(8,128)(2,1)} %copy-done.15, bf16[512,2048]{1,0:T(8,128)(2,1)} %pad_maximum_fusion.turned_ref, bf16[512,1024]{1,0:T(8,128)(2,1)} %copy.89.attended_ref, ...), custom_call_target="tpu_custom_call" | custom-call | tf_op jit(solution)/shard_map/reduce_layer/pallas_call | solution.py:781
  382.1 2.8 slice_convert_fusion
  384.9 2.1 convert_add_fusion.1
  388.3 1.3 copy.92
  389.6 1.3 copy.91
  393.0 4.2 %convert_element_type.110 = f32[1024,1024]{1,0:T(8,128)} convert(bf16[1024,1024]{1,0:T(8,128)(2,1)} %get-tuple-element.35) | non-fusion elementwise | flops 1048576 | bytes 6291456 | tf_op jit(solution)/shard_map/convert_element_type | solution.py:997
  397.1 1.6 convert_element_type.111
  399.5 2.5 convert_element_type.113
  (195 shorter events, 29.8 us)
Async XLA Ops:
  7.2 9.6 %copy-start.4 = (bf16[512,1024]{1,0:T(8,128)(2,1)S(1)}, bf16[512,1024]{1,0:T(8,128)(2,1)}, u32[]{:S(2)}) copy-start(bf16[512,1024]{1,0:T(8,128)(2,1)} %param.14) | copy-start | bytes 3145732
  7.2 11.5 %copy-start.63 = (s32[1,512]{1,0:T(1,128)S(1)}, s32[1,512]{1,0:T(1,128)}, u32[]{:S(2)}) copy-start(s32[1,512]{1,0:T(1,128)} %param.15) | copy-start | bytes 6148
  7.2 11.7 %copy-start.52 = (f32[1024]{0:T(1024)S(1)}, f32[1024]{0:T(1024)}, u32[]{:S(2)}) copy-start(f32[1024]{0:T(1024)} %param.17) | copy-start | bytes 12292
  7.2 281.9 %reduce-scatter.2.cloned.1.call-start = ((), (), s32[]{:S(2)}) async-start(), calls=%async_computation.1 | async-start | bytes 9437184 | tf_op jit(solution)/shard_map/reduce_scatter | solution.py:870
  7.3 46.0 %collective-permute-start.2 = (bf16[512,1024]{1,0:T(8,128)(2,1)}, bf16[512,1024]{1,0:T(8,128)(2,1)S(1)}, u32[]{:S(2)}, u32[]{:S(2)}) collective-permute-start(bf16[512,1024]{1,0:T(8,128)(2,1)} %grad_own.1), channel_id=1, source_target_pairs={{0,5},{1,4},{2,7},{3,6},{4,1},{5,0},{6,3},{7,2},{8,13},{9,12},{10,... | collective-permute-start | bytes 3145736 | tf_op jit(solution)/shard_map/ppermute | solution.py:508
  11.2 45.9 %collective-permute-start.1 = (bf16[512,1024]{1,0:T(8,128)(2,1)}, bf16[512,1024]{1,0:T(8,128)(2,1)}, u32[]{:S(2)}, u32[]{:S(2)}) collective-permute-start(bf16[512,1024]{1,0:T(8,128)(2,1)} %grad_own.1), channel_id=1, source_target_pairs={{0,4},{2,6},{4,0},{6,2},{1,5},{3,7},{5,1},{7,3},{8,12},{10,14},{12... | collective-permute-start | bytes 3145736 | tf_op jit(solution)/shard_map/ppermute | solution.py:506
  11.8 45.7 %collective-permute-start = (bf16[512,1024]{1,0:T(8,128)(2,1)}, bf16[512,1024]{1,0:T(8,128)(2,1)}, u32[]{:S(2)}, u32[]{:S(2)}) collective-permute-start(bf16[512,1024]{1,0:T(8,128)(2,1)} %grad_own.1), channel_id=1, source_target_pairs={{0,1},{1,0},{2,3},{3,2},{4,5},{5,4},{6,7},{7,6},{8,9},{9,8},{10,11... | collective-permute-start | bytes 3145736 | tf_op jit(solution)/shard_map/ppermute | solution.py:505
  11.9 41.3 %collective-permute-start.4 = (bf16[256,1024]{1,0:T(8,128)(2,1)}, bf16[256,1024]{1,0:T(8,128)(2,1)}, u32[]{:S(2)}, u32[]{:S(2)}) collective-permute-start(bf16[256,1024]{1,0:T(8,128)(2,1)} %bitcast.172), channel_id=1, source_target_pairs={{0,8},{8,16},{16,24},{24,0},{1,9},{9,17},{17,25},{25,1},{2,10},{10... | collective-permute-start | bytes 1572872 | tf_op jit(solution)/shard_map/ppermute | solution.py:510
  15.1 4.8 %copy-start.34 = (bf16[1024,512]{1,0:T(8,128)(2,1)}, bf16[1024,512]{1,0:T(8,128)(2,1)S(1)}, u32[]{:S(2)}) copy-start(bf16[1024,512]{1,0:T(8,128)(2,1)S(1)} %pad_maximum_fusion.2.pair_own) | copy-start | bytes 3145732
  15.2 38.1 %collective-permute-start.3 = (bf16[1024,512]{1,0:T(8,128)(2,1)S(1)}, bf16[1024,512]{1,0:T(8,128)(2,1)}, u32[]{:S(2)}, u32[]{:S(2)}) collective-permute-start(bf16[1024,512]{1,0:T(8,128)(2,1)S(1)} %pad_maximum_fusion.2.pair_own), channel_id=1, source_target_pairs={{0,8},{8,16},{16,24},{24,0},{1,9},{9,17},{17,25},{25,1},{2,10},{10... | collective-permute-start | bytes 3145736 | tf_op jit(solution)/shard_map/ppermute | solution.py:509
  18.6 5.4 %copy-start.26 = (f32[512,32]{0,1:T(8,128)}, f32[512,32]{0,1:T(8,128)S(1)}, u32[]{:S(2)}) copy-start(f32[512,32]{0,1:T(8,128)S(1)} %get-tuple-element.116) | copy-start | bytes 196612
  20.8 19.7 %copy-start.17 = (bf16[512,512]{0,1:T(8,128)(2,1)}, bf16[512,512]{0,1:T(8,128)(2,1)S(1)}, u32[]{:S(2)}) copy-start(bf16[512,512]{0,1:T(8,128)(2,1)S(1)} %convolution_convert_fusion.1) | copy-start | bytes 1572868
  24.1 8.2 %copy-start.35 = (bf16[512,8,32]{0,2,1:T(8,128)(2,1)}, bf16[512,8,32]{0,2,1:T(8,128)(2,1)S(1)}, u32[]{:S(2)}) copy-start(bf16[512,8,32]{0,2,1:T(8,128)(2,1)S(1)} %get-tuple-element.105) | copy-start | bytes 786436
  24.1 8.2 %copy-start.37 = (bf16[512,8,32]{0,2,1:T(8,128)(2,1)}, bf16[512,8,32]{0,2,1:T(8,128)(2,1)S(1)}, u32[]{:S(2)}) copy-start(bf16[512,8,32]{0,2,1:T(8,128)(2,1)S(1)} %get-tuple-element.106) | copy-start | bytes 786436
  24.5 7.8 %copy-start.20 = (bf16[512,16,32]{0,2,1:T(8,128)(2,1)}, bf16[512,16,32]{0,2,1:T(8,128)(2,1)S(1)}, u32[]{:S(2)}) copy-start(bf16[512,16,32]{0,2,1:T(8,128)(2,1)S(1)} %get-tuple-element.101) | copy-start | bytes 1572868
  24.5 7.8 %copy-start.22 = (bf16[512,16,32]{0,2,1:T(8,128)(2,1)}, bf16[512,16,32]{0,2,1:T(8,128)(2,1)S(1)}, u32[]{:S(2)}) copy-start(bf16[512,16,32]{0,2,1:T(8,128)(2,1)S(1)} %get-tuple-element.102) | copy-start | bytes 1572868
  40.5 8.7 %copy-start.41 = (f32[2,8,512]{2,1,0:T(8,128)}, f32[2,8,512]{2,1,0:T(8,128)S(1)}, u32[]{:S(2)}) copy-start(f32[2,8,512]{2,1,0:T(8,128)S(1)} %log_add_fusion) | copy-start | bytes 98308
  40.5 8.7 %copy-start.23 = (bf16[1024,1024]{1,0:T(8,128)(2,1)S(1)}, bf16[1024,1024]{1,0:T(8,128)(2,1)}, u32[]{:S(2)}) copy-start(bf16[1024,1024]{1,0:T(8,128)(2,1)} %param.21) | copy-start | bytes 6291460
  52.5 4.7 %copy-start.56 = (f32[512]{0:T(512)}, f32[512]{0:T(512)S(1)}, u32[]{:S(2)}) copy-start(f32[512]{0:T(512)S(1)} %fusion.42) | copy-start | bytes 6148
  220.2 4.1 %copy-start.2 = (f32[512,1024]{1,0:T(8,128)S(1)}, f32[512,1024]{1,0:T(8,128)}, u32[]{:S(2)}) copy-start(f32[512,1024]{1,0:T(8,128)} %copy-done.1) | copy-start | bytes 6291460
  220.2 4.1 %copy-start.47 = (bf16[1024,16]{0,1:T(8,128)(2,1)S(1)}, bf16[1024,16]{0,1:T(8,128)(2,1)}, u32[]{:S(2)}) copy-start(bf16[1024,16]{0,1:T(8,128)(2,1)} %param.23) | copy-start | bytes 98308
  220.2 4.1 %copy-start.51 = (f32[1024]{0:T(1024)S(1)}, f32[1024]{0:T(1024)}, u32[]{:S(2)}) copy-start(f32[1024]{0:T(1024)} %param.22) | copy-start | bytes 12292
  220.2 4.1 %copy-start.60 = (f32[512]{0:T(512)S(1)}, f32[512]{0:T(512)}, u32[]{:S(2)}) copy-start(f32[512]{0:T(512)} %copy-done.59) | copy-start | bytes 6148
  222.7 68.9 %collective-permute-start.5 = (bf16[768,1024]{1,0:T(8,128)(2,1)}, bf16[768,1024]{1,0:T(8,128)(2,1)}, u32[]{:S(2)}, u32[]{:S(2)}) collective-permute-start(bf16[768,1024]{1,0:T(8,128)(2,1)} %get-tuple-element.30), channel_id=1, source_target_pairs={{0,8},{8,16},{16,24},{24,0},{1,9},{9,17},{17,25},{25,1},{2,10},{10... | collective-permute-start | bytes 4718600 | tf_op jit(solution)/shard_map/ppermute | solution.py:581
  233.1 9.1 %copy-start.6 = (bf16[512,1024]{0,1:T(8,128)(2,1)}, bf16[512,1024]{0,1:T(8,128)(2,1)S(1)}, u32[]{:S(2)}) copy-start(bf16[512,1024]{0,1:T(8,128)(2,1)S(1)} %copy.81) | copy-start | bytes 3145732
  233.1 10.8 %copy-start.18 = (bf16[512,512]{0,1:T(8,128)(2,1)S(1)}, bf16[512,512]{0,1:T(8,128)(2,1)}, u32[]{:S(2)}) copy-start(bf16[512,512]{0,1:T(8,128)(2,1)} %copy-done.17) | copy-start | bytes 1572868
  252.0 8.8 %copy-start.21 = (bf16[512,16,32]{0,2,1:T(8,128)(2,1)S(1)}, bf16[512,16,32]{0,2,1:T(8,128)(2,1)}, u32[]{:S(2)}) copy-start(bf16[512,16,32]{0,2,1:T(8,128)(2,1)} %copy-done.20) | copy-start | bytes 1572868
  260.8 4.3 %copy-start = (bf16[8,2,512,512]{2,3,1,0:T(8,128)(2,1)}, bf16[8,2,512,512]{2,3,1,0:T(8,128)(2,1)S(1)}, u32[]{:S(2)}) copy-start(bf16[8,2,512,512]{2,3,1,0:T(8,128)(2,1)S(1)} %fusion.2) | copy-start | bytes 25165828
  260.8 4.3 %copy-start.27 = (f32[512,32]{0,1:T(8,128)S(1)}, f32[512,32]{0,1:T(8,128)}, u32[]{:S(2)}) copy-start(f32[512,32]{0,1:T(8,128)} %copy-done.26) | copy-start | bytes 196612
  260.8 4.3 %copy-start.43 = (f32[512,32]{0,1:T(8,128)S(1)}, f32[512,32]{0,1:T(8,128)}, u32[]{:S(2)}) copy-start(f32[512,32]{0,1:T(8,128)} %get-tuple-element.114) | copy-start | bytes 196612
  282.7 6.3 %copy-start.3 = (f32[512,1024]{1,0:T(8,128)S(1)}, f32[512,1024]{1,0:T(8,128)}, u32[]{:S(2)}) copy-start(f32[512,1024]{1,0:T(8,128)} %copy-done.1) | copy-start | bytes 6291460
  393.0 4.2 %copy-start.33 = (bf16[1024,512]{1,0:T(8,128)(2,1)S(1)}, bf16[1024,512]{1,0:T(8,128)(2,1)}, u32[]{:S(2)}) copy-start(bf16[1024,512]{1,0:T(8,128)(2,1)} %get-tuple-element.36) | copy-start | bytes 3145732
  (44 other events, 96.9 us)
Sparse Core Ops, SparseCore 0:
  220.3 68.7 reduce-scatter.1
